TPU v7x, 32 devices: a whole 2x2x4 slice. The times are simulated.
32 devices in a mesh: seq: 8 (over z, x), head: 4 (over y, core).
Axes of the slice: x: 2, y: 2, z: 4, core: 2. Of those that a mesh axis runs over, the one named last changes fastest.
Arguments:
- queries: bfloat16 [8192, 4096], P('seq', 'head'), may hold values from -120 to 120
- keys: bfloat16 [8192, 512], P('seq', 'head'), may hold values from -6 to 6
- values: bfloat16 [8192, 512], P('seq', 'head'), may hold values from -6 to 6
- mid_pool: bfloat16 [4, 8], P('head'), may hold values from -3 to 3
- coarse_pool: bfloat16 [4, 256], P('head'), may hold values from -0.375 to 0.375
Outputs:
- attended: bfloat16 [8192, 4096], P(('seq', 'head'))
All inputs are finite; a program needn't handle non-finite values.
Results may differ from a plain program's by a relative error of at most 0.0092.
Values may be sent and summed in bfloat16 or wider, within the bound.
No kernel may reach another device: no remote copies, remote signals or barrier semaphores. Data moves between devices by JAX's collectives and lax.ppermute only.
A program may use at most 128 MiB of HBM per device.

v0:
```python
import math

import jax
import jax.numpy as jnp
from jax import lax
from jax.sharding import PartitionSpec as P

HEAD_DIM = 128
BLK = 256
GROUP = 8
MIDS = 256
MIDB = 8


def passed_along(array, axis, by):
    size = lax.axis_size(axis)
    pairs = [(i, i + by) for i in range(size) if 0 <= i + by < size]
    return lax.ppermute(array, axis, pairs)


def summarize(source, pooling, group_size, kv_here):
    rows_here = source.shape[0]
    grouped = source.reshape(rows_here // group_size, group_size, kv_here, HEAD_DIM)
    summary = jnp.einsum("gthd,ht->ghd", grouped, pooling, preferred_element_type=jnp.float32)
    return summary.astype(jnp.bfloat16).reshape(rows_here // group_size, kv_here * HEAD_DIM)


def body(queries, keys, values, mid_pool, coarse_pool):
    tokens_here = queries.shape[0]
    columns = queries.shape[1]
    kv_columns = keys.shape[1]
    kv_here = kv_columns // HEAD_DIM
    sharing = columns // HEAD_DIM // kv_here
    block_count = tokens_here // BLK
    per_group = BLK // GROUP
    hop_count = (MIDB + block_count) // block_count
    device = lax.axis_index("seq")
    logit_scale = 1.0 / math.sqrt(HEAD_DIM)
    mid_keys = summarize(keys, mid_pool, GROUP, kv_here)
    mid_values = summarize(values, mid_pool, GROUP, kv_here)
    summary_key_rows = summarize(keys, coarse_pool, BLK, kv_here)
    coarse_values = summarize(values, coarse_pool, BLK, kv_here)
    tail_keys, tail_values, near_mid_k, near_mid_v = passed_along(
        (keys[tokens_here - BLK :], values[tokens_here - BLK :], mid_keys, mid_values), "seq", 1
    )
    arrivals = [(near_mid_k, near_mid_v)]
    carried = (near_mid_k, near_mid_v)
    for distance in range(2, hop_count + 1):
        carried = passed_along((carried[0], carried[1]), "seq", 1)
        arrivals.append(carried)
    mid_shape = ((hop_count + 1) * block_count, per_group, kv_here, HEAD_DIM)
    mid_blocks_k = jnp.concatenate([pair[0] for pair in arrivals[::-1]] + [mid_keys]).reshape(
        mid_shape
    )
    mid_blocks_v = jnp.concatenate([pair[1] for pair in arrivals[::-1]] + [mid_values]).reshape(
        mid_shape
    )
    all_coarse_k, all_coarse_v = (
        lax.all_gather(summary_key_rows, "seq", axis=0, tiled=True),
        lax.all_gather(coarse_values, "seq", axis=0, tiled=True),
    )
    coarse_total = all_coarse_k.shape[0]
    all_coarse_k = all_coarse_k.reshape(coarse_total, kv_here, HEAD_DIM)
    all_coarse_v = all_coarse_v.reshape(coarse_total, kv_here, HEAD_DIM)
    block_shape = (block_count + 1, BLK, kv_here, HEAD_DIM)
    key_blocks = jnp.concatenate([tail_keys, keys]).reshape(block_shape)
    value_blocks = jnp.concatenate([tail_values, values]).reshape(block_shape)
    blocked_queries = queries.reshape(block_count, BLK, kv_here, sharing, HEAD_DIM)
    step_blocks = min(block_count, max(1, 512 // BLK))
    pieces = []
    for start_block in range(0, block_count, step_blocks):
        stop_block = start_block + step_blocks
        query_rows = blocked_queries[start_block:stop_block]
        local_keys = jnp.concatenate(
            [key_blocks[start_block:stop_block], key_blocks[start_block + 1 : stop_block + 1]],
            axis=1,
        )
        near_values = jnp.concatenate(
            [value_blocks[start_block:stop_block], value_blocks[start_block + 1 : stop_block + 1]],
            axis=1,
        )
        mid_start = hop_count * block_count - 1 - MIDB + start_block
        far_keys = jnp.concatenate(
            [
                mid_blocks_k[mid_start + offset : mid_start + offset + step_blocks]
                for offset in range(MIDB)
            ],
            axis=1,
        )
        far_values = jnp.concatenate(
            [
                mid_blocks_v[mid_start + offset : mid_start + offset + step_blocks]
                for offset in range(MIDB)
            ],
            axis=1,
        )
        local_scores = (
            jnp.einsum(
                "bqhsd,bkhd->bhsqk", query_rows, local_keys, preferred_element_type=jnp.float32
            )
            * logit_scale
        )
        middle_level_scores = (
            jnp.einsum(
                "bqhsd,bkhd->bhsqk", query_rows, far_keys, preferred_element_type=jnp.float32
            )
            * logit_scale
        )
        summary_score_rows = (
            jnp.einsum(
                "bqhsd,chd->bhsqc", query_rows, all_coarse_k, preferred_element_type=jnp.float32
            )
            * logit_scale
        )
        block_ids = (device * block_count + start_block + jnp.arange(step_blocks, dtype=jnp.int32))[
            :, None, None, None, None
        ]
        query_pos = block_ids * BLK + jnp.arange(BLK, dtype=jnp.int32)[None, None, None, :, None]
        key_pos = (
            block_ids * BLK - BLK + jnp.arange(2 * BLK, dtype=jnp.int32)[None, None, None, None, :]
        )
        near_ok = (key_pos >= 0) & (key_pos <= query_pos)
        mid_ok = (block_ids - 1 - MIDB) * per_group + jnp.arange(MIDS, dtype=jnp.int32)[
            None, None, None, None, :
        ] >= 0
        coarse_ok = (
            jnp.arange(coarse_total, dtype=jnp.int32)[None, None, None, None, :]
            <= block_ids - MIDB - 2
        )
        scores = jnp.concatenate(
            [
                jnp.where(near_ok, local_scores, -jnp.inf),
                jnp.where(mid_ok, middle_level_scores, -jnp.inf),
                jnp.where(coarse_ok, summary_score_rows, -jnp.inf),
            ],
            axis=-1,
        )
        row_max = jnp.max(scores, axis=-1, keepdims=True)
        exponent = jnp.exp(scores - row_max)
        row_total = jnp.sum(exponent, axis=-1, keepdims=True)
        softmax_weights = (exponent / row_total).astype(jnp.bfloat16)
        near_part = softmax_weights[..., : 2 * BLK]
        mid_part = softmax_weights[..., 2 * BLK : 2 * BLK + MIDS]
        coarse_part = softmax_weights[..., 2 * BLK + MIDS :]
        output_rows = jnp.einsum(
            "bhsqk,bkhd->bqhsd", near_part, near_values, preferred_element_type=jnp.float32
        )
        output_rows = output_rows + jnp.einsum(
            "bhsqk,bkhd->bqhsd", mid_part, far_values, preferred_element_type=jnp.float32
        )
        output_rows = output_rows + jnp.einsum(
            "bhsqc,chd->bqhsd", coarse_part, all_coarse_v, preferred_element_type=jnp.float32
        )
        pieces.append(output_rows.astype(jnp.bfloat16).reshape(step_blocks * BLK, columns))
    attended = jnp.concatenate(pieces, axis=0)
    return lax.all_to_all(attended, "head", split_axis=0, concat_axis=1, tiled=True)


def solution(mesh):
    return jax.shard_map(
        body,
        mesh=mesh,
        in_specs=(
            P("seq", "head"),
            P("seq", "head"),
            P("seq", "head"),
            P("head", None),
            P("head", None),
        ),
        out_specs=P(("seq", "head"), None),
        check_vma=False,
    )
```

profile of v0, /device:TPU:0, one launch (start us, length us, event | category | flops | bytes accessed | tf_op | source)
XLA Modules:
  0.0 165.0 jit_solution(9400403829575613246)
XLA Ops:
  0.0 1.2 fusion.34
  1.3 4.9 %collective-permute-start.2 = (bf16[128,128]{1,0:T(8,128)(2,1)S(1)}, bf16[128,128]{1,0:T(8,128)(2,1)S(1)}, u32[]{:S(2)}, u32[]{:S(2)}) collective-permute-start(bf16[128,128]{1,0:T(8,128)(2,1)S(1)} %convert_element_type.44), channel_id=1, source_target_pairs={{0,4},{4,8},{8,12},{12,16},{16,20},{20,24},{24,28},{1,5},{5,9},{9,... | collective-permute-start | bytes 98312 | tf_op jit(solution)/shard_map/ppermute | solution.py:18
  6.1 0.8 slice.243
  7.0 3.4 %collective-permute-start.1 = (bf16[256,128]{1,0:T(8,128)(2,1)S(1)}, bf16[256,128]{1,0:T(8,128)(2,1)S(1)}, u32[]{:S(2)}, u32[]{:S(2)}) collective-permute-start(bf16[256,128]{1,0:T(8,128)(2,1)S(1)} %slice.243), channel_id=1, source_target_pairs={{0,4},{4,8},{8,12},{12,16},{16,20},{20,24},{24,28},{1,5},{5,9},{9,... | collective-permute-start | bytes 196616 | tf_op jit(solution)/shard_map/ppermute | solution.py:18
  10.5 1.2 fusion.32
  11.6 4.0 %collective-permute-start.5 = (bf16[128,128]{1,0:T(8,128)(2,1)S(1)}, bf16[128,128]{1,0:T(8,128)(2,1)}, u32[]{:S(2)}, u32[]{:S(2)}) collective-permute-start(bf16[128,128]{1,0:T(8,128)(2,1)S(1)} %convert_element_type.47), channel_id=1, source_target_pairs={{0,4},{4,8},{8,12},{12,16},{16,20},{20,24},{24,28},{1,5},{5,9},{9,... | collective-permute-start | bytes 98312 | tf_op jit(solution)/shard_map/ppermute | solution.py:18
  15.7 0.8 slice.238
  16.5 2.8 %collective-permute-start = (bf16[256,128]{1,0:T(8,128)(2,1)S(1)}, bf16[256,128]{1,0:T(8,128)(2,1)S(1)}, u32[]{:S(2)}, u32[]{:S(2)}) collective-permute-start(bf16[256,128]{1,0:T(8,128)(2,1)S(1)} %slice.238), channel_id=1, source_target_pairs={{0,4},{4,8},{8,12},{12,16},{16,20},{20,24},{24,28},{1,5},{5,9},{9,... | collective-permute-start | bytes 196616 | tf_op jit(solution)/shard_map/ppermute | solution.py:18
  19.8 1.7 %slice_bitcast_fusion.13 = (bf16[64,8,8,128]{3,1,2,0:T(8,128)(2,1)S(1)}, bf16[64,8,8,128]{3,1,2,0:T(8,128)(2,1)S(1)}) fusion(bf16[1024,1024]{1,0:T(8,128)(2,1)} %param.5), kind=kLoop, calls=%fused_computation.36 | loop fusion | bytes 4194304
  21.5 0.3 copy.126
  21.9 0.1 fusion.42
  22.1 17.8 %all-gather = bf16[8,4,128]{2,1,0:T(4,128)(2,1)S(1)} all-gather(bf16[1,4,128]{2,1,0:T(4,128)(2,1)S(1)} %convert_bitcast_fusion.1), channel_id=1, replica_groups=mesh['seq'=8,'head'=4] {'seq'}, dimensions={0}, use_global_device_ids=true | all-gather | bytes 9216 | tf_op jit(solution)/shard_map/all_gather | solution.py:59
  39.9 0.1 fusion.40
  40.0 0.3 copy.128
  40.4 1.9 %fusion.59 = (f32[2,8,256]{2,1,0:T(8,128)}, f32[2,1,8,256,32]{3,4,2,0,1:T(8,128)}) fusion(bf16[32,128,1,1]{1,0,3,2:T(8,128)(2,1)S(1)} %bitcast.272, bf16[2,256,8,128]{3,2,1,0:T(8,128)(2,1)S(1)} %bitcast.248, pred[2,32]{1,0:T(4,128)(4,1)S(1)} %iota_compare_fusion.1), kind=kOutput, calls=%fused_computation.132 | convolution fusion | flops 33943552 | bytes 1597504 | tf_op jit(solution)/shard_map/bqhsd,chd->bhsqc/dot_general | solution.py:110
  42.3 1.1 fusion.56
  43.4 0.3 compare_and_fusion.1
  43.7 0.3 compare_and_fusion
  44.2 16.8 %all-gather.1 = bf16[8,4,128]{2,1,0:T(4,128)(2,1)S(1)} all-gather(bf16[1,4,128]{2,1,0:T(4,128)(2,1)S(1)} %convert_bitcast_fusion), channel_id=1, replica_groups=mesh['seq'=8,'head'=4] {'seq'}, dimensions={0}, use_global_device_ids=true | all-gather | bytes 9216 | tf_op jit(solution)/shard_map/all_gather | solution.py:60
  61.0 4.0 %collective-permute-start.3 = (bf16[128,128]{1,0:T(8,128)(2,1)S(1)}, bf16[128,128]{1,0:T(8,128)(2,1)}, u32[]{:S(2)}, u32[]{:S(2)}) collective-permute-start(bf16[128,128]{1,0:T(8,128)(2,1)S(1)} %collective-permute-done.2), channel_id=1, source_target_pairs={{0,4},{4,8},{8,12},{12,16},{16,20},{20,24},{24,28},{1,5},{5,9},{9,... | collective-permute-start | bytes 98312 | tf_op jit(solution)/shard_map/ppermute | solution.py:18
  65.0 1.9 %collective-permute-start.6 = (bf16[128,128]{1,0:T(8,128)(2,1)}, bf16[128,128]{1,0:T(8,128)(2,1)}, u32[]{:S(2)}, u32[]{:S(2)}) collective-permute-start(bf16[128,128]{1,0:T(8,128)(2,1)} %collective-permute-done.5), channel_id=1, source_target_pairs={{0,4},{4,8},{8,12},{12,16},{16,20},{20,24},{24,28},{1,5},{5,9},{9,... | collective-permute-start | bytes 98312 | tf_op jit(solution)/shard_map/ppermute | solution.py:18
  67.0 5.2 %fusion.60 = (f32[2,8,256]{2,1,0:T(8,128)}, f32[2,1,8,256,512]{3,4,2,0,1:T(8,128)}) fusion(bf16[2,256,8,128]{3,2,1,0:T(8,128)(2,1)S(1)} %bitcast.249, bf16[2,256,1,128]{3,1,0,2:T(8,128)(2,1)S(1)} %bitcast.263, bf16[2,256,1,128]{3,1,0,2:T(8,128)(2,1)S(1)} %bitcast.262, pred[2,256,512]{1,2,0:T(8,128)(4,1)S(1)} %compare_and_fusion.1), kind=kOutput, calls=%fused_computation.133 | convolution fusion | flops 543682560 | bytes 9977856 | tf_op jit(solution)/shard_map/bqhsd,bkhd->bhsqk/dot_general | solution.py:98
  72.2 5.2 %fusion.57 = (f32[2,8,256]{2,1,0:T(8,128)}, f32[2,1,8,256,512]{3,4,2,0,1:T(8,128)}) fusion(bf16[2,256,8,128]{3,2,1,0:T(8,128)(2,1)S(1)} %bitcast.246, bf16[2,256,1,128]{3,1,0,2:T(8,128)(2,1)S(1)} %bitcast.260, bf16[2,256,1,128]{3,1,0,2:T(8,128)(2,1)S(1)} %bitcast.261, pred[2,256,512]{1,2,0:T(8,128)(4,1)S(1)} %compare_and_fusion), kind=kOutput, calls=%fused_computation.130 | convolution fusion | flops 543682560 | bytes 9977856 | tf_op jit(solution)/shard_map/bqhsd,bkhd->bhsqk/dot_general | solution.py:98
  77.4 2.1 %collective-permute-start.4 = (bf16[128,128]{1,0:T(8,128)(2,1)}, bf16[128,128]{1,0:T(8,128)(2,1)}, u32[]{:S(2)}, u32[]{:S(2)}) collective-permute-start(bf16[128,128]{1,0:T(8,128)(2,1)} %collective-permute-done.3), channel_id=1, source_target_pairs={{0,4},{4,8},{8,12},{12,16},{16,20},{20,24},{24,28},{1,5},{5,9},{9,... | collective-permute-start | bytes 98312 | tf_op jit(solution)/shard_map/ppermute | solution.py:18
  79.6 0.1 copy.76
  79.7 0.1 copy.77
  80.1 1.5 collective-permute-start.7
  81.6 1.5 fusion.55
  83.3 1.0 fusion.61
  84.3 1.1 maximum_maximum_fusion.1
  85.3 5.6 %fusion.3 = f32[2,8,256]{2,1,0:T(8,128)S(1)} fusion(f32[2,1,8,256,32]{3,4,2,0,1:T(8,128)} %get-tuple-element.54, f32[2,1,8,256,256]{3,4,2,0,1:T(8,128)S(1)} %get-tuple-element.58, f32[2,1,8,256,512]{3,4,2,0,1:T(8,128)} %get-tuple-element.56, f32[2,8,256]{2,1,0:T(8,128)S(1)} %maximum_maximum_fusion.1), kind=kLoop, calls=%fused_computation.9 | loop fusion | flops 13103104 | bytes 13139968 | tf_op jit(solution)/shard_map/reduce_sum | solution.py:140
  91.0 4.2 %divide_convert_fusion.1 = bf16[2,1,8,256,800]{3,4,2,0,1:T(8,128)(2,1)} fusion(f32[2,1,8,256,32]{3,4,2,0,1:T(8,128)S(1)} %copy-done.5, f32[2,1,8,256,256]{3,4,2,0,1:T(8,128)S(1)} %get-tuple-element.58, f32[2,1,8,256,512]{3,4,2,0,1:T(8,128)S(1)} %bitcast.244, f32[2,8,256]{2,1,0:T(8,128)S(1)} %fusion.3, f32[2,8,256]{2,1,0:T(8,128)S(1)} %maximum_maximum_fusion.1), kind=kLoop, calls=%fused_computation.5 | loop fusion | flops 16384000 | bytes 19693568 | tf_op jit(solution)/shard_map/convert_element_type | solution.py:141
  95.2 1.5 fusion.54
  96.6 0.1 copy.84
  96.8 0.1 copy.85
  96.9 0.1 copy.86
  97.0 0.1 copy.87
  97.2 0.1 copy.88
  97.3 0.1 copy.89
  97.4 0.1 copy.82
  97.5 0.1 copy.83
  97.7 0.2 concatenate.93
  97.9 2.2 %fusion.9 = f32[2,128,8,256]{3,1,2,0:T(8,128)S(1)} fusion(bf16[2,1,8,256,800]{3,4,2,0,1:T(8,128)(2,1)} %divide_convert_fusion.1, bf16[2,256,1,128]{1,3,0,2:T(8,128)(2,1)S(1)} %concatenate.93), kind=kOutput, calls=%fused_computation.21 | convolution fusion | flops 268435456 | bytes 4325376 | tf_op jit(solution)/shard_map/bhsqk,bkhd->bqhsd/dot_general | solution.py:148
  100.1 1.7 %fusion.23 = f32[128,2,8,256]{3,0,2,1:T(8,128)S(1)} fusion(bf16[32,128,1,1]{1,0,3,2:T(8,128)(2,1)S(1)} %bitcast.270, bf16[2,1,8,256,800]{3,4,2,0,1:T(8,128)(2,1)} %divide_convert_fusion.1), kind=kOutput, calls=%fused_computation.48 | convolution fusion | flops 33554432 | bytes 2367488 | tf_op jit(solution)/shard_map/bhsqc,chd->bqhsd/dot_general | solution.py:151
  101.8 0.8 fusion.11
  102.6 1.5 copy.91
  104.1 2.6 %copy.157 = bf16[64,8,8,128]{3,1,2,0:T(8,128)(2,1)} copy(bf16[64,8,8,128]{3,2,1,0:T(8,128)(2,1)} %bitcast.256) | data formatting | bytes 2097152
  106.6 1.3 constant_dynamic-update-slice_fusion.9
  108.0 1.3 constant_dynamic-update-slice_fusion.8
  109.3 1.8 %fusion.58 = (f32[2,8,256]{2,1,0:T(8,128)S(1)}, f32[2,1,8,256,256]{3,4,2,0,1:T(8,128)S(1)}) fusion(bf16[2,256,8,128]{3,2,1,0:T(8,128)(2,1)S(1)} %bitcast.247, bf16[2,256,1,128]{3,1,0,2:T(8,128)(2,1)} %constant_dynamic-update-slice_fusion.8, pred[2,256]{1,0:T(4,128)(4,1)S(1)} %add_compare_fusion), kind=kOutput, calls=%fused_computation.131 | convolution fusion | flops 271577088 | bytes 5390848 | tf_op jit(solution)/shard_map/bqhsd,bkhd->bhsqk/dot_general | solution.py:104
  111.1 5.2 %fusion.2 = f32[2,8,256]{2,1,0:T(8,128)S(1)} fusion(f32[2,1,8,256,32]{3,4,2,0,1:T(8,128)S(1)} %get-tuple-element.48, f32[2,1,8,256,256]{3,4,2,0,1:T(8,128)S(1)} %get-tuple-element.52, f32[2,1,8,256,512]{3,4,2,0,1:T(8,128)} %get-tuple-element.50, f32[2,8,256]{2,1,0:T(8,128)S(1)} %maximum_maximum_fusion), kind=kLoop, calls=%fused_computation.8 | loop fusion | flops 13103104 | bytes 13139968 | tf_op jit(solution)/shard_map/reduce_sum | solution.py:140
  116.4 4.1 %divide_convert_fusion = bf16[2,1,8,256,800]{3,4,2,0,1:T(8,128)(2,1)} fusion(f32[2,1,8,256,32]{3,4,2,0,1:T(8,128)S(1)} %get-tuple-element.48, f32[2,1,8,256,256]{3,4,2,0,1:T(8,128)S(1)} %get-tuple-element.52, f32[2,1,8,256,512]{3,4,2,0,1:T(8,128)S(1)} %bitcast.242, f32[2,8,256]{2,1,0:T(8,128)S(1)} %fusion.2, f32[2,8,256]{2,1,0:T(8,128)S(1)} %maximum_maximum_fusion), kind=kLoop, calls=%fused_computation.4 | loop fusion | flops 16384000 | bytes 19693568 | tf_op jit(solution)/shard_map/convert_element_type | solution.py:141
  120.6 0.1 copy.104
  120.7 0.1 copy.105
  120.8 1.4 fusion.22
  122.2 0.2 concatenate.100
  122.5 2.0 %fusion.8 = f32[2,128,8,256]{3,1,2,0:T(8,128)S(1)} fusion(bf16[2,1,8,256,800]{3,4,2,0,1:T(8,128)(2,1)} %divide_convert_fusion, bf16[2,256,1,128]{1,3,0,2:T(8,128)(2,1)S(1)} %concatenate.100), kind=kOutput, calls=%fused_computation.19 | convolution fusion | flops 268435456 | bytes 4325376 | tf_op jit(solution)/shard_map/bhsqk,bkhd->bqhsd/dot_general | solution.py:148
  124.5 3.0 %fusion.10 = bf16[2,256,1,8,128]{1,4,3,0,2:T(8,128)(2,1)S(1)} fusion(f32[128,2,8,256]{3,0,2,1:T(8,128)S(1)} %fusion.22, f32[2,128,8,256]{3,1,2,0:T(8,128)S(1)} %fusion.8, bf16[2,1,8,256,800]{3,4,2,0,1:T(8,128)(2,1)} %divide_convert_fusion, bf16[2,256,1,128]{1,3,0,2:T(8,128)(2,1)S(1)} %copy.93, bf16[2,256,1,128]{1,3,0,2:T(8,128)(2,1)S(1)} %copy.92), kind=kOutput, calls=%fused_computation.24 | convolution fusion | flops 538968064 | bytes 9699328 | tf_op jit(solution)/shard_map/bhsqk,bkhd->bqhsd/dot_general | solution.py:145
  127.5 0.8 copy.107
  128.3 0.3 copy.156
  128.6 1.5 pad_maximum_fusion
  130.1 28.3 %all_to_all.19 = bf16[4,256,1024]{2,1,0:T(8,128)(2,1)S(1)} all-to-all(bf16[4,256,1024]{2,1,0:T(8,128)(2,1)S(1)} %bitcast.251), channel_id=1, replica_groups=mesh['seq'=8,'head'=4] {'head'}, dimensions={0} | all-to-all | bytes 4194304 | tf_op jit(solution)/shard_map/all_to_all | solution.py:156
  158.3 2.6 %copy.108 = bf16[256,4,1024]{0,2,1:T(8,128)(2,1)} copy(bf16[256,4,1024]{2,0,1:T(8,128)(2,1)S(1)} %bitcast.252) | data formatting | bytes 4194304 | tf_op jit(solution)/shard_map/all_to_all | solution.py:156
  160.9 4.1 %copy.109 = bf16[256,4096]{1,0:T(8,128)(2,1)} copy(bf16[256,4096]{0,1:T(8,128)(2,1)} %bitcast.253) | data formatting | bytes 4194304 | tf_op jit(solution)/shard_map/all_to_all | solution.py:156
  (81 shorter events, 1.3 us)
Async XLA Ops:
  0.0 21.9 %copy-start = (bf16[1,256]{1,0:T(2,128)(2,1)S(1)}, bf16[1,256]{1,0:T(2,128)(2,1)}, u32[]{:S(2)}) copy-start(bf16[1,256]{1,0:T(2,128)(2,1)} %param.9) | copy-start | bytes 1540
  0.0 21.9 %copy-start.3 = (bf16[1024,128]{1,0:T(8,128)(2,1)S(1)}, bf16[1024,128]{1,0:T(8,128)(2,1)}, u32[]{:S(2)}) copy-start(bf16[1024,128]{1,0:T(8,128)(2,1)} %param.6) | copy-start | bytes 786436
  0.0 39.8 %copy-start.4 = (bf16[1024,128]{1,0:T(8,128)(2,1)S(1)}, bf16[1024,128]{1,0:T(8,128)(2,1)}, u32[]{:S(2)}) copy-start(bf16[1024,128]{1,0:T(8,128)(2,1)} %param.7) | copy-start | bytes 786436
  1.2 42.5 %copy-start.8 = (bf16[128,128]{1,0:T(8,128)(2,1)}, bf16[128,128]{1,0:T(8,128)(2,1)S(1)}, u32[]{:S(2)}) copy-start(bf16[128,128]{1,0:T(8,128)(2,1)S(1)} %convert_element_type.44) | copy-start | bytes 98308
  1.3 59.7 %collective-permute-start.2 = (bf16[128,128]{1,0:T(8,128)(2,1)S(1)}, bf16[128,128]{1,0:T(8,128)(2,1)S(1)}, u32[]{:S(2)}, u32[]{:S(2)}) collective-permute-start(bf16[128,128]{1,0:T(8,128)(2,1)S(1)} %convert_element_type.44), channel_id=1, source_target_pairs={{0,4},{4,8},{8,12},{12,16},{16,20},{20,24},{24,28},{1,5},{5,9},{9,... | collective-permute-start | bytes 98312 | tf_op jit(solution)/shard_map/ppermute | solution.py:18
  7.0 59.9 %collective-permute-start.1 = (bf16[256,128]{1,0:T(8,128)(2,1)S(1)}, bf16[256,128]{1,0:T(8,128)(2,1)S(1)}, u32[]{:S(2)}, u32[]{:S(2)}) collective-permute-start(bf16[256,128]{1,0:T(8,128)(2,1)S(1)} %slice.243), channel_id=1, source_target_pairs={{0,4},{4,8},{8,12},{12,16},{16,20},{20,24},{24,28},{1,5},{5,9},{9,... | collective-permute-start | bytes 196616 | tf_op jit(solution)/shard_map/ppermute | solution.py:18
  11.6 55.3 %copy-start.6 = (bf16[128,128]{1,0:T(8,128)(2,1)}, bf16[128,128]{1,0:T(8,128)(2,1)S(1)}, u32[]{:S(2)}) copy-start(bf16[128,128]{1,0:T(8,128)(2,1)S(1)} %convert_element_type.47) | copy-start | bytes 98308
  11.6 53.3 %collective-permute-start.5 = (bf16[128,128]{1,0:T(8,128)(2,1)S(1)}, bf16[128,128]{1,0:T(8,128)(2,1)}, u32[]{:S(2)}, u32[]{:S(2)}) collective-permute-start(bf16[128,128]{1,0:T(8,128)(2,1)S(1)} %convert_element_type.47), channel_id=1, source_target_pairs={{0,4},{4,8},{8,12},{12,16},{16,20},{20,24},{24,28},{1,5},{5,9},{9,... | collective-permute-start | bytes 98312 | tf_op jit(solution)/shard_map/ppermute | solution.py:18
  16.5 63.0 %collective-permute-start = (bf16[256,128]{1,0:T(8,128)(2,1)S(1)}, bf16[256,128]{1,0:T(8,128)(2,1)S(1)}, u32[]{:S(2)}, u32[]{:S(2)}) collective-permute-start(bf16[256,128]{1,0:T(8,128)(2,1)S(1)} %slice.238), channel_id=1, source_target_pairs={{0,4},{4,8},{8,12},{12,16},{16,20},{20,24},{24,28},{1,5},{5,9},{9,... | collective-permute-start | bytes 196616 | tf_op jit(solution)/shard_map/ppermute | solution.py:18
  61.0 16.4 %copy-start.9 = (bf16[128,128]{1,0:T(8,128)(2,1)}, bf16[128,128]{1,0:T(8,128)(2,1)S(1)}, u32[]{:S(2)}) copy-start(bf16[128,128]{1,0:T(8,128)(2,1)S(1)} %collective-permute-done.2) | copy-start | bytes 98308
  61.0 16.4 %collective-permute-start.3 = (bf16[128,128]{1,0:T(8,128)(2,1)S(1)}, bf16[128,128]{1,0:T(8,128)(2,1)}, u32[]{:S(2)}, u32[]{:S(2)}) collective-permute-start(bf16[128,128]{1,0:T(8,128)(2,1)S(1)} %collective-permute-done.2), channel_id=1, source_target_pairs={{0,4},{4,8},{8,12},{12,16},{16,20},{20,24},{24,28},{1,5},{5,9},{9,... | collective-permute-start | bytes 98312 | tf_op jit(solution)/shard_map/ppermute | solution.py:18
  65.0 15.1 %collective-permute-start.6 = (bf16[128,128]{1,0:T(8,128)(2,1)}, bf16[128,128]{1,0:T(8,128)(2,1)}, u32[]{:S(2)}, u32[]{:S(2)}) collective-permute-start(bf16[128,128]{1,0:T(8,128)(2,1)} %collective-permute-done.5), channel_id=1, source_target_pairs={{0,4},{4,8},{8,12},{12,16},{16,20},{20,24},{24,28},{1,5},{5,9},{9,... | collective-permute-start | bytes 98312 | tf_op jit(solution)/shard_map/ppermute | solution.py:18
  77.4 4.2 %collective-permute-start.4 = (bf16[128,128]{1,0:T(8,128)(2,1)}, bf16[128,128]{1,0:T(8,128)(2,1)}, u32[]{:S(2)}, u32[]{:S(2)}) collective-permute-start(bf16[128,128]{1,0:T(8,128)(2,1)} %collective-permute-done.3), channel_id=1, source_target_pairs={{0,4},{4,8},{8,12},{12,16},{16,20},{20,24},{24,28},{1,5},{5,9},{9,... | collective-permute-start | bytes 98312 | tf_op jit(solution)/shard_map/ppermute | solution.py:18
  80.1 15.0 %collective-permute-start.7 = (bf16[128,128]{1,0:T(8,128)(2,1)}, bf16[128,128]{1,0:T(8,128)(2,1)S(1)}, u32[]{:S(2)}, u32[]{:S(2)}) collective-permute-start(bf16[128,128]{1,0:T(8,128)(2,1)} %collective-permute-done.6), channel_id=1, source_target_pairs={{0,4},{4,8},{8,12},{12,16},{16,20},{20,24},{24,28},{1,5},{5,9},{9,... | collective-permute-start | bytes 98312 | tf_op jit(solution)/shard_map/ppermute | solution.py:18
  83.3 7.7 %copy-start.10 = (bf16[2,256,1,128]{3,1,0,2:T(8,128)(2,1)}, bf16[2,256,1,128]{3,1,0,2:T(8,128)(2,1)S(1)}, u32[]{:S(2)}) copy-start(bf16[2,256,1,128]{3,1,0,2:T(8,128)(2,1)S(1)} %get-tuple-element.36) | copy-start | bytes 393220
  83.3 7.7 %slice-start.2 = ((s8[8388608]{0:T(1024)(128)(4,1)}), s8[4194304]{0:T(1024)(128)(4,1)S(1)}, s32[]{:S(2)}) async-start(s8[8388608]{0:T(1024)(128)(4,1)} %bitcast.243), calls=%async_computation.3 | async-start | bytes 8388608
  85.3 5.6 %slice-start.3 = ((s8[8388608]{0:T(1024)(128)(4,1)}), s8[4194304]{0:T(1024)(128)(4,1)S(1)}, s32[]{:S(2)}) async-start(s8[8388608]{0:T(1024)(128)(4,1)} %bitcast.243), calls=%async_computation.4 | async-start | bytes 8388608
  85.3 5.6 %copy-start.5 = (f32[2,1,8,256,32]{3,4,2,0,1:T(8,128)S(1)}, f32[2,1,8,256,32]{3,4,2,0,1:T(8,128)}, u32[]{:S(2)}) copy-start(f32[2,1,8,256,32]{3,4,2,0,1:T(8,128)} %get-tuple-element.54) | copy-start | bytes 1572868
  91.0 4.2 %copy-start.7 = (bf16[128,128]{1,0:T(8,128)(2,1)S(1)}, bf16[128,128]{1,0:T(8,128)(2,1)}, u32[]{:S(2)}) copy-start(bf16[128,128]{1,0:T(8,128)(2,1)} %copy-done.6) | copy-start | bytes 98308
  97.9 3.9 %copy-start.2 = (bf16[2,1,8,256,800]{3,4,2,0,1:T(8,128)(2,1)S(1)}, bf16[2,1,8,256,800]{3,4,2,0,1:T(8,128)(2,1)}, u32[]{:S(2)}) copy-start(bf16[2,1,8,256,800]{3,4,2,0,1:T(8,128)(2,1)} %divide_convert_fusion.1) | copy-start | bytes 19660804
  102.6 8.5 %copy-start.11 = (f32[2,8,256]{2,1,0:T(8,128)S(1)}, f32[2,8,256]{2,1,0:T(8,128)}, u32[]{:S(2)}) copy-start(f32[2,8,256]{2,1,0:T(8,128)} %get-tuple-element.47) | copy-start | bytes 49156
  102.6 8.5 %copy-start.12 = (f32[2,8,256]{2,1,0:T(8,128)S(1)}, f32[2,8,256]{2,1,0:T(8,128)}, u32[]{:S(2)}) copy-start(f32[2,8,256]{2,1,0:T(8,128)} %get-tuple-element.49) | copy-start | bytes 49156
  109.3 7.1 %slice-start = ((s8[8388608]{0:T(1024)(128)(4,1)}), s8[4194304]{0:T(1024)(128)(4,1)S(1)}, s32[]{:S(2)}) async-start(s8[8388608]{0:T(1024)(128)(4,1)} %bitcast.241), calls=%async_computation.1 | async-start | bytes 8388608
  111.1 5.3 %slice-start.1 = ((s8[8388608]{0:T(1024)(128)(4,1)}), s8[4194304]{0:T(1024)(128)(4,1)S(1)}, s32[]{:S(2)}) async-start(s8[8388608]{0:T(1024)(128)(4,1)} %bitcast.241), calls=%async_computation.2 | async-start | bytes 8388608
  116.4 4.1 %copy-start.14 = (bf16[64,128]{1,0:T(8,128)(2,1)S(1)}, bf16[64,128]{1,0:T(8,128)(2,1)}, u32[]{:S(2)}) copy-start(bf16[64,128]{1,0:T(8,128)(2,1)} %get-tuple-element.20) | copy-start | bytes 49156
  116.4 4.3 %copy-start.13 = (bf16[64,128]{1,0:T(8,128)(2,1)S(1)}, bf16[64,128]{1,0:T(8,128)(2,1)}, u32[]{:S(2)}) copy-start(bf16[64,128]{1,0:T(8,128)(2,1)} %get-tuple-element.21) | copy-start | bytes 49156
  128.6 36.4 %copy-start.1 = (bf16[1,256]{1,0:T(2,128)(2,1)S(1)}, bf16[1,256]{1,0:T(2,128)(2,1)}, u32[]{:S(2)}) copy-start(bf16[1,256]{1,0:T(2,128)(2,1)} %param.9) | copy-start | bytes 1540
where the time goes:
time: 166 us; the launch traced here: 165 us
  blocking collectives  62.8 us (38%)
  matrix products  30 us (18%)
  other arithmetic  26.3 us (16%)
  starting transfers between devices  24.8 us (15%)
  local copies, waits for them, and re-layouts  20.6 us (12%)
    all_to_all x1, blocking collectives, body(): lax.all_to_all(attended, 'head', split_axis=0, concat_axis=1, tiled=True)  28.3 us
    ppermute x8, starting transfers between devices, passed_along(): return lax.ppermute(array, axis, pairs)  24.8 us
    all_gather x1, blocking collectives, body(): lax.all_gather(summary_key_rows, 'seq', axis=0, tiled=True)  17.8 us
    all_gather x1, blocking collectives, body(): lax.all_gather(coarse_values, 'seq', axis=0, tiled=True)  16.8 us
    reduce_sum x2, other arithmetic, body(): row_total = jnp.sum(exponent, axis=-1, keepdims=True)  10.8 us
    dot_general x2, matrix products, body(): jnp.einsum('bqhsd,bkhd->bhsqk', query_rows, local_keys, preferred_element...  10.4 us
    convert_element_type x2, other arithmetic, body(): softmax_weights = (exponent / row_total).astype(jnp.bfloat16)  8.28 us
    all_to_all x2, local copies, waits for them, and re-layouts, body(): lax.all_to_all(attended, 'head', split_axis=0, concat_axis=1, tiled=True)  6.62 us
  transfers between devices with their start and end apart: 8, of which 0 were waited for; matrix products, arithmetic and copies ran while one was open for 21% of the time, Pallas kernels for 0%

commit v1 on v0

v1 whole, which is shorter than its diff:
```python
import functools
import math

import jax
import jax.numpy as jnp
from jax import lax
from jax.experimental import pallas as pl
from jax.experimental.pallas import tpu as pltpu
from jax.sharding import PartitionSpec as P

HEAD_DIM = 128
BLK = 256
GROUP = 8
MIDS = 256
MIDB = 8
PER_GROUP = BLK // GROUP
LANES = 128
NEG = -1e30
EXP_SCALE = math.log2(math.e) / math.sqrt(HEAD_DIM)
BF16 = jnp.bfloat16
F32 = jnp.float32


def round_up(value, multiple):
    return -(-value // multiple) * multiple


def cyclic(array, axis, by):
    size = lax.axis_size(axis)
    return lax.ppermute(array, axis, [(i, (i + by) % size) for i in range(size)])


def exchange(array, axis, flip):
    size = lax.axis_size(axis)
    return lax.ppermute(array, axis, [(i, i ^ flip) for i in range(size)])


def pool_kernel(block_count, last_blocks, slot, keys_ref, values_ref, mid_ref, coarse_ref,
                coarse_out, mids_out, last_out, first_out):
    rows = block_count * PER_GROUP
    repeat = (
        lax.broadcasted_iota(jnp.int32, (GROUP, BLK), 1) % GROUP
        == lax.broadcasted_iota(jnp.int32, (GROUP, BLK), 0)
    ).astype(BF16)
    tiled = jnp.dot(mid_ref[...], repeat, preferred_element_type=F32)
    owner = lax.broadcasted_iota(jnp.int32, (PER_GROUP, BLK), 1) // GROUP
    mine = owner == lax.broadcasted_iota(jnp.int32, (PER_GROUP, BLK), 0)
    mid_weights = jnp.where(mine, jnp.broadcast_to(tiled, (PER_GROUP, BLK)), 0.0)
    coarse_weights = coarse_ref[...].astype(F32)
    row = lax.broadcasted_iota(jnp.int32, (slot, BLK), 0)
    for source, mid_base, coarse_base in ((keys_ref, 0, 0), (values_ref, rows, slot)):
        total = jnp.zeros((slot, HEAD_DIM), F32)
        for block in range(block_count):
            here = source[block * BLK : (block + 1) * BLK, :]
            weights = jnp.concatenate(
                [mid_weights, jnp.where(row == block, jnp.broadcast_to(coarse_weights, (slot, BLK)), 0.0)]
            ).astype(BF16)
            pooled = jnp.dot(weights, here, preferred_element_type=F32)
            mids = pooled[:PER_GROUP].astype(BF16)
            total = total + pooled[PER_GROUP:]
            start = mid_base + block * PER_GROUP
            mids_out[start : start + PER_GROUP, :] = mids
            first_out[2 * BLK + start : 2 * BLK + start + PER_GROUP, :] = mids
            late = block - (block_count - last_blocks)
            if late >= 0:
                start = (mid_base // rows) * last_blocks * PER_GROUP + late * PER_GROUP
                last_out[start : start + PER_GROUP, :] = mids
        coarse_out[coarse_base : coarse_base + slot, :] = total.astype(BF16)
    edge = (block_count - 1) * BLK
    first_out[:BLK, :] = keys_ref[edge : edge + BLK, :]
    first_out[BLK : 2 * BLK, :] = values_ref[edge : edge + BLK, :]


def pool(keys, values, mid_pool, coarse_pool, block_count, last_blocks, slot):
    rows = block_count * PER_GROUP
    shapes = (
        (2 * slot, HEAD_DIM),
        (2 * rows, HEAD_DIM),
        (2 * last_blocks * PER_GROUP, HEAD_DIM),
        (2 * BLK + 2 * rows, HEAD_DIM),
    )
    return pl.pallas_call(
        functools.partial(pool_kernel, block_count, last_blocks, slot),
        out_shape=[jax.ShapeDtypeStruct(shape, BF16) for shape in shapes],
        cost_estimate=pl.CostEstimate(
            flops=4 * keys.size * (PER_GROUP + slot), bytes_accessed=6 * keys.size, transcendentals=0
        ),
        name="pool",
    )(keys, values, mid_pool, coarse_pool)


def attend_kernel(geometry, info_ref, q_ref, keys_ref, values_ref, first_ref, *rest):
    block_count, hops, last_blocks, slot, reach, width, step_heads = geometry
    further = rest[: hops - 1]
    mids_ref, coarse_ref, _, out_ref, mid_scratch, all_keys, all_values, bias = rest[hops - 1 :]
    rows = block_count * PER_GROUP
    target = info_ref[0]
    device = info_ref[1]
    block = device * block_count + target
    coarse_at = MIDS
    prev_at = MIDS + width
    own_at = prev_at + BLK

    @pl.when(pl.program_id(0) == 0)
    def _():
        for which, everything in ((0, all_keys), (1, all_values)):
            at = 0
            for index in range(hops - 2, -1, -1):
                ref = further[index]
                size = ref.shape[0] // 2
                mid_scratch[at : at + size, :] = ref[which * size : (which + 1) * size, :]
                at += size
            start = 2 * BLK + which * rows
            mid_scratch[at : at + rows, :] = first_ref[start : start + rows, :]
            at += rows
            mid_scratch[at : at + rows, :] = mids_ref[which * rows : (which + 1) * rows, :]
            window = pl.ds(pl.multiple_of(target * PER_GROUP, PER_GROUP), MIDS)
            everything[:MIDS, :HEAD_DIM] = mid_scratch[window, :]
            wide = coarse_ref[...].astype(F32).reshape(reach, 2, slot, HEAD_DIM)[:, which]
            wide = wide.reshape(reach * slot, HEAD_DIM)
            if width > reach * slot:
                wide = jnp.concatenate([wide, jnp.zeros((width - reach * slot, HEAD_DIM), F32)])
            everything[coarse_at : coarse_at + width, :HEAD_DIM] = wide.astype(BF16)
            source = (keys_ref, values_ref)[which]
            before = pl.ds(pl.multiple_of(jnp.maximum(target - 1, 0) * BLK, BLK), BLK)
            own = pl.ds(pl.multiple_of(target * BLK, BLK), BLK)
            everything[prev_at : prev_at + BLK, :HEAD_DIM] = source[before, :]
            everything[own_at : own_at + BLK, :HEAD_DIM] = source[own, :]

            @pl.when(target == 0)
            def _():
                everything[prev_at : prev_at + BLK, :HEAD_DIM] = first_ref[
                    which * BLK : (which + 1) * BLK, :
                ]

        all_values[:, HEAD_DIM:] = jnp.ones((own_at + BLK, HEAD_DIM), BF16)
        lane = lax.broadcasted_iota(jnp.int32, (8, own_at), 1)
        mid_ok = lane >= (MIDB + 1 - block) * PER_GROUP
        far = (lane - coarse_at) // slot
        nth = (lane - coarse_at) % slot
        coarse_ok = (
            (nth < block_count)
            & (far < reach)
            & (far <= device)
            & (far * block_count - nth + target >= MIDB + 2)
        )
        mid_bias = jnp.where(mid_ok, 0.0, NEG)
        coarse_bias = jnp.where(coarse_ok, 0.0, NEG)
        prev_bias = jnp.where(block * (lane + 1) >= 1, 0.0, NEG)
        bias[...] = jnp.where(
            lane < coarse_at, mid_bias, jnp.where(lane < prev_at, coarse_bias, prev_bias)
        )

    causal = lax.broadcasted_iota(jnp.int32, (BLK, BLK), 0) >= lax.broadcasted_iota(
        jnp.int32, (BLK, BLK), 1
    )
    for head in range(step_heads):
        columns = slice(head * HEAD_DIM, (head + 1) * HEAD_DIM)
        scores = lax.dot_general(
            q_ref[:, columns], all_keys[...], (((1,), (1,)), ((), ())), preferred_element_type=F32
        )
        left = scores[:, :own_at] + bias[0:1, :]
        own = jnp.where(causal, scores[:, own_at:], NEG)
        top = jnp.maximum(
            jnp.max(left, axis=-1, keepdims=True), jnp.max(own, axis=-1, keepdims=True)
        )
        left = jnp.exp2((left - top) * EXP_SCALE).astype(BF16)
        own = jnp.exp2((own - top) * EXP_SCALE).astype(BF16)
        mixed = jnp.dot(left, all_values[:own_at, :], preferred_element_type=F32) + jnp.dot(
            own, all_values[own_at:, :], preferred_element_type=F32
        )
        out_ref[:, columns] = (mixed[:, :HEAD_DIM] / mixed[:, HEAD_DIM:]).astype(BF16)


def attend(info, queries, shared, after, head_start, heads, geometry, full_columns=None):
    block_count, hops, last_blocks, slot, reach, width, step_heads = geometry
    step = step_heads * HEAD_DIM
    first = head_start // step_heads
    total = MIDS + width + 2 * BLK
    out_columns = heads * HEAD_DIM if full_columns is None else full_columns
    own_steps = queries.shape[1] // step
    if full_columns is None:
        out_map = lambda i, info: (0, i)
    else:
        out_map = lambda i, info: (0, info[2] * own_steps + i)
    whole = [pl.BlockSpec(a.shape, lambda i, info: (0, 0)) for a in shared]
    mid_rows = (hops + 1) * block_count * PER_GROUP
    return pl.pallas_call(
        functools.partial(attend_kernel, geometry),
        grid_spec=pltpu.PrefetchScalarGridSpec(
            num_scalar_prefetch=1,
            grid=(heads // step_heads,),
            in_specs=[pl.BlockSpec((BLK, step), lambda i, info: (info[0], first + i))]
            + whole
            + [pl.BlockSpec(memory_space=pl.ANY)],
            out_specs=pl.BlockSpec((BLK, step), out_map),
            scratch_shapes=[
                pltpu.VMEM((mid_rows, HEAD_DIM), BF16),
                pltpu.VMEM((total, HEAD_DIM), BF16),
                pltpu.VMEM((total, 2 * HEAD_DIM), BF16),
                pltpu.VMEM((8, MIDS + width + BLK), F32),
            ],
        ),
        out_shape=jax.ShapeDtypeStruct((BLK, out_columns), BF16),
        compiler_params=pltpu.CompilerParams(vmem_limit_bytes=32 * 1024 * 1024),
        cost_estimate=pl.CostEstimate(
            flops=6 * BLK * heads * total * HEAD_DIM,
            bytes_accessed=4 * BLK * heads * HEAD_DIM + 1024 * 1024,
            transcendentals=BLK * heads * total,
        ),
        name="attend",
    )(info, queries, *shared, after)


def place_kernel(info_ref, piece_ref, _, out_ref):
    out_ref[...] = piece_ref[...]


def place(info, output, piece, at, flip, columns):
    step = math.gcd(piece.shape[1], at) if at else piece.shape[1]
    per_device = columns // step
    return pl.pallas_call(
        place_kernel,
        grid_spec=pltpu.PrefetchScalarGridSpec(
            num_scalar_prefetch=1,
            grid=(piece.shape[1] // step,),
            in_specs=[
                pl.BlockSpec((BLK, step), lambda i, info: (0, i)),
                pl.BlockSpec(memory_space=pl.ANY),
            ],
            out_specs=pl.BlockSpec(
                (BLK, step), lambda i, info: (0, (info[2] ^ flip) * per_device + at // step + i)
            ),
        ),
        out_shape=jax.ShapeDtypeStruct(output.shape, output.dtype),
        input_output_aliases={2: 0},
        cost_estimate=pl.CostEstimate(
            flops=piece.size, bytes_accessed=4 * piece.size, transcendentals=0
        ),
        name="place",
    )(info, piece, output)


def body(queries, keys, values, mid_pool, coarse_pool):
    tokens_here, columns = queries.shape
    heads_here = columns // HEAD_DIM
    block_count = tokens_here // BLK
    members = lax.axis_size("head")
    length = lax.axis_size("seq")
    assert keys.shape[1] == HEAD_DIM and block_count == members
    assert block_count <= MIDB and members & (members - 1) == 0
    device = lax.axis_index("seq")
    member = lax.axis_index("head")
    hops = -(-(MIDB + 1) // block_count)
    last_blocks = MIDB + 1 - (hops - 1) * block_count
    slot = round_up(block_count, 8)

    coarse, mids, last, first = pool(
        keys, values, mid_pool, coarse_pool, block_count, last_blocks, slot
    )
    near = cyclic(first, "seq", 1)
    further = [cyclic(mids, "seq", by) for by in range(2, hops)] + [cyclic(last, "seq", hops)]
    reach = 1
    while reach < length:
        coarse = jnp.concatenate([coarse, cyclic(coarse, "seq", reach)])
        reach *= 2
    width = round_up(reach * slot, LANES)
    geometry = (block_count, hops, last_blocks, slot, reach, width, 2)
    shared = (keys, values, near, *further, mids, coarse)

    def info(flip):
        return jnp.stack([member ^ flip, device, member]).astype(jnp.int32)

    plan = []
    for flip in range(members // 2, members):
        half = heads_here // 2 if flip > members // 2 else heads_here // 4
        plan += [(flip, 0, half), (flip, half, heads_here - half)]
    plan += [(flip, 0, heads_here) for flip in range(1, members // 2)]
    after = coarse
    arrived = []
    for flip, start, heads in plan:
        after = attend(info(flip), queries, shared, after, start, heads, geometry)
        arrived.append((flip, start, exchange(after, "head", flip)))
    output = attend(
        info(0), queries, shared, after, 0, heads_here, geometry, full_columns=members * columns
    )
    order = [p for p in arrived if p[0] < members // 2] + [p for p in arrived if p[0] >= members // 2]
    for flip, start, piece in order:
        output = place(info(0), output, piece, start * HEAD_DIM, flip, columns)
    return output


def solution(mesh):
    return jax.shard_map(
        body,
        mesh=mesh,
        in_specs=(
            P("seq", "head"),
            P("seq", "head"),
            P("seq", "head"),
            P("head", None),
            P("head", None),
        ),
        out_specs=P(("seq", "head"), None),
        check_vma=False,
    )
```

time: 166 us -> 81.5 us (0.49)
  blocking collectives: 62.8 us -> 0 us
  Pallas kernels: 0 us -> 34.8 us
  matrix products: 30 us -> 0 us
  other arithmetic: 26.3 us -> 1.66 us
  waiting for transfers between devices: 0.02 us -> 23.2 us
  starting transfers between devices: 24.8 us -> 12.5 us
  local copies, waits for them, and re-layouts: 20.6 us -> 8.63 us
    pallas_call x0 -> x12, Pallas kernels: none -> 34.8 us  [the longest x6 20.1 us: attend(): pl.pallas_call(functools.partial(attend_kernel, geometry), grid_spec=pltp...]
    all_gather x2 -> x0, blocking collectives: 34.6 us -> none  [the longest x1 17.8 us: body(): lax.all_gather(summary_key_rows, 'seq', axis=0, tiled=True)]
    all_to_all x1 -> x0, blocking collectives: 28.3 us -> none  [body(): lax.all_to_all(attended, 'head', split_axis=0, concat_axis=1, tiled=True)]
    dot_general x14 -> x0, matrix products: 27.6 us -> none  [the longest x2 10.4 us: body(): jnp.einsum('bqhsd,bkhd->bhsqk', query_rows, local_keys, preferred_element...]
    ppermute x8 -> x11, waiting for transfers between devices: 0.02 us -> 23.2 us  [the longest x5 13.1 us: exchange(): return lax.ppermute(array, axis, [(i, i ^ flip) for i in range(size)])]
    ppermute x8 -> x11, starting transfers between devices: 24.8 us -> 12.5 us  [the longest x6 8.6 us: cyclic(): lax.ppermute(array, axis, [(i, (i + by) % size) for i in range(size)])]
    reduce_sum x2 -> x0, other arithmetic: 10.8 us -> none  [body(): row_total = jnp.sum(exponent, axis=-1, keepdims=True)]
    convert_element_type x4 -> x0, other arithmetic: 8.3 us -> none  [the longest x2 8.28 us: body(): softmax_weights = (exponent / row_total).astype(jnp.bfloat16)]
  transfers between devices with their start and end apart: 8 -> 11, of which waited for: 0 -> 3; matrix products, arithmetic and copies ran while one was open for 21% -> 3% of each run, Pallas kernels for 0% -> 19%
where the time goes in v1:
time: 81.5 us; the launch traced here: 80.9 us
  Pallas kernels  34.8 us (43%)
  waiting for transfers between devices  23.2 us (28%)
  starting transfers between devices  12.5 us (15%)
  local copies, waits for them, and re-layouts  8.63 us (11%)
  other arithmetic  1.66 us (2%)
    pallas_call x6, Pallas kernels, attend(): pl.pallas_call(functools.partial(attend_kernel, geometry), grid_spec=pltp...  20.1 us
    ppermute x5, waiting for transfers between devices, exchange(): return lax.ppermute(array, axis, [(i, i ^ flip) for i in range(size)])  13.1 us
    pallas_call x5, Pallas kernels, place(): pl.pallas_call(place_kernel, grid_spec=pltpu.PrefetchScalarGridSpec(num_s...  12.7 us
    ppermute x6, waiting for transfers between devices, cyclic(): lax.ppermute(array, axis, [(i, (i + by) % size) for i in range(size)])  10.1 us
    unnamed x25, local copies, waits for them, and re-layouts  8.63 us
    ppermute x6, starting transfers between devices, cyclic(): lax.ppermute(array, axis, [(i, (i + by) % size) for i in range(size)])  8.6 us
    ppermute x5, starting transfers between devices, exchange(): return lax.ppermute(array, axis, [(i, i ^ flip) for i in range(size)])  3.92 us
    pallas_call x1, Pallas kernels, pool(): pl.pallas_call(functools.partial(pool_kernel, block_count, last_blocks, s...  2.05 us
  transfers between devices with their start and end apart: 11, of which 3 were waited for; matrix products, arithmetic and copies ran while one was open for 3% of the time, Pallas kernels for 19%

profile of v1, /device:TPU:0, one launch (start us, length us, event | category | flops | bytes accessed | tf_op | source)
XLA Modules:
  0.0 80.9 jit_solution(4407461046392637804)
XLA Ops:
  0.0 2.1 %pool.1 = (bf16[16,128]{1,0:T(8,128)(2,1)}, bf16[256,128]{1,0:T(8,128)(2,1)}, bf16[64,128]{1,0:T(8,128)(2,1)}, bf16[768,128]{1,0:T(8,128)(2,1)}) custom-call(bf16[1024,128]{1,0:T(8,128)(2,1)} %keys_ref.13, bf16[1024,128]{1,0:T(8,128)(2,1)} %values_ref.13, bf16[1,8]{1,0:T(2,128)(2,1)} %mid_ref.1, bf16[1,256]{1,0:T(2,128)(2,1)} %coarse_ref.1), custom_call_target="tpu_custom_call" | custom-call | flops 20971520 | bytes 786432 | tf_op jit(solution)/shard_map/pool/pallas_call | solution.py:82
  2.1 3.0 %collective-permute-start.3 = (bf16[16,128]{1,0:T(8,128)(2,1)}, bf16[16,128]{1,0:T(8,128)(2,1)S(1)}, u32[]{:S(2)}, u32[]{:S(2)}) collective-permute-start(bf16[16,128]{1,0:T(8,128)(2,1)} %get-tuple-element.12), channel_id=1, source_target_pairs={{0,4},{4,8},{8,12},{12,16},{16,20},{20,24},{24,28},{28,0},{1,5},{5... | collective-permute-start | bytes 12296 | tf_op jit(solution)/shard_map/ppermute | solution.py:30
  5.0 2.6 %collective-permute-start.2 = (bf16[64,128]{1,0:T(8,128)(2,1)}, bf16[64,128]{1,0:T(8,128)(2,1)S(1)}, u32[]{:S(2)}, u32[]{:S(2)}) collective-permute-start(bf16[64,128]{1,0:T(8,128)(2,1)} %get-tuple-element.11), channel_id=1, source_target_pairs={{0,12},{4,16},{8,20},{12,24},{16,28},{20,0},{24,4},{28,8},{1,13},{... | collective-permute-start | bytes 49160 | tf_op jit(solution)/shard_map/ppermute | solution.py:30
  7.6 1.6 %collective-permute-start.1 = (bf16[256,128]{1,0:T(8,128)(2,1)}, bf16[256,128]{1,0:T(8,128)(2,1)S(1)}, u32[]{:S(2)}, u32[]{:S(2)}) collective-permute-start(bf16[256,128]{1,0:T(8,128)(2,1)} %get-tuple-element.10.rest_2_), channel_id=1, source_target_pairs={{0,8},{4,12},{8,16},{12,20},{16,24},{20,28},{24,0},{28,4},{1,9},{5... | collective-permute-start | bytes 196616 | tf_op jit(solution)/shard_map/ppermute | solution.py:30
  9.2 1.5 %collective-permute-start = (bf16[768,128]{1,0:T(8,128)(2,1)}, bf16[768,128]{1,0:T(8,128)(2,1)S(1)}, u32[]{:S(2)}, u32[]{:S(2)}) collective-permute-start(bf16[768,128]{1,0:T(8,128)(2,1)} %get-tuple-element.9), channel_id=1, source_target_pairs={{0,4},{4,8},{8,12},{12,16},{16,20},{20,24},{24,28},{28,0},{1,5},{5... | collective-permute-start | bytes 589832 | tf_op jit(solution)/shard_map/ppermute | solution.py:30
  10.7 0.7 constant_dynamic-update-slice_fusion.3
  11.3 0.1 add_add_fusion.2.info_ref
  11.4 0.1 add_add_fusion.1.info_ref
  11.5 0.1 add_add_fusion.3.info_ref
  11.6 0.0 collective-permute-done.3
  11.6 0.7 pad_maximum_fusion.1
  12.2 0.0 collective-permute-start.4
  12.2 5.4 %collective-permute-done.4 = bf16[32,128]{1,0:T(8,128)(2,1)S(1)} collective-permute-done((bf16[32,128]{1,0:T(8,128)(2,1)S(1)}, bf16[32,128]{1,0:T(8,128)(2,1)S(1)}, u32[]{:S(2)}, u32[]{:S(2)}) %collective-permute-start.4) | collective-permute-done | bytes 8224 | tf_op jit(solution)/shard_map/ppermute | solution.py:30
  17.7 0.7 pad_maximum_fusion
  18.4 0.0 collective-permute-start.5
  18.4 4.6 %collective-permute-done.5 = bf16[64,128]{1,0:T(8,128)(2,1)S(1)} collective-permute-done((bf16[64,128]{1,0:T(8,128)(2,1)S(1)}, bf16[64,128]{1,0:T(8,128)(2,1)S(1)}, u32[]{:S(2)}, u32[]{:S(2)}) %collective-permute-start.5) | collective-permute-done | bytes 16416 | tf_op jit(solution)/shard_map/ppermute | solution.py:30
  23.0 0.0 collective-permute-done.2.rest_1_
  23.0 0.0 collective-permute-done.1.rest_0_
  23.0 0.0 collective-permute-done.first_ref
  23.0 0.0 copy-start
  23.0 1.6 %copy-done = bf16[1024,1024]{1,0:T(8,128)(2,1)S(1)} copy-done((bf16[1024,1024]{1,0:T(8,128)(2,1)S(1)}, bf16[1024,1024]{1,0:T(8,128)(2,1)}, u32[]{:S(2)}) %copy-start) | copy-done | bytes 2097176
  24.6 0.0 copy-start.2
  24.6 0.9 %copy-done.2 = bf16[1024,128]{1,0:T(8,128)(2,1)S(1)} copy-done((bf16[1024,128]{1,0:T(8,128)(2,1)S(1)}, bf16[1024,128]{1,0:T(8,128)(2,1)}, u32[]{:S(2)}) %copy-start.2) | copy-done | bytes 262168
  25.6 0.0 copy-start.3
  25.6 0.9 %copy-done.3 = bf16[1024,128]{1,0:T(8,128)(2,1)S(1)} copy-done((bf16[1024,128]{1,0:T(8,128)(2,1)S(1)}, bf16[1024,128]{1,0:T(8,128)(2,1)}, u32[]{:S(2)}) %copy-start.3) | copy-done | bytes 262168
  26.5 0.0 copy-start.4
  26.5 0.8 %copy-done.4 = bf16[256,128]{1,0:T(8,128)(2,1)S(1)} copy-done((bf16[256,128]{1,0:T(8,128)(2,1)S(1)}, bf16[256,128]{1,0:T(8,128)(2,1)}, u32[]{:S(2)}) %copy-start.4) | copy-done | bytes 65560
  27.4 1.6 %attend.6.rest_4_ = bf16[256,256]{1,0:T(8,128)(2,1)S(1)} custom-call(s32[3]{0:T(128)S(1)} %add_add_fusion.2.info_ref, bf16[1024,1024]{1,0:T(8,128)(2,1)S(1)} %copy-done, bf16[1024,128]{1,0:T(8,128)(2,1)S(1)} %copy-done.2, bf16[1024,128]{1,0:T(8,128)(2,1)S(1)} %copy-done.3, bf16[768,128]{1,0:T(8,128)(2,1)S(1)} %collective-permute-done.first_ref, ...), custom_call_target="tpu_custom_call" | custom-call | flops 352321536 | bytes 1310720 | tf_op jit(solution)/shard_map/attend/pallas_call | solution.py:188
  28.9 0.0 copy-start.1
  28.9 3.6 %attend.7.rest_4_ = bf16[256,768]{1,0:T(8,128)(2,1)S(1)} custom-call(s32[3]{0:T(128)S(1)} %add_add_fusion.2.info_ref, bf16[1024,1024]{1,0:T(8,128)(2,1)S(1)} %copy-done, bf16[1024,128]{1,0:T(8,128)(2,1)S(1)} %copy-done.2, bf16[1024,128]{1,0:T(8,128)(2,1)S(1)} %copy-done.3, bf16[768,128]{1,0:T(8,128)(2,1)S(1)} %collective-permute-done.first_ref, ...), custom_call_target="tpu_custom_call" | custom-call | flops 1056964608 | bytes 1835008 | tf_op jit(solution)/shard_map/attend/pallas_call | solution.py:188
  32.5 0.0 copy-done.1
  32.5 2.6 %attend.8.rest_4_ = bf16[256,512]{1,0:T(8,128)(2,1)S(1)} custom-call(s32[3]{0:T(128)S(1)} %add_add_fusion.1.info_ref, bf16[1024,1024]{1,0:T(8,128)(2,1)S(1)} %copy-done.1, bf16[1024,128]{1,0:T(8,128)(2,1)S(1)} %copy-done.2, bf16[1024,128]{1,0:T(8,128)(2,1)S(1)} %copy-done.3, bf16[768,128]{1,0:T(8,128)(2,1)S(1)} %collective-permute-done.first_ref, ...), custom_call_target="tpu_custom_call" | custom-call | flops 704643072 | bytes 1572864 | tf_op jit(solution)/shard_map/attend/pallas_call | solution.py:188
  35.1 2.6 %attend.9.rest_4_ = bf16[256,512]{1,0:T(8,128)(2,1)S(1)} custom-call(s32[3]{0:T(128)S(1)} %add_add_fusion.1.info_ref, bf16[1024,1024]{1,0:T(8,128)(2,1)S(1)} %copy-done.1, bf16[1024,128]{1,0:T(8,128)(2,1)S(1)} %copy-done.2, bf16[1024,128]{1,0:T(8,128)(2,1)S(1)} %copy-done.3, bf16[768,128]{1,0:T(8,128)(2,1)S(1)} %collective-permute-done.first_ref, ...), custom_call_target="tpu_custom_call" | custom-call | flops 704643072 | bytes 1572864 | tf_op jit(solution)/shard_map/attend/pallas_call | solution.py:188
  37.8 4.5 %attend.10.rest_4_ = bf16[256,1024]{1,0:T(8,128)(2,1)S(1)} custom-call(s32[3]{0:T(128)S(1)} %add_add_fusion.3.info_ref, bf16[1024,1024]{1,0:T(8,128)(2,1)S(1)} %copy-done.1, bf16[1024,128]{1,0:T(8,128)(2,1)S(1)} %copy-done.2, bf16[1024,128]{1,0:T(8,128)(2,1)S(1)} %copy-done.3, bf16[768,128]{1,0:T(8,128)(2,1)S(1)} %collective-permute-done.first_ref, ...), custom_call_target="tpu_custom_call" | custom-call | flops 1409286144 | bytes 2097152 | tf_op jit(solution)/shard_map/attend/pallas_call | solution.py:188
  42.3 0.1 collective-permute-start.10
  42.4 1.6 %collective-permute-start.8 = (bf16[256,768]{1,0:T(8,128)(2,1)S(1)}, bf16[256,768]{1,0:T(8,128)(2,1)S(1)}, u32[]{:S(2)}, u32[]{:S(2)}) collective-permute-start(bf16[256,768]{1,0:T(8,128)(2,1)S(1)} %attend.7.rest_4_), channel_id=1, source_target_pairs={{0,2},{1,3},{2,0},{3,1},{4,6},{5,7},{6,4},{7,5},{8,10},{9,11},{10,... | collective-permute-start | bytes 1179656 | tf_op jit(solution)/shard_map/ppermute | solution.py:35
  44.0 0.2 collective-permute-start.7
  44.2 1.5 %collective-permute-start.6 = (bf16[256,512]{1,0:T(8,128)(2,1)S(1)}, bf16[256,512]{1,0:T(8,128)(2,1)S(1)}, u32[]{:S(2)}, u32[]{:S(2)}) collective-permute-start(bf16[256,512]{1,0:T(8,128)(2,1)S(1)} %attend.9.rest_4_), channel_id=1, source_target_pairs={{0,3},{1,2},{2,1},{3,0},{4,7},{5,6},{6,5},{7,4},{8,11},{9,10},{10,... | collective-permute-start | bytes 786440 | tf_op jit(solution)/shard_map/ppermute | solution.py:35
  45.7 0.1 add_add_fusion.info_ref
  45.8 0.0 copy-start.5
  45.8 0.5 collective-permute-start.9
  46.3 5.2 %attend.11._ = bf16[256,4096]{1,0:T(8,128)(2,1)} custom-call(s32[3]{0:T(128)S(1)} %add_add_fusion.info_ref, bf16[1024,1024]{1,0:T(8,128)(2,1)S(1)} %copy-done.1, bf16[1024,128]{1,0:T(8,128)(2,1)S(1)} %copy-done.2, bf16[1024,128]{1,0:T(8,128)(2,1)S(1)} %copy-done.3, bf16[768,128]{1,0:T(8,128)(2,1)S(1)} %collective-permute-done.first_ref, ...), custom_call_target="tpu_custom_call" | custom-call | flops 1409286144 | bytes 2097152 | tf_op jit(solution)/shard_map/attend/pallas_call | solution.py:188
  51.5 0.0 copy-done.5
  51.5 0.0 collective-permute-done.10.piece_ref
  51.5 0.0 copy-start.6
  51.5 0.8 copy-done.6
  52.3 2.5 %place.5._ = bf16[256,4096]{1,0:T(8,128)(2,1)} custom-call(s32[3]{0:T(128)} %copy-done.5, bf16[256,1024]{1,0:T(8,128)(2,1)} %copy-done.6, bf16[256,4096]{1,0:T(8,128)(2,1)} %attend.11._), custom_call_target="tpu_custom_call", output_to_operand_aliasing={{}: (2, {})} | custom-call | flops 262144 | bytes 1048576 | tf_op jit(solution)/shard_map/place/pallas_call | solution.py:222
  54.8 13.1 %collective-permute-done.9.piece_ref = bf16[256,256]{1,0:T(8,128)(2,1)S(1)} collective-permute-done((bf16[256,256]{1,0:T(8,128)(2,1)S(1)}, bf16[256,256]{1,0:T(8,128)(2,1)S(1)}, u32[]{:S(2)}, u32[]{:S(2)}) %collective-permute-start.9) | collective-permute-done | bytes 131104 | tf_op jit(solution)/shard_map/ppermute | solution.py:35
  67.9 0.0 copy-start.10
  67.9 0.6 copy-done.10
  68.6 2.2 %place.6._ = bf16[256,4096]{1,0:T(8,128)(2,1)} custom-call(s32[3]{0:T(128)} %copy-done.5, bf16[256,256]{1,0:T(8,128)(2,1)} %copy-done.10, bf16[256,4096]{1,0:T(8,128)(2,1)} %place.5._), custom_call_target="tpu_custom_call", output_to_operand_aliasing={{}: (2, {})} | custom-call | flops 65536 | bytes 262144 | tf_op jit(solution)/shard_map/place/pallas_call | solution.py:222
  70.8 0.0 collective-permute-done.8.piece_ref
  70.8 0.0 copy-start.7
  70.8 0.8 copy-done.7
  71.6 3.3 %place.7._ = bf16[256,4096]{1,0:T(8,128)(2,1)} custom-call(s32[3]{0:T(128)} %copy-done.5, bf16[256,768]{1,0:T(8,128)(2,1)} %copy-done.7, bf16[256,4096]{1,0:T(8,128)(2,1)} %place.6._), custom_call_target="tpu_custom_call", output_to_operand_aliasing={{}: (2, {})} | custom-call | flops 196608 | bytes 786432 | tf_op jit(solution)/shard_map/place/pallas_call | solution.py:222
  74.9 0.0 collective-permute-done.7.piece_ref
  74.9 0.0 copy-start.9
  74.9 0.7 copy-done.9
  75.6 2.3 %place.8._ = bf16[256,4096]{1,0:T(8,128)(2,1)} custom-call(s32[3]{0:T(128)} %copy-done.5, bf16[256,512]{1,0:T(8,128)(2,1)} %copy-done.9, bf16[256,4096]{1,0:T(8,128)(2,1)} %place.7._), custom_call_target="tpu_custom_call", output_to_operand_aliasing={{}: (2, {})} | custom-call | flops 131072 | bytes 524288 | tf_op jit(solution)/shard_map/place/pallas_call | solution.py:222
  77.9 0.0 collective-permute-done.6.piece_ref
  77.9 0.0 copy-start.8
  77.9 0.7 copy-done.8
  78.6 2.3 %place.9 = bf16[256,4096]{1,0:T(8,128)(2,1)} custom-call(s32[3]{0:T(128)} %copy-done.5, bf16[256,512]{1,0:T(8,128)(2,1)} %copy-done.8, bf16[256,4096]{1,0:T(8,128)(2,1)} %place.8._), custom_call_target="tpu_custom_call", output_to_operand_aliasing={{}: (2, {})} | custom-call | flops 131072 | bytes 524288 | tf_op jit(solution)/shard_map/place/pallas_call | solution.py:222
  (3 shorter events, 0.0 us)
Async XLA Ops:
  2.1 9.5 %collective-permute-start.3 = (bf16[16,128]{1,0:T(8,128)(2,1)}, bf16[16,128]{1,0:T(8,128)(2,1)S(1)}, u32[]{:S(2)}, u32[]{:S(2)}) collective-permute-start(bf16[16,128]{1,0:T(8,128)(2,1)} %get-tuple-element.12), channel_id=1, source_target_pairs={{0,4},{4,8},{8,12},{12,16},{16,20},{20,24},{24,28},{28,0},{1,5},{5... | collective-permute-start | bytes 12296 | tf_op jit(solution)/shard_map/ppermute | solution.py:30
  5.0 18.0 %collective-permute-start.2 = (bf16[64,128]{1,0:T(8,128)(2,1)}, bf16[64,128]{1,0:T(8,128)(2,1)S(1)}, u32[]{:S(2)}, u32[]{:S(2)}) collective-permute-start(bf16[64,128]{1,0:T(8,128)(2,1)} %get-tuple-element.11), channel_id=1, source_target_pairs={{0,12},{4,16},{8,20},{12,24},{16,28},{20,0},{24,4},{28,8},{1,13},{... | collective-permute-start | bytes 49160 | tf_op jit(solution)/shard_map/ppermute | solution.py:30
  7.6 15.4 %collective-permute-start.1 = (bf16[256,128]{1,0:T(8,128)(2,1)}, bf16[256,128]{1,0:T(8,128)(2,1)S(1)}, u32[]{:S(2)}, u32[]{:S(2)}) collective-permute-start(bf16[256,128]{1,0:T(8,128)(2,1)} %get-tuple-element.10.rest_2_), channel_id=1, source_target_pairs={{0,8},{4,12},{8,16},{12,20},{16,24},{20,28},{24,0},{28,4},{1,9},{5... | collective-permute-start | bytes 196616 | tf_op jit(solution)/shard_map/ppermute | solution.py:30
  9.2 13.9 %collective-permute-start = (bf16[768,128]{1,0:T(8,128)(2,1)}, bf16[768,128]{1,0:T(8,128)(2,1)S(1)}, u32[]{:S(2)}, u32[]{:S(2)}) collective-permute-start(bf16[768,128]{1,0:T(8,128)(2,1)} %get-tuple-element.9), channel_id=1, source_target_pairs={{0,4},{4,8},{8,12},{12,16},{16,20},{20,24},{24,28},{28,0},{1,5},{5... | collective-permute-start | bytes 589832 | tf_op jit(solution)/shard_map/ppermute | solution.py:30
  12.2 5.4 %collective-permute-start.4 = (bf16[32,128]{1,0:T(8,128)(2,1)S(1)}, bf16[32,128]{1,0:T(8,128)(2,1)S(1)}, u32[]{:S(2)}, u32[]{:S(2)}) collective-permute-start(bf16[32,128]{1,0:T(8,128)(2,1)S(1)} %pad_maximum_fusion.1), channel_id=1, source_target_pairs={{0,8},{4,12},{8,16},{12,20},{16,24},{20,28},{24,0},{28,4},{1,9},{5... | collective-permute-start | bytes 24584 | tf_op jit(solution)/shard_map/ppermute | solution.py:30
  18.4 4.6 %collective-permute-start.5 = (bf16[64,128]{1,0:T(8,128)(2,1)S(1)}, bf16[64,128]{1,0:T(8,128)(2,1)S(1)}, u32[]{:S(2)}, u32[]{:S(2)}) collective-permute-start(bf16[64,128]{1,0:T(8,128)(2,1)S(1)} %pad_maximum_fusion), channel_id=1, source_target_pairs={{0,16},{4,20},{8,24},{12,28},{16,0},{20,4},{24,8},{28,12},{1,17},{... | collective-permute-start | bytes 49160 | tf_op jit(solution)/shard_map/ppermute | solution.py:30
  23.0 1.6 %copy-start = (bf16[1024,1024]{1,0:T(8,128)(2,1)S(1)}, bf16[1024,1024]{1,0:T(8,128)(2,1)}, u32[]{:S(2)}) copy-start(bf16[1024,1024]{1,0:T(8,128)(2,1)} %q_ref.11) | copy-start | bytes 6291460
  24.6 0.9 %copy-start.2 = (bf16[1024,128]{1,0:T(8,128)(2,1)S(1)}, bf16[1024,128]{1,0:T(8,128)(2,1)}, u32[]{:S(2)}) copy-start(bf16[1024,128]{1,0:T(8,128)(2,1)} %keys_ref.13) | copy-start | bytes 786436
  25.6 0.9 %copy-start.3 = (bf16[1024,128]{1,0:T(8,128)(2,1)S(1)}, bf16[1024,128]{1,0:T(8,128)(2,1)}, u32[]{:S(2)}) copy-start(bf16[1024,128]{1,0:T(8,128)(2,1)} %values_ref.13) | copy-start | bytes 786436
  26.5 0.8 %copy-start.4 = (bf16[256,128]{1,0:T(8,128)(2,1)S(1)}, bf16[256,128]{1,0:T(8,128)(2,1)}, u32[]{:S(2)}) copy-start(bf16[256,128]{1,0:T(8,128)(2,1)} %get-tuple-element.10.rest_2_) | copy-start | bytes 196612
  28.9 3.6 %copy-start.1 = (bf16[1024,1024]{1,0:T(8,128)(2,1)S(1)}, bf16[1024,1024]{1,0:T(8,128)(2,1)}, u32[]{:S(2)}) copy-start(bf16[1024,1024]{1,0:T(8,128)(2,1)} %q_ref.11) | copy-start | bytes 6291460
  42.3 9.2 %collective-permute-start.10 = (bf16[256,1024]{1,0:T(8,128)(2,1)S(1)}, bf16[256,1024]{1,0:T(8,128)(2,1)S(1)}, u32[]{:S(2)}, u32[]{:S(2)}) collective-permute-start(bf16[256,1024]{1,0:T(8,128)(2,1)S(1)} %attend.10.rest_4_), channel_id=1, source_target_pairs={{0,1},{1,0},{2,3},{3,2},{4,5},{5,4},{6,7},{7,6},{8,9},{9,8},{10,11... | collective-permute-start | bytes 1572872 | tf_op jit(solution)/shard_map/ppermute | solution.py:35
  42.4 28.4 %collective-permute-start.8 = (bf16[256,768]{1,0:T(8,128)(2,1)S(1)}, bf16[256,768]{1,0:T(8,128)(2,1)S(1)}, u32[]{:S(2)}, u32[]{:S(2)}) collective-permute-start(bf16[256,768]{1,0:T(8,128)(2,1)S(1)} %attend.7.rest_4_), channel_id=1, source_target_pairs={{0,2},{1,3},{2,0},{3,1},{4,6},{5,7},{6,4},{7,5},{8,10},{9,11},{10,... | collective-permute-start | bytes 1179656 | tf_op jit(solution)/shard_map/ppermute | solution.py:35
  44.0 30.9 %collective-permute-start.7 = (bf16[256,512]{1,0:T(8,128)(2,1)S(1)}, bf16[256,512]{1,0:T(8,128)(2,1)S(1)}, u32[]{:S(2)}, u32[]{:S(2)}) collective-permute-start(bf16[256,512]{1,0:T(8,128)(2,1)S(1)} %attend.8.rest_4_), channel_id=1, source_target_pairs={{0,3},{1,2},{2,1},{3,0},{4,7},{5,6},{6,5},{7,4},{8,11},{9,10},{10,... | collective-permute-start | bytes 786440 | tf_op jit(solution)/shard_map/ppermute | solution.py:35
  44.2 33.7 %collective-permute-start.6 = (bf16[256,512]{1,0:T(8,128)(2,1)S(1)}, bf16[256,512]{1,0:T(8,128)(2,1)S(1)}, u32[]{:S(2)}, u32[]{:S(2)}) collective-permute-start(bf16[256,512]{1,0:T(8,128)(2,1)S(1)} %attend.9.rest_4_), channel_id=1, source_target_pairs={{0,3},{1,2},{2,1},{3,0},{4,7},{5,6},{6,5},{7,4},{8,11},{9,10},{10,... | collective-permute-start | bytes 786440 | tf_op jit(solution)/shard_map/ppermute | solution.py:35
  45.8 5.7 %copy-start.5 = (s32[3]{0:T(128)}, s32[3]{0:T(128)S(1)}, u32[]{:S(2)}) copy-start(s32[3]{0:T(128)S(1)} %add_add_fusion.info_ref) | copy-start | bytes 40
  45.8 22.1 %collective-permute-start.9 = (bf16[256,256]{1,0:T(8,128)(2,1)S(1)}, bf16[256,256]{1,0:T(8,128)(2,1)S(1)}, u32[]{:S(2)}, u32[]{:S(2)}) collective-permute-start(bf16[256,256]{1,0:T(8,128)(2,1)S(1)} %attend.6.rest_4_), channel_id=1, source_target_pairs={{0,2},{1,3},{2,0},{3,1},{4,6},{5,7},{6,4},{7,5},{8,10},{9,11},{10,... | collective-permute-start | bytes 393224 | tf_op jit(solution)/shard_map/ppermute | solution.py:35
  51.5 0.8 copy-start.6
  67.9 0.6 copy-start.10
  70.8 0.8 copy-start.7
  74.9 0.7 copy-start.9
  77.9 0.7 copy-start.8

commit v2 on v1

--- a/solution.py
+++ b/solution.py
@@ -7,6 +7,7 @@
 from jax.experimental import pallas as pl
 from jax.experimental.pallas import tpu as pltpu
 from jax.sharding import PartitionSpec as P
+
 
 HEAD_DIM = 128
 BLK = 256
@@ -16,6 +17,7 @@
 PER_GROUP = BLK // GROUP
 LANES = 128
 NEG = -1e30
+VMEM_LIMIT = 16 * 1024 * 1024
 EXP_SCALE = math.log2(math.e) / math.sqrt(HEAD_DIM)
 BF16 = jnp.bfloat16
 F32 = jnp.float32
@@ -30,13 +32,33 @@
     return lax.ppermute(array, axis, [(i, (i + by) % size) for i in range(size)])
 
 
+def off_chip(*arrays):
+    return [pltpu.with_memory_space_constraint(a, pltpu.HBM) for a in arrays]
+
+
 def exchange(array, axis, flip):
     size = lax.axis_size(axis)
     return lax.ppermute(array, axis, [(i, i ^ flip) for i in range(size)])
 
 
-def pool_kernel(block_count, last_blocks, slot, keys_ref, values_ref, mid_ref, coarse_ref,
-                coarse_out, mids_out, last_out, first_out):
+def pool_kernel(block_count, last_blocks, slot, keys_hbm, values_hbm, mid_hbm, coarse_hbm,
+                keys_ref, values_ref, coarse_out, mids_out, last_out, first_out,
+                mid_ref, coarse_ref, arrived):
+    copies = [
+        pltpu.make_async_copy(source, target, arrived.at[i])
+        for i, (source, target) in enumerate(
+            (
+                (mid_hbm, mid_ref),
+                (coarse_hbm, coarse_ref),
+                (keys_hbm, keys_ref),
+                (values_hbm, values_ref),
+            )
+        )
+    ]
+    for copy in copies:
+        copy.start()
+    for copy in copies:
+        copy.wait()
     rows = block_count * PER_GROUP
     repeat = (
         lax.broadcasted_iota(jnp.int32, (GROUP, BLK), 1) % GROUP
@@ -74,6 +96,8 @@
 def pool(keys, values, mid_pool, coarse_pool, block_count, last_blocks, slot):
     rows = block_count * PER_GROUP
     shapes = (
+        keys.shape,
+        values.shape,
         (2 * slot, HEAD_DIM),
         (2 * rows, HEAD_DIM),
         (2 * last_blocks * PER_GROUP, HEAD_DIM),
@@ -81,16 +105,67 @@
     )
     return pl.pallas_call(
         functools.partial(pool_kernel, block_count, last_blocks, slot),
+        in_specs=[pl.BlockSpec(memory_space=pltpu.HBM)] * 4,
+        out_specs=[pl.BlockSpec(memory_space=pltpu.VMEM) for _ in shapes],
         out_shape=[jax.ShapeDtypeStruct(shape, BF16) for shape in shapes],
+        scratch_shapes=[
+            pltpu.VMEM(mid_pool.shape, BF16),
+            pltpu.VMEM(coarse_pool.shape, BF16),
+            pltpu.SemaphoreType.DMA((4,)),
+        ],
         cost_estimate=pl.CostEstimate(
             flops=4 * keys.size * (PER_GROUP + slot), bytes_accessed=6 * keys.size, transcendentals=0
         ),
+        compiler_params=pltpu.CompilerParams(vmem_limit_bytes=VMEM_LIMIT),
         name="pool",
-    )(keys, values, mid_pool, coarse_pool)
+    )(*off_chip(keys, values, mid_pool, coarse_pool))
+
+
+def join_kernel(one_ref, two_ref, out_ref):
+    size = one_ref.shape[0]
+    out_ref[:size, :] = one_ref[...]
+    out_ref[size:, :] = two_ref[...]
+
+
+def join(one, two):
+    return pl.pallas_call(
+        join_kernel,
+        out_shape=jax.ShapeDtypeStruct((one.shape[0] + two.shape[0], one.shape[1]), one.dtype),
+        compiler_params=pltpu.CompilerParams(vmem_limit_bytes=VMEM_LIMIT),
+        name="join",
+    )(one, two)
+
+
+def load_kernel(*refs):
+    count = len(refs) // 2
+    copies = [
+        pltpu.make_async_copy(refs[i], refs[count + i], refs[-1].at[i]) for i in range(count)
+    ]
+    for copy in copies:
+        copy.start()
+    for copy in copies:
+        copy.wait()
+
+
+def load(*arrays):
+    return pl.pallas_call(
+        load_kernel,
+        in_specs=[pl.BlockSpec(memory_space=pltpu.HBM) for _ in arrays],
+        out_specs=[pl.BlockSpec(memory_space=pltpu.VMEM) for _ in arrays],
+        out_shape=[jax.ShapeDtypeStruct(a.shape, a.dtype) for a in arrays],
+        scratch_shapes=[pltpu.SemaphoreType.DMA((len(arrays),))],
+        compiler_params=pltpu.CompilerParams(vmem_limit_bytes=VMEM_LIMIT),
+        cost_estimate=pl.CostEstimate(
+            flops=2 * sum(a.size for a in arrays),
+            bytes_accessed=4 * sum(a.size for a in arrays),
+            transcendentals=0,
+        ),
+        name="load",
+    )(*off_chip(*arrays))
 
 
 def attend_kernel(geometry, info_ref, q_ref, keys_ref, values_ref, first_ref, *rest):
-    block_count, hops, last_blocks, slot, reach, width, step_heads = geometry
+    block_count, hops, _, slot, reach, width, step_heads = geometry
     further = rest[: hops - 1]
     mids_ref, coarse_ref, _, out_ref, mid_scratch, all_keys, all_values, bias = rest[hops - 1 :]
     rows = block_count * PER_GROUP
@@ -173,7 +248,7 @@
 
 
 def attend(info, queries, shared, after, head_start, heads, geometry, full_columns=None):
-    block_count, hops, last_blocks, slot, reach, width, step_heads = geometry
+    block_count, hops, _, _, _, width, step_heads = geometry
     step = step_heads * HEAD_DIM
     first = head_start // step_heads
     total = MIDS + width + 2 * BLK
@@ -202,7 +277,7 @@
             ],
         ),
         out_shape=jax.ShapeDtypeStruct((BLK, out_columns), BF16),
-        compiler_params=pltpu.CompilerParams(vmem_limit_bytes=32 * 1024 * 1024),
+        compiler_params=pltpu.CompilerParams(vmem_limit_bytes=VMEM_LIMIT),
         cost_estimate=pl.CostEstimate(
             flops=6 * BLK * heads * total * HEAD_DIM,
             bytes_accessed=4 * BLK * heads * HEAD_DIM + 1024 * 1024,
@@ -212,28 +287,28 @@
     )(info, queries, *shared, after)
 
 
-def place_kernel(info_ref, piece_ref, _, out_ref):
-    out_ref[...] = piece_ref[...]
+def place_kernel(flip, at, columns, info_ref, piece_ref, _, out_ref, done):
+    start = pl.multiple_of((info_ref[2] ^ flip) * columns + at, HEAD_DIM)
+    copy = pltpu.make_async_copy(
+        piece_ref, out_ref.at[:, pl.ds(start, piece_ref.shape[1])], done
+    )
+    copy.start()
+    copy.wait()
 
 
 def place(info, output, piece, at, flip, columns):
-    step = math.gcd(piece.shape[1], at) if at else piece.shape[1]
-    per_device = columns // step
-    return pl.pallas_call(
-        place_kernel,
-        grid_spec=pltpu.PrefetchScalarGridSpec(
-            num_scalar_prefetch=1,
-            grid=(piece.shape[1] // step,),
-            in_specs=[
-                pl.BlockSpec((BLK, step), lambda i, info: (0, i)),
-                pl.BlockSpec(memory_space=pl.ANY),
-            ],
-            out_specs=pl.BlockSpec(
-                (BLK, step), lambda i, info: (0, (info[2] ^ flip) * per_device + at // step + i)
-            ),
-        ),
+    return pl.pallas_call(
+        functools.partial(place_kernel, flip, at, columns),
+        in_specs=[
+            pl.BlockSpec(memory_space=pltpu.SMEM),
+            pl.BlockSpec(memory_space=pltpu.VMEM),
+            pl.BlockSpec(memory_space=pl.ANY),
+        ],
+        out_specs=pl.BlockSpec(memory_space=pl.ANY),
+        scratch_shapes=[pltpu.SemaphoreType.DMA(())],
         out_shape=jax.ShapeDtypeStruct(output.shape, output.dtype),
         input_output_aliases={2: 0},
+        compiler_params=pltpu.CompilerParams(vmem_limit_bytes=VMEM_LIMIT),
         cost_estimate=pl.CostEstimate(
             flops=piece.size, bytes_accessed=4 * piece.size, transcendentals=0
         ),
@@ -255,15 +330,19 @@
     last_blocks = MIDB + 1 - (hops - 1) * block_count
     slot = round_up(block_count, 8)
 
-    coarse, mids, last, first = pool(
+    keys, values, coarse, mids, last, first = pool(
         keys, values, mid_pool, coarse_pool, block_count, last_blocks, slot
     )
-    near = cyclic(first, "seq", 1)
-    further = [cyclic(mids, "seq", by) for by in range(2, hops)] + [cyclic(last, "seq", hops)]
-    reach = 1
+    reach, step = 1, 0
     while reach < length:
-        coarse = jnp.concatenate([coarse, cyclic(coarse, "seq", reach)])
-        reach *= 2
+        arriving = cyclic(coarse, "seq", reach)
+        if step == 0:
+            near = cyclic(first, "seq", 1)
+            (queries,) = load(queries)
+        coarse = join(coarse, arriving)
+        reach, step = 2 * reach, step + 1
+    further = [cyclic(mids, "seq", by) for by in range(2, hops)]
+    further += [cyclic(last, "seq", hops)]
     width = round_up(reach * slot, LANES)
     geometry = (block_count, hops, last_blocks, slot, reach, width, 2)
     shared = (keys, values, near, *further, mids, coarse)
@@ -271,23 +350,26 @@
     def info(flip):
         return jnp.stack([member ^ flip, device, member]).astype(jnp.int32)
 
-    plan = []
-    for flip in range(members // 2, members):
-        half = heads_here // 2 if flip > members // 2 else heads_here // 4
-        plan += [(flip, 0, half), (flip, half, heads_here - half)]
-    plan += [(flip, 0, heads_here) for flip in range(1, members // 2)]
     after = coarse
     arrived = []
-    for flip, start, heads in plan:
+    for flip, start, heads in send_plan(members, heads_here):
         after = attend(info(flip), queries, shared, after, start, heads, geometry)
         arrived.append((flip, start, exchange(after, "head", flip)))
     output = attend(
-        info(0), queries, shared, after, 0, heads_here, geometry, full_columns=members * columns
+        info(0), queries, shared, after, 0, heads_here, geometry, members * columns
     )
     order = [p for p in arrived if p[0] < members // 2] + [p for p in arrived if p[0] >= members // 2]
     for flip, start, piece in order:
         output = place(info(0), output, piece, start * HEAD_DIM, flip, columns)
     return output
+
+
+def send_plan(members, heads):
+    plan = []
+    for flip in range(members // 2, members):
+        half = heads // 2 if flip > members // 2 else heads // 4
+        plan += [(flip, 0, half), (flip, half, heads - half)]
+    return plan + [(flip, 0, heads) for flip in range(1, members // 2)]
 
 
 def solution(mesh):

time: 81.5 us -> 66.1 us (0.81)
  local copies, waits for them, and re-layouts: 8.63 us -> 0 us
  Pallas kernels: 34.8 us -> 29.5 us
  other arithmetic: 1.66 us -> 0.31 us
    unnamed x25 -> x0, local copies, waits for them, and re-layouts: 8.63 us -> none
    pallas_call x5 -> x9, Pallas kernels: 12.7 us -> 7.99 us  [the longest x5 6.38 us: place(): pl.pallas_call(functools.partial(place_kernel, flip, at, columns), in_spe...]
    ppermute x5, waiting for transfers between devices: 13.1 us -> 15.1 us  [exchange(): return lax.ppermute(array, axis, [(i, i ^ flip) for i in range(size)])]
    ppermute x6, waiting for transfers between devices: 10.1 us -> 8.32 us  [cyclic(): lax.ppermute(array, axis, [(i, (i + by) % size) for i in range(size)])]
    concatenate x2 -> x0, other arithmetic: 1.36 us -> none  [body(): coarse = jnp.concatenate([coarse, cyclic(coarse, 'seq', reach)])]
  transfers between devices with their start and end apart: 11 -> 11, of which waited for: 3 -> 3; matrix products, arithmetic and copies ran while one was open for 3% -> 0% of each run, Pallas kernels for 19% -> 18%
where the time goes in v2:
time: 66.1 us; the launch traced here: 65.9 us
  Pallas kernels  29.5 us (45%)
  waiting for transfers between devices  23.4 us (35%)
  starting transfers between devices  12.6 us (19%)
    pallas_call x6, Pallas kernels, attend(): pl.pallas_call(functools.partial(attend_kernel, geometry), grid_spec=pltp...  20.1 us
    ppermute x5, waiting for transfers between devices, exchange(): return lax.ppermute(array, axis, [(i, i ^ flip) for i in range(size)])  15.1 us
    ppermute x6, starting transfers between devices, cyclic(): lax.ppermute(array, axis, [(i, (i + by) % size) for i in range(size)])  8.68 us
    ppermute x6, waiting for transfers between devices, cyclic(): lax.ppermute(array, axis, [(i, (i + by) % size) for i in range(size)])  8.32 us
    pallas_call x5, Pallas kernels, place(): pl.pallas_call(functools.partial(place_kernel, flip, at, columns), in_spe...  6.38 us
    ppermute x5, starting transfers between devices, exchange(): return lax.ppermute(array, axis, [(i, i ^ flip) for i in range(size)])  3.91 us
    pallas_call x1, Pallas kernels, load(): pl.pallas_call(load_kernel, in_specs=[pl.BlockSpec(memory_space=pltpu.HBM...  1.6 us
    pallas_call x1, Pallas kernels, pool(): pl.pallas_call(functools.partial(pool_kernel, block_count, last_blocks, s...  1.42 us
  transfers between devices with their start and end apart: 11, of which 3 were waited for; matrix products, arithmetic and copies ran while one was open for 0% of the time, Pallas kernels for 18%

profile of v2, /device:TPU:0, one launch (start us, length us, event | category | flops | bytes accessed | tf_op | source)
XLA Modules:
  0.0 65.9 jit_solution(9400655608534501696)
XLA Ops:
  0.0 1.4 %pool.1 = (bf16[1024,128]{1,0:T(8,128)(2,1)S(1)}, bf16[1024,128]{1,0:T(8,128)(2,1)S(1)}, bf16[16,128]{1,0:T(8,128)(2,1)S(1)}, bf16[256,128]{1,0:T(8,128)(2,1)S(1...) custom-call(bf16[1024,128]{1,0:T(8,128)(2,1)} %keys_hbm.1, bf16[1024,128]{1,0:T(8,128)(2,1)} %values_hbm.1, ...), custom_call_target="tpu_custom_call" | custom-call | flops 20971520 | bytes 786432 | tf_op jit(solution)/shard_map/pool/pallas_call | solution.py:106
  1.4 3.0 %collective-permute-start.3 = (bf16[16,128]{1,0:T(8,128)(2,1)S(1)}, bf16[16,128]{1,0:T(8,128)(2,1)S(1)}, u32[]{:S(2)}, u32[]{:S(2)}) collective-permute-start(bf16[16,128]{1,0:T(8,128)(2,1)S(1)} %get-tuple-element.16.one_ref), channel_id=1, source_target_pairs={{0,4},{4,8},{8,12},{12,16},{16,20},{20,24},{24,28},{28,0},{1,5},{5... | collective-permute-start | bytes 12296 | tf_op jit(solution)/shard_map/ppermute | solution.py:32
  4.5 2.6 %collective-permute-start.2 = (bf16[64,128]{1,0:T(8,128)(2,1)S(1)}, bf16[64,128]{1,0:T(8,128)(2,1)S(1)}, u32[]{:S(2)}, u32[]{:S(2)}) collective-permute-start(bf16[64,128]{1,0:T(8,128)(2,1)S(1)} %get-tuple-element.15), channel_id=1, source_target_pairs={{0,12},{4,16},{8,20},{12,24},{16,28},{20,0},{24,4},{28,8},{1,13},{... | collective-permute-start | bytes 49160 | tf_op jit(solution)/shard_map/ppermute | solution.py:32
  7.0 1.6 %collective-permute-start.1 = (bf16[256,128]{1,0:T(8,128)(2,1)S(1)}, bf16[256,128]{1,0:T(8,128)(2,1)S(1)}, u32[]{:S(2)}, u32[]{:S(2)}) collective-permute-start(bf16[256,128]{1,0:T(8,128)(2,1)S(1)} %get-tuple-element.14.rest_2_), channel_id=1, source_target_pairs={{0,8},{4,12},{8,16},{12,20},{16,24},{20,28},{24,0},{28,4},{1,9},{5... | collective-permute-start | bytes 196616 | tf_op jit(solution)/shard_map/ppermute | solution.py:32
  8.6 1.5 %collective-permute-start = (bf16[768,128]{1,0:T(8,128)(2,1)S(1)}, bf16[768,128]{1,0:T(8,128)(2,1)S(1)}, u32[]{:S(2)}, u32[]{:S(2)}) collective-permute-start(bf16[768,128]{1,0:T(8,128)(2,1)S(1)} %get-tuple-element.13), channel_id=1, source_target_pairs={{0,4},{4,8},{8,12},{12,16},{16,20},{20,24},{24,28},{28,0},{1,5},{5... | collective-permute-start | bytes 589832 | tf_op jit(solution)/shard_map/ppermute | solution.py:32
  10.1 0.1 add_add_fusion.2.info_ref
  10.2 0.0 collective-permute-done.3.two_ref
  10.2 0.0 collective-permute-start.4
  10.2 0.1 add_add_fusion.1.info_ref
  10.3 5.4 %collective-permute-done.4.two_ref = bf16[32,128]{1,0:T(8,128)(2,1)S(1)} collective-permute-done((bf16[32,128]{1,0:T(8,128)(2,1)S(1)}, bf16[32,128]{1,0:T(8,128)(2,1)S(1)}, u32[]{:S(2)}, u32[]{:S(2)}) %collective-permute-start.4) | collective-permute-done | bytes 8224 | tf_op jit(solution)/shard_map/ppermute | solution.py:32
  15.6 0.0 collective-permute-start.5
  15.6 0.1 add_add_fusion.3.info_ref
  15.7 1.6 %load.1.q_ref = bf16[1024,1024]{1,0:T(8,128)(2,1)S(1)} custom-call(bf16[1024,1024]{1,0:T(8,128)(2,1)} %refs_0_.1), custom_call_target="tpu_custom_call" | custom-call | flops 2097152 | bytes 4194304 | tf_op jit(solution)/shard_map/load/pallas_call | solution.py:151
  17.3 3.0 %collective-permute-done.5.two_ref = bf16[64,128]{1,0:T(8,128)(2,1)S(1)} collective-permute-done((bf16[64,128]{1,0:T(8,128)(2,1)S(1)}, bf16[64,128]{1,0:T(8,128)(2,1)S(1)}, u32[]{:S(2)}, u32[]{:S(2)}) %collective-permute-start.5) | collective-permute-done | bytes 16416 | tf_op jit(solution)/shard_map/ppermute | solution.py:32
  20.3 0.0 collective-permute-done.2.rest_1_
  20.3 0.0 collective-permute-done.1.rest_0_
  20.3 0.0 collective-permute-done.first_ref
  20.3 1.6 %attend.6.rest_4_ = bf16[256,256]{1,0:T(8,128)(2,1)S(1)} custom-call(s32[3]{0:T(128)S(1)} %add_add_fusion.2.info_ref, bf16[1024,1024]{1,0:T(8,128)(2,1)S(1)} %load.1.q_ref, bf16[1024,128]{1,0:T(8,128)(2,1)S(1)} %get-tuple-element.11.keys_ref, bf16[1024,128]{1,0:T(8,128)(2,1)S(1)} %get-tuple-element.12.values_ref, ...), custom_call_target="tpu_custom_call" | custom-call | flops 352321536 | bytes 1310720 | tf_op jit(solution)/shard_map/attend/pallas_call | solution.py:263
  21.9 3.6 %attend.7.rest_4_ = bf16[256,768]{1,0:T(8,128)(2,1)S(1)} custom-call(s32[3]{0:T(128)S(1)} %add_add_fusion.2.info_ref, bf16[1024,1024]{1,0:T(8,128)(2,1)S(1)} %load.1.q_ref, bf16[1024,128]{1,0:T(8,128)(2,1)S(1)} %get-tuple-element.11.keys_ref, bf16[1024,128]{1,0:T(8,128)(2,1)S(1)} %get-tuple-element.12.values_ref, ...), custom_call_target="tpu_custom_call" | custom-call | flops 1056964608 | bytes 1835008 | tf_op jit(solution)/shard_map/attend/pallas_call | solution.py:263
  25.4 2.6 %attend.8.rest_4_ = bf16[256,512]{1,0:T(8,128)(2,1)S(1)} custom-call(s32[3]{0:T(128)S(1)} %add_add_fusion.1.info_ref, bf16[1024,1024]{1,0:T(8,128)(2,1)S(1)} %load.1.q_ref, bf16[1024,128]{1,0:T(8,128)(2,1)S(1)} %get-tuple-element.11.keys_ref, bf16[1024,128]{1,0:T(8,128)(2,1)S(1)} %get-tuple-element.12.values_ref, ...), custom_call_target="tpu_custom_call" | custom-call | flops 704643072 | bytes 1572864 | tf_op jit(solution)/shard_map/attend/pallas_call | solution.py:263
  28.0 2.6 %attend.9.rest_4_ = bf16[256,512]{1,0:T(8,128)(2,1)S(1)} custom-call(s32[3]{0:T(128)S(1)} %add_add_fusion.1.info_ref, bf16[1024,1024]{1,0:T(8,128)(2,1)S(1)} %load.1.q_ref, bf16[1024,128]{1,0:T(8,128)(2,1)S(1)} %get-tuple-element.11.keys_ref, bf16[1024,128]{1,0:T(8,128)(2,1)S(1)} %get-tuple-element.12.values_ref, ...), custom_call_target="tpu_custom_call" | custom-call | flops 704643072 | bytes 1572864 | tf_op jit(solution)/shard_map/attend/pallas_call | solution.py:263
  30.7 4.5 %attend.10.rest_4_ = bf16[256,1024]{1,0:T(8,128)(2,1)S(1)} custom-call(s32[3]{0:T(128)S(1)} %add_add_fusion.3.info_ref, bf16[1024,1024]{1,0:T(8,128)(2,1)S(1)} %load.1.q_ref, bf16[1024,128]{1,0:T(8,128)(2,1)S(1)} %get-tuple-element.11.keys_ref, bf16[1024,128]{1,0:T(8,128)(2,1)S(1)} %get-tuple-element.12.values_ref, ...), custom_call_target="tpu_custom_call" | custom-call | flops 1409286144 | bytes 2097152 | tf_op jit(solution)/shard_map/attend/pallas_call | solution.py:263
  35.2 0.1 collective-permute-start.10
  35.3 1.7 %collective-permute-start.8 = (bf16[256,768]{1,0:T(8,128)(2,1)S(1)}, bf16[256,768]{1,0:T(8,128)(2,1)S(1)}, u32[]{:S(2)}, u32[]{:S(2)}) collective-permute-start(bf16[256,768]{1,0:T(8,128)(2,1)S(1)} %attend.7.rest_4_), channel_id=1, source_target_pairs={{0,2},{1,3},{2,0},{3,1},{4,6},{5,7},{6,4},{7,5},{8,10},{9,11},{10,... | collective-permute-start | bytes 1179656 | tf_op jit(solution)/shard_map/ppermute | solution.py:41
  36.9 0.2 collective-permute-start.7
  37.1 1.5 %collective-permute-start.6 = (bf16[256,512]{1,0:T(8,128)(2,1)S(1)}, bf16[256,512]{1,0:T(8,128)(2,1)S(1)}, u32[]{:S(2)}, u32[]{:S(2)}) collective-permute-start(bf16[256,512]{1,0:T(8,128)(2,1)S(1)} %attend.9.rest_4_), channel_id=1, source_target_pairs={{0,3},{1,2},{2,1},{3,0},{4,7},{5,6},{6,5},{7,4},{8,11},{9,10},{10,... | collective-permute-start | bytes 786440 | tf_op jit(solution)/shard_map/ppermute | solution.py:41
  38.7 0.1 add_add_fusion.info_ref
  38.8 0.4 collective-permute-start.9
  39.2 5.2 %attend.11._ = bf16[256,4096]{1,0:T(8,128)(2,1)} custom-call(s32[3]{0:T(128)S(1)} %add_add_fusion.info_ref, bf16[1024,1024]{1,0:T(8,128)(2,1)S(1)} %load.1.q_ref, bf16[1024,128]{1,0:T(8,128)(2,1)S(1)} %get-tuple-element.11.keys_ref, bf16[1024,128]{1,0:T(8,128)(2,1)S(1)} %get-tuple-element.12.values_ref, bf16[768,128]{1,0:T(8,128)(2,1)S(1)} %collective-permute-done.first_ref, ...), custom_call_target="tpu_custom_call" | custom-call | flops 1409286144 | bytes 2097152 | tf_op jit(solution)/shard_map/attend/pallas_call | solution.py:263
  44.4 0.0 collective-permute-done.10.piece_ref
  44.4 1.3 %place.5._ = bf16[256,4096]{1,0:T(8,128)(2,1)} custom-call(s32[3]{0:T(128)S(1)} %add_add_fusion.info_ref, bf16[256,1024]{1,0:T(8,128)(2,1)S(1)} %collective-permute-done.10.piece_ref, bf16[256,4096]{1,0:T(8,128)(2,1)} %attend.11._), custom_call_target="tpu_custom_call", output_to_operand_aliasing={{}: (2, {})} | custom-call | flops 262144 | bytes 1048576 | tf_op jit(solution)/shard_map/place/pallas_call | solution.py:300
  45.7 15.1 %collective-permute-done.9.piece_ref = bf16[256,256]{1,0:T(8,128)(2,1)S(1)} collective-permute-done((bf16[256,256]{1,0:T(8,128)(2,1)S(1)}, bf16[256,256]{1,0:T(8,128)(2,1)S(1)}, u32[]{:S(2)}, u32[]{:S(2)}) %collective-permute-start.9) | collective-permute-done | bytes 131104 | tf_op jit(solution)/shard_map/ppermute | solution.py:41
  60.8 1.2 %place.6._ = bf16[256,4096]{1,0:T(8,128)(2,1)} custom-call(s32[3]{0:T(128)S(1)} %add_add_fusion.info_ref, bf16[256,256]{1,0:T(8,128)(2,1)S(1)} %collective-permute-done.9.piece_ref, bf16[256,4096]{1,0:T(8,128)(2,1)} %place.5._), custom_call_target="tpu_custom_call", output_to_operand_aliasing={{}: (2, {})} | custom-call | flops 65536 | bytes 262144 | tf_op jit(solution)/shard_map/place/pallas_call | solution.py:300
  62.1 0.0 collective-permute-done.8.piece_ref
  62.1 1.3 %place.7._ = bf16[256,4096]{1,0:T(8,128)(2,1)} custom-call(s32[3]{0:T(128)S(1)} %add_add_fusion.info_ref, bf16[256,768]{1,0:T(8,128)(2,1)S(1)} %collective-permute-done.8.piece_ref, bf16[256,4096]{1,0:T(8,128)(2,1)} %place.6._), custom_call_target="tpu_custom_call", output_to_operand_aliasing={{}: (2, {})} | custom-call | flops 196608 | bytes 786432 | tf_op jit(solution)/shard_map/place/pallas_call | solution.py:300
  63.4 0.0 collective-permute-done.7.piece_ref
  63.4 1.3 %place.8._ = bf16[256,4096]{1,0:T(8,128)(2,1)} custom-call(s32[3]{0:T(128)S(1)} %add_add_fusion.info_ref, bf16[256,512]{1,0:T(8,128)(2,1)S(1)} %collective-permute-done.7.piece_ref, bf16[256,4096]{1,0:T(8,128)(2,1)} %place.7._), custom_call_target="tpu_custom_call", output_to_operand_aliasing={{}: (2, {})} | custom-call | flops 131072 | bytes 524288 | tf_op jit(solution)/shard_map/place/pallas_call | solution.py:300
  64.7 0.0 collective-permute-done.6.piece_ref
  64.7 1.3 %place.9 = bf16[256,4096]{1,0:T(8,128)(2,1)} custom-call(s32[3]{0:T(128)S(1)} %add_add_fusion.info_ref, bf16[256,512]{1,0:T(8,128)(2,1)S(1)} %collective-permute-done.6.piece_ref, bf16[256,4096]{1,0:T(8,128)(2,1)} %place.8._), custom_call_target="tpu_custom_call", output_to_operand_aliasing={{}: (2, {})} | custom-call | flops 131072 | bytes 524288 | tf_op jit(solution)/shard_map/place/pallas_call | solution.py:300
  (3 shorter events, 0.0 us)
Async XLA Ops:
  1.4 8.7 %collective-permute-start.3 = (bf16[16,128]{1,0:T(8,128)(2,1)S(1)}, bf16[16,128]{1,0:T(8,128)(2,1)S(1)}, u32[]{:S(2)}, u32[]{:S(2)}) collective-permute-start(bf16[16,128]{1,0:T(8,128)(2,1)S(1)} %get-tuple-element.16.one_ref), channel_id=1, source_target_pairs={{0,4},{4,8},{8,12},{12,16},{16,20},{20,24},{24,28},{28,0},{1,5},{5... | collective-permute-start | bytes 12296 | tf_op jit(solution)/shard_map/ppermute | solution.py:32
  4.5 15.8 %collective-permute-start.2 = (bf16[64,128]{1,0:T(8,128)(2,1)S(1)}, bf16[64,128]{1,0:T(8,128)(2,1)S(1)}, u32[]{:S(2)}, u32[]{:S(2)}) collective-permute-start(bf16[64,128]{1,0:T(8,128)(2,1)S(1)} %get-tuple-element.15), channel_id=1, source_target_pairs={{0,12},{4,16},{8,20},{12,24},{16,28},{20,0},{24,4},{28,8},{1,13},{... | collective-permute-start | bytes 49160 | tf_op jit(solution)/shard_map/ppermute | solution.py:32
  7.0 13.3 %collective-permute-start.1 = (bf16[256,128]{1,0:T(8,128)(2,1)S(1)}, bf16[256,128]{1,0:T(8,128)(2,1)S(1)}, u32[]{:S(2)}, u32[]{:S(2)}) collective-permute-start(bf16[256,128]{1,0:T(8,128)(2,1)S(1)} %get-tuple-element.14.rest_2_), channel_id=1, source_target_pairs={{0,8},{4,12},{8,16},{12,20},{16,24},{20,28},{24,0},{28,4},{1,9},{5... | collective-permute-start | bytes 196616 | tf_op jit(solution)/shard_map/ppermute | solution.py:32
  8.6 11.7 %collective-permute-start = (bf16[768,128]{1,0:T(8,128)(2,1)S(1)}, bf16[768,128]{1,0:T(8,128)(2,1)S(1)}, u32[]{:S(2)}, u32[]{:S(2)}) collective-permute-start(bf16[768,128]{1,0:T(8,128)(2,1)S(1)} %get-tuple-element.13), channel_id=1, source_target_pairs={{0,4},{4,8},{8,12},{12,16},{16,20},{20,24},{24,28},{28,0},{1,5},{5... | collective-permute-start | bytes 589832 | tf_op jit(solution)/shard_map/ppermute | solution.py:32
  10.2 5.5 %collective-permute-start.4 = (bf16[32,128]{1,0:T(8,128)(2,1)S(1)}, bf16[32,128]{1,0:T(8,128)(2,1)S(1)}, u32[]{:S(2)}, u32[]{:S(2)}) collective-permute-start(bf16[32,128]{1,0:T(8,128)(2,1)S(1)} %join.3.one_ref), channel_id=1, source_target_pairs={{0,8},{4,12},{8,16},{12,20},{16,24},{20,28},{24,0},{28,4},{1,9},{5... | collective-permute-start | bytes 24584 | tf_op jit(solution)/shard_map/ppermute | solution.py:32
  15.6 4.6 %collective-permute-start.5 = (bf16[64,128]{1,0:T(8,128)(2,1)S(1)}, bf16[64,128]{1,0:T(8,128)(2,1)S(1)}, u32[]{:S(2)}, u32[]{:S(2)}) collective-permute-start(bf16[64,128]{1,0:T(8,128)(2,1)S(1)} %join.4.one_ref), channel_id=1, source_target_pairs={{0,16},{4,20},{8,24},{12,28},{16,0},{20,4},{24,8},{28,12},{1,17},{... | collective-permute-start | bytes 49160 | tf_op jit(solution)/shard_map/ppermute | solution.py:32
  35.2 9.2 %collective-permute-start.10 = (bf16[256,1024]{1,0:T(8,128)(2,1)S(1)}, bf16[256,1024]{1,0:T(8,128)(2,1)S(1)}, u32[]{:S(2)}, u32[]{:S(2)}) collective-permute-start(bf16[256,1024]{1,0:T(8,128)(2,1)S(1)} %attend.10.rest_4_), channel_id=1, source_target_pairs={{0,1},{1,0},{2,3},{3,2},{4,5},{5,4},{6,7},{7,6},{8,9},{9,8},{10,11... | collective-permute-start | bytes 1572872 | tf_op jit(solution)/shard_map/ppermute | solution.py:41
  35.3 26.8 %collective-permute-start.8 = (bf16[256,768]{1,0:T(8,128)(2,1)S(1)}, bf16[256,768]{1,0:T(8,128)(2,1)S(1)}, u32[]{:S(2)}, u32[]{:S(2)}) collective-permute-start(bf16[256,768]{1,0:T(8,128)(2,1)S(1)} %attend.7.rest_4_), channel_id=1, source_target_pairs={{0,2},{1,3},{2,0},{3,1},{4,6},{5,7},{6,4},{7,5},{8,10},{9,11},{10,... | collective-permute-start | bytes 1179656 | tf_op jit(solution)/shard_map/ppermute | solution.py:41
  36.9 26.5 %collective-permute-start.7 = (bf16[256,512]{1,0:T(8,128)(2,1)S(1)}, bf16[256,512]{1,0:T(8,128)(2,1)S(1)}, u32[]{:S(2)}, u32[]{:S(2)}) collective-permute-start(bf16[256,512]{1,0:T(8,128)(2,1)S(1)} %attend.8.rest_4_), channel_id=1, source_target_pairs={{0,3},{1,2},{2,1},{3,0},{4,7},{5,6},{6,5},{7,4},{8,11},{9,10},{10,... | collective-permute-start | bytes 786440 | tf_op jit(solution)/shard_map/ppermute | solution.py:41
  37.1 27.5 %collective-permute-start.6 = (bf16[256,512]{1,0:T(8,128)(2,1)S(1)}, bf16[256,512]{1,0:T(8,128)(2,1)S(1)}, u32[]{:S(2)}, u32[]{:S(2)}) collective-permute-start(bf16[256,512]{1,0:T(8,128)(2,1)S(1)} %attend.9.rest_4_), channel_id=1, source_target_pairs={{0,3},{1,2},{2,1},{3,0},{4,7},{5,6},{6,5},{7,4},{8,11},{9,10},{10,... | collective-permute-start | bytes 786440 | tf_op jit(solution)/shard_map/ppermute | solution.py:41
  38.8 22.1 %collective-permute-start.9 = (bf16[256,256]{1,0:T(8,128)(2,1)S(1)}, bf16[256,256]{1,0:T(8,128)(2,1)S(1)}, u32[]{:S(2)}, u32[]{:S(2)}) collective-permute-start(bf16[256,256]{1,0:T(8,128)(2,1)S(1)} %attend.6.rest_4_), channel_id=1, source_target_pairs={{0,2},{1,3},{2,0},{3,1},{4,6},{5,7},{6,4},{7,5},{8,10},{9,11},{10,... | collective-permute-start | bytes 393224 | tf_op jit(solution)/shard_map/ppermute | solution.py:41

commit v3 on v2

v3 whole, which is shorter than its diff:
```python
import functools
import math

import jax
import jax.numpy as jnp
from jax import lax
from jax.experimental import pallas as pl
from jax.experimental.pallas import tpu as pltpu
from jax.sharding import PartitionSpec as P


HEAD_DIM = 128
BLK = 256
GROUP = 8
MIDS = 256
MIDB = 8
PER_GROUP = BLK // GROUP
LANES = 128
NEG = -1e30
HALF = BLK // 2
CHUNK = 32
VMEM_LIMIT = 16 * 1024 * 1024
ATTEND_LIMIT = 28 * 1024 * 1024
EXP_SCALE = math.log2(math.e) / math.sqrt(HEAD_DIM)
BF16 = jnp.bfloat16
F32 = jnp.float32


def round_up(value, multiple):
    return -(-value // multiple) * multiple


def cyclic(array, axis, by):
    size = lax.axis_size(axis)
    return lax.ppermute(array, axis, [(i, (i + by) % size) for i in range(size)])


def off_chip(*arrays):
    return [pltpu.with_memory_space_constraint(a, pltpu.HBM) for a in arrays]


def exchange(array, axis, flip):
    size = lax.axis_size(axis)
    return lax.ppermute(array, axis, [(i, i ^ flip) for i in range(size)])


def pool_kernel(block_count, last_blocks, slot, keys_hbm, values_hbm, mid_hbm, coarse_hbm,
                keys_ref, values_ref, coarse_out, mids_out, last_out, first_out,
                mid_ref, coarse_ref, arrived):
    copies = [
        pltpu.make_async_copy(source, target, arrived.at[i])
        for i, (source, target) in enumerate(
            (
                (mid_hbm, mid_ref),
                (coarse_hbm, coarse_ref),
                (keys_hbm, keys_ref),
                (values_hbm, values_ref),
            )
        )
    ]
    for copy in copies:
        copy.start()
    for copy in copies:
        copy.wait()
    rows = block_count * PER_GROUP
    repeat = (
        lax.broadcasted_iota(jnp.int32, (GROUP, BLK), 1) % GROUP
        == lax.broadcasted_iota(jnp.int32, (GROUP, BLK), 0)
    ).astype(BF16)
    tiled = jnp.dot(mid_ref[...], repeat, preferred_element_type=F32)
    owner = lax.broadcasted_iota(jnp.int32, (PER_GROUP, BLK), 1) // GROUP
    mine = owner == lax.broadcasted_iota(jnp.int32, (PER_GROUP, BLK), 0)
    mid_weights = jnp.where(mine, jnp.broadcast_to(tiled, (PER_GROUP, BLK)), 0.0)
    coarse_weights = coarse_ref[...].astype(F32)
    row = lax.broadcasted_iota(jnp.int32, (slot, BLK), 0)
    for source, mid_base, coarse_base in ((keys_ref, 0, 0), (values_ref, rows, slot)):
        total = jnp.zeros((slot, HEAD_DIM), F32)
        for block in range(block_count):
            here = source[block * BLK : (block + 1) * BLK, :]
            weights = jnp.concatenate(
                [mid_weights, jnp.where(row == block, jnp.broadcast_to(coarse_weights, (slot, BLK)), 0.0)]
            ).astype(BF16)
            pooled = jnp.dot(weights, here, preferred_element_type=F32)
            mids = pooled[:PER_GROUP].astype(BF16)
            total = total + pooled[PER_GROUP:]
            start = mid_base + block * PER_GROUP
            mids_out[start : start + PER_GROUP, :] = mids
            first_out[2 * BLK + start : 2 * BLK + start + PER_GROUP, :] = mids
            late = block - (block_count - last_blocks)
            if late >= 0:
                start = (mid_base // rows) * last_blocks * PER_GROUP + late * PER_GROUP
                last_out[start : start + PER_GROUP, :] = mids
        coarse_out[coarse_base : coarse_base + slot, :] = total.astype(BF16)
    edge = (block_count - 1) * BLK
    first_out[:BLK, :] = keys_ref[edge : edge + BLK, :]
    first_out[BLK : 2 * BLK, :] = values_ref[edge : edge + BLK, :]


def pool(keys, values, mid_pool, coarse_pool, block_count, last_blocks, slot):
    rows = block_count * PER_GROUP
    shapes = (
        keys.shape,
        values.shape,
        (2 * slot, HEAD_DIM),
        (2 * rows, HEAD_DIM),
        (2 * last_blocks * PER_GROUP, HEAD_DIM),
        (2 * BLK + 2 * rows, HEAD_DIM),
    )
    return pl.pallas_call(
        functools.partial(pool_kernel, block_count, last_blocks, slot),
        in_specs=[pl.BlockSpec(memory_space=pltpu.HBM)] * 4,
        out_specs=[pl.BlockSpec(memory_space=pltpu.VMEM) for _ in shapes],
        out_shape=[jax.ShapeDtypeStruct(shape, BF16) for shape in shapes],
        scratch_shapes=[
            pltpu.VMEM(mid_pool.shape, BF16),
            pltpu.VMEM(coarse_pool.shape, BF16),
            pltpu.SemaphoreType.DMA((4,)),
        ],
        cost_estimate=pl.CostEstimate(
            flops=4 * keys.size * (PER_GROUP + slot), bytes_accessed=6 * keys.size, transcendentals=0
        ),
        compiler_params=pltpu.CompilerParams(vmem_limit_bytes=VMEM_LIMIT),
        name="pool",
    )(*off_chip(keys, values, mid_pool, coarse_pool))


def join_kernel(one_ref, two_ref, out_ref):
    size = one_ref.shape[0]
    out_ref[:size, :] = one_ref[...]
    out_ref[size:, :] = two_ref[...]


def join(one, two):
    return pl.pallas_call(
        join_kernel,
        out_shape=jax.ShapeDtypeStruct((one.shape[0] + two.shape[0], one.shape[1]), one.dtype),
        compiler_params=pltpu.CompilerParams(vmem_limit_bytes=VMEM_LIMIT),
        name="join",
    )(one, two)


def load_kernel(*refs):
    count = len(refs) // 2
    copies = [
        pltpu.make_async_copy(refs[i], refs[count + i], refs[-1].at[i]) for i in range(count)
    ]
    for copy in copies:
        copy.start()
    for copy in copies:
        copy.wait()


def load(*arrays):
    return pl.pallas_call(
        load_kernel,
        in_specs=[pl.BlockSpec(memory_space=pltpu.HBM) for _ in arrays],
        out_specs=[pl.BlockSpec(memory_space=pltpu.VMEM) for _ in arrays],
        out_shape=[jax.ShapeDtypeStruct(a.shape, a.dtype) for a in arrays],
        scratch_shapes=[pltpu.SemaphoreType.DMA((len(arrays),))],
        compiler_params=pltpu.CompilerParams(vmem_limit_bytes=VMEM_LIMIT),
        cost_estimate=pl.CostEstimate(
            flops=2 * sum(a.size for a in arrays),
            bytes_accessed=4 * sum(a.size for a in arrays),
            transcendentals=0,
        ),
        name="load",
    )(*off_chip(*arrays))


def fill_summaries(geometry, target, width, sources, mid_scratch, which, write):
    block_count, hops, _, slot, reach = geometry
    source, first_ref = sources[which], sources[2]
    further, mids_ref, coarse_ref = sources[3 : 2 + hops], sources[-2], sources[-1]
    rows = block_count * PER_GROUP
    at = 0
    for index in range(hops - 2, -1, -1):
        size = further[index].shape[0] // 2
        mid_scratch[at : at + size, :] = further[index][which * size : (which + 1) * size, :]
        at += size
    start = 2 * BLK + which * rows
    mid_scratch[at : at + rows, :] = first_ref[start : start + rows, :]
    at += rows
    mid_scratch[at : at + rows, :] = mids_ref[which * rows : (which + 1) * rows, :]
    window = pl.ds(pl.multiple_of(target * PER_GROUP, PER_GROUP), MIDS)
    write(0, mid_scratch[window, :])
    wide = coarse_ref[...].astype(F32).reshape(reach, 2, slot, HEAD_DIM)[:, which]
    wide = wide.reshape(reach * slot, HEAD_DIM)
    if width > reach * slot:
        wide = jnp.concatenate([wide, jnp.zeros((width - reach * slot, HEAD_DIM), F32)])
    write(MIDS, wide.astype(BF16))
    before = pl.ds(pl.multiple_of(jnp.maximum(target - 1, 0) * BLK, BLK), BLK)
    write(MIDS + width, source[before, :])

    @pl.when(target == 0)
    def _():
        write(MIDS + width, first_ref[which * BLK : (which + 1) * BLK, :])


def pack_kernel(geometry, info_ref, *refs):
    sources, (_, out_ref, mid_scratch) = refs[:-3], refs[-3:]
    _, _, _, slot, reach = geometry
    for which in range(2):
        columns = slice(which * HEAD_DIM, (which + 1) * HEAD_DIM)

        def write(at, value):
            out_ref[at : at + value.shape[0], columns] = value

        fill_summaries(geometry, info_ref[0], reach * slot, sources, mid_scratch, which, write)


def whole_in_vmem(count):
    return [pl.BlockSpec(memory_space=pltpu.VMEM)] * count


def mid_rows(geometry):
    block_count, hops = geometry[:2]
    return (hops + 1) * block_count * PER_GROUP


def pack(info, shared, after, geometry):
    _, _, _, slot, reach = geometry
    rows = MIDS + reach * slot + BLK
    return pl.pallas_call(
        functools.partial(pack_kernel, geometry),
        in_specs=[pl.BlockSpec(memory_space=pltpu.SMEM)]
        + whole_in_vmem(len(shared))
        + [pl.BlockSpec(memory_space=pl.ANY)],
        out_specs=pl.BlockSpec(memory_space=pltpu.VMEM),
        out_shape=jax.ShapeDtypeStruct((rows, 2 * HEAD_DIM), BF16),
        scratch_shapes=[pltpu.VMEM((mid_rows(geometry), HEAD_DIM), BF16)],
        compiler_params=pltpu.CompilerParams(vmem_limit_bytes=VMEM_LIMIT),
        cost_estimate=pl.CostEstimate(
            flops=rows * HEAD_DIM, bytes_accessed=8 * rows * HEAD_DIM, transcendentals=0
        ),
        name="pack",
    )(info, *shared, after)


def fill_bias(geometry, target, device, width, bias):
    block_count, _, _, slot, reach = geometry
    block = device * block_count + target
    coarse_at = MIDS
    prev_at = MIDS + width
    lane = lax.broadcasted_iota(jnp.int32, bias.shape, 1)
    mid_ok = lane >= (MIDB + 1 - block) * PER_GROUP
    far = (lane - coarse_at) // slot
    nth = (lane - coarse_at) % slot
    coarse_ok = (
        (nth < block_count)
        & (far < reach)
        & (far <= device)
        & (far * block_count - nth + target >= MIDB + 2)
    )
    mid_bias = jnp.where(mid_ok, 0.0, NEG)
    coarse_bias = jnp.where(coarse_ok, 0.0, NEG)
    prev_bias = jnp.where(block * (lane + 1) >= 1, 0.0, NEG)
    bias[...] = jnp.where(
        lane < coarse_at, mid_bias, jnp.where(lane < prev_at, coarse_bias, prev_bias)
    )


def attend_rows(q_ref, row_start, head_start, heads, out_ref, scratch):
    all_keys, all_values, bias, scores, weights = scratch
    own_at = bias.shape[1]
    all_values[:, HEAD_DIM:] = jnp.ones((own_at + BLK, HEAD_DIM), BF16)

    group = max(1, heads // 2)
    units = [(first, half) for first in range(0, heads, group) for half in range(2)]
    row = lax.broadcasted_iota(jnp.int32, (CHUNK, HALF), 0)
    column = lax.broadcasted_iota(jnp.int32, (CHUNK, HALF), 1)

    def columns(head):
        return slice(head * HEAD_DIM, (head + 1) * HEAD_DIM)

    def score(unit):
        first, half = units[unit]
        seen = own_at + (half + 1) * HALF
        rows_here = pl.ds(pl.multiple_of(row_start + half * HALF, HALF), HALF)
        stacked = jnp.concatenate(
            [q_ref[rows_here, columns(head_start + first + i)] for i in range(group)]
        )
        scores[unit % 2, :, :seen] = lax.dot_general(
            stacked, all_keys[:seen, :], (((1,), (1,)), ((), ())), preferred_element_type=F32
        )

    def weigh(unit):
        _, half = units[unit]
        seen = own_at + (half + 1) * HALF
        for at in range(0, group * HALF, CHUNK):
            here = slice(at, at + CHUNK)
            parts = [scores[unit % 2, here, :own_at] + bias[0:1, :]]
            if half:
                parts.append(scores[unit % 2, here, own_at : own_at + HALF])
            edge = scores[unit % 2, here, seen - HALF : seen]
            parts.append(jnp.where(row + at % HALF >= column, edge, NEG))
            chunk = jnp.concatenate(parts, axis=1)
            top = jnp.max(chunk, axis=-1, keepdims=True)
            weights[unit % 2, here, :seen] = jnp.exp2((chunk - top) * EXP_SCALE).astype(BF16)

    def mix(unit):
        first, half = units[unit]
        seen = own_at + (half + 1) * HALF
        mixed = jnp.dot(
            weights[unit % 2, :, :seen], all_values[:seen, :], preferred_element_type=F32
        )
        mixed = (mixed[:, :HEAD_DIM] / mixed[:, HEAD_DIM:]).astype(BF16)
        for i in range(group):
            out_ref[half * HALF : (half + 1) * HALF, columns(first + i)] = mixed[
                i * HALF : (i + 1) * HALF
            ]

    for unit in range(len(units) + 2):
        if unit < len(units):
            score(unit)
        if 1 <= unit <= len(units):
            weigh(unit - 1)
        if unit >= 2:
            mix(unit - 2)


def attend_kernel(geometry, width, head_start, heads, info_ref, q_ref, *rest):
    sources, rest = rest[: geometry[1] + 4], rest[geometry[1] + 4 :]
    _, out_ref, mid_scratch = rest[:3]
    scratch = rest[3:]
    target, device = info_ref[0], info_ref[1]
    own_at = MIDS + width + BLK
    for which in range(2):
        everything = scratch[which]

        def write(at, value):
            everything[at : at + value.shape[0], :HEAD_DIM] = value

        fill_summaries(geometry, target, width, sources, mid_scratch, which, write)
        own = pl.ds(pl.multiple_of(target * BLK, BLK), BLK)
        write(own_at, sources[which][own, :])
    fill_bias(geometry, target, device, width, scratch[2])
    attend_rows(q_ref, target * BLK, head_start, heads, out_ref, scratch)


def shipped_kernel(geometry, width, heads, info_ref, early_ref, late_ref, _, out_ref, *scratch):
    _, _, _, slot, reach = geometry
    used = MIDS + reach * slot
    own_at = MIDS + width + BLK
    for which in range(2):
        everything = scratch[which]
        columns = slice(which * HEAD_DIM, (which + 1) * HEAD_DIM)
        everything[:used, :HEAD_DIM] = late_ref[:used, columns]
        if width > reach * slot:
            everything[used : MIDS + width, :HEAD_DIM] = jnp.zeros(
                (MIDS + width - used, HEAD_DIM), BF16
            )
        everything[MIDS + width : own_at, :HEAD_DIM] = late_ref[used:, columns]
        at = (heads + which) * HEAD_DIM
        everything[own_at:, :HEAD_DIM] = early_ref[:, at : at + HEAD_DIM]
    fill_bias(geometry, info_ref[0], info_ref[1], width, scratch[2])
    attend_rows(early_ref, 0, 0, heads, out_ref, scratch)


def attend_call(kernel, operands, heads, width, out_columns, out_map, extra_scratch, alias):
    total = MIDS + width + 2 * BLK
    unit_rows = max(1, heads // 2) * HALF
    whole = [pl.BlockSpec(a.shape, lambda i, info: (0, 0)) for a in operands[1:-1]]
    return pl.pallas_call(
        kernel,
        grid_spec=pltpu.PrefetchScalarGridSpec(
            num_scalar_prefetch=1,
            grid=(1,),
            in_specs=whole + [pl.BlockSpec(memory_space=pl.ANY)],
            out_specs=pl.BlockSpec((BLK, heads * HEAD_DIM), out_map),
            scratch_shapes=extra_scratch
            + [
                pltpu.VMEM((total, HEAD_DIM), BF16),
                pltpu.VMEM((total, 2 * HEAD_DIM), BF16),
                pltpu.VMEM((8, total - BLK), F32),
                pltpu.VMEM((2, unit_rows, total), F32),
                pltpu.VMEM((2, unit_rows, total), BF16),
            ],
        ),
        out_shape=jax.ShapeDtypeStruct((BLK, out_columns), BF16),
        input_output_aliases={len(operands) - 1: 0} if alias else {},
        compiler_params=pltpu.CompilerParams(vmem_limit_bytes=ATTEND_LIMIT),
        cost_estimate=pl.CostEstimate(
            flops=6 * BLK * heads * total * HEAD_DIM,
            bytes_accessed=4 * BLK * heads * HEAD_DIM + 1024 * 1024,
            transcendentals=BLK * heads * total,
        ),
        name="attend",
    )(*operands)


def attend(info, queries, shared, after, head_start, heads, geometry, full_columns=None):
    width = round_up(geometry[4] * geometry[3], LANES)
    if full_columns is None:
        out_columns, out_map = heads * HEAD_DIM, lambda i, info: (0, 0)
    else:
        out_columns, out_map = full_columns, lambda i, info: (0, info[2])
    return attend_call(
        functools.partial(attend_kernel, geometry, width, head_start, heads),
        (info, queries, *shared, after),
        heads,
        width,
        out_columns,
        out_map,
        [pltpu.VMEM((mid_rows(geometry), HEAD_DIM), BF16)],
        False,
    )


def attend_shipped(info, early, late, output, flip, heads, geometry):
    width = round_up(geometry[4] * geometry[3], LANES)
    return attend_call(
        functools.partial(shipped_kernel, geometry, width, heads),
        (info, early, late, output),
        heads,
        width,
        output.shape[1],
        lambda i, info: (0, info[2] ^ flip),
        [],
        True,
    )


def prepare_kernel(info_ref, queries_hbm, keys_hbm, values_hbm, out_ref, done):
    rows = pl.ds(pl.multiple_of(info_ref[0] * BLK, BLK), BLK)
    copies, at = [], 0
    for i, source in enumerate((queries_hbm, keys_hbm, values_hbm)):
        columns = slice(at, at + source.shape[1])
        copies.append(
            pltpu.make_async_copy(source.at[rows, :], out_ref.at[:, columns], done.at[i])
        )
        at += source.shape[1]
    for copy in copies:
        copy.start()
    for copy in copies:
        copy.wait()


def prepare(info, queries, keys, values):
    columns = queries.shape[1] + 2 * HEAD_DIM
    return pl.pallas_call(
        prepare_kernel,
        in_specs=[pl.BlockSpec(memory_space=pltpu.SMEM)]
        + [pl.BlockSpec(memory_space=pltpu.HBM)] * 3,
        out_specs=pl.BlockSpec(memory_space=pltpu.VMEM),
        out_shape=jax.ShapeDtypeStruct((BLK, columns), BF16),
        scratch_shapes=[pltpu.SemaphoreType.DMA((3,))],
        compiler_params=pltpu.CompilerParams(vmem_limit_bytes=VMEM_LIMIT),
        cost_estimate=pl.CostEstimate(
            flops=BLK * columns, bytes_accessed=4 * BLK * columns, transcendentals=0
        ),
        name="prepare",
    )(info, *off_chip(queries, keys, values))


def place_kernel(spots, columns, info_ref, *refs):
    pieces, out_ref, done = refs[: len(spots)], refs[-2], refs[-1]
    copies = []
    for i, (flip, at) in enumerate(spots):
        start = pl.multiple_of((info_ref[2] ^ flip) * columns + at, HEAD_DIM)
        target = out_ref.at[:, pl.ds(start, pieces[i].shape[1])]
        copies.append(pltpu.make_async_copy(pieces[i], target, done.at[i]))
    for copy in copies:
        copy.start()
    for copy in copies:
        copy.wait()


def place(info, output, pieces, columns):
    spots = [(flip, start * HEAD_DIM) for flip, start, _ in pieces]
    size = sum(piece.size for _, _, piece in pieces)
    return pl.pallas_call(
        functools.partial(place_kernel, spots, columns),
        in_specs=[pl.BlockSpec(memory_space=pltpu.SMEM)]
        + [pl.BlockSpec(memory_space=pltpu.VMEM)] * len(pieces)
        + [pl.BlockSpec(memory_space=pl.ANY)],
        out_specs=pl.BlockSpec(memory_space=pl.ANY),
        scratch_shapes=[pltpu.SemaphoreType.DMA((len(pieces),))],
        out_shape=jax.ShapeDtypeStruct(output.shape, output.dtype),
        input_output_aliases={len(pieces) + 1: 0},
        compiler_params=pltpu.CompilerParams(vmem_limit_bytes=VMEM_LIMIT),
        cost_estimate=pl.CostEstimate(flops=size, bytes_accessed=4 * size, transcendentals=0),
        name="place",
    )(info, *[piece for _, _, piece in pieces], output)


def body(queries, keys, values, mid_pool, coarse_pool):
    tokens_here, columns = queries.shape
    heads_here = columns // HEAD_DIM
    block_count = tokens_here // BLK
    members = lax.axis_size("head")
    length = lax.axis_size("seq")
    assert keys.shape[1] == HEAD_DIM and block_count == members
    assert block_count <= MIDB and members & (members - 1) == 0
    device = lax.axis_index("seq")
    member = lax.axis_index("head")
    hops = -(-(MIDB + 1) // block_count)
    last_blocks = MIDB + 1 - (hops - 1) * block_count
    slot = round_up(block_count, 8)

    away = members // 2

    def info(flip):
        return jnp.stack([member ^ flip, device, member]).astype(jnp.int32)

    early = prepare(info(away), queries, keys, values)
    early = exchange(early, "head", away)
    keys, values, coarse, mids, last, first = pool(
        keys, values, mid_pool, coarse_pool, block_count, last_blocks, slot
    )
    reach, step = 1, 0
    while reach < length:
        arriving = cyclic(coarse, "seq", reach)
        if step == 0:
            near = cyclic(first, "seq", 1)
        if 2 * reach >= length:
            (queries,) = load(queries)
        coarse = join(coarse, arriving)
        reach, step = 2 * reach, step + 1
    further = [cyclic(mids, "seq", by) for by in range(2, hops)]
    further += [cyclic(last, "seq", hops)]
    geometry = (block_count, hops, last_blocks, slot, reach)
    shared = (keys, values, near, *further, mids, coarse)

    late = pack(info(away), shared, coarse, geometry)
    after = late
    late = exchange(late, "head", away)
    arrived = []
    for flip in sent_flips(members):
        after = attend(info(flip), queries, shared, after, 0, heads_here, geometry)
        arrived.append((flip, 0, exchange(after, "head", flip)))
    output = attend(
        info(0), queries, shared, after, 0, heads_here, geometry, members * columns
    )
    output = attend_shipped(info(0), early, late, output, away, heads_here, geometry)
    output = place(info(0), output, [p for p in arrived if p[0] < away], columns)
    return place(info(0), output, [p for p in arrived if p[0] > away], columns)


def sent_flips(members):
    return [*range(members // 2 + 1, members), *range(1, members // 2)]


def solution(mesh):
    return jax.shard_map(
        body,
        mesh=mesh,
        in_specs=(
            P("seq", "head"),
            P("seq", "head"),
            P("seq", "head"),
            P("head", None),
            P("head", None),
        ),
        out_specs=P(("seq", "head"), None),
        check_vma=False,
    )
```

time: 66.1 us -> 58.7 us (0.89)
  Pallas kernels: 29.5 us -> 23.1 us
  waiting for transfers between devices: 23.4 us -> 22.2 us
    pallas_call x11 -> x8, Pallas kernels: 26.4 us -> 20 us  [the longest x4 15.1 us: attend_call(): pl.pallas_call(kernel, grid_spec=pltpu.PrefetchScalarGridSpec(num_scalar_...]
    ppermute x5 -> x4, waiting for transfers between devices: 15.1 us -> 14.1 us  [exchange(): return lax.ppermute(array, axis, [(i, i ^ flip) for i in range(size)])]
    ppermute x5 -> x4, starting transfers between devices: 3.91 us -> 3.78 us  [exchange(): return lax.ppermute(array, axis, [(i, i ^ flip) for i in range(size)])]
  transfers between devices with their start and end apart: 11 -> 10, of which waited for: 3 -> 3; matrix products, arithmetic and copies ran while one was open for 0% -> 1% of each run, Pallas kernels for 18% -> 35%
where the time goes in v3:
time: 58.7 us; the launch traced here: 58.5 us
  Pallas kernels  23.1 us (39%)
  waiting for transfers between devices  22.2 us (38%)
  starting transfers between devices  12.7 us (22%)
    pallas_call x4, Pallas kernels, attend_call(): pl.pallas_call(kernel, grid_spec=pltpu.PrefetchScalarGridSpec(num_scalar_...  15.1 us
    ppermute x4, waiting for transfers between devices, exchange(): return lax.ppermute(array, axis, [(i, i ^ flip) for i in range(size)])  14.1 us
    ppermute x6, starting transfers between devices, cyclic(): lax.ppermute(array, axis, [(i, (i + by) % size) for i in range(size)])  8.87 us
    ppermute x6, waiting for transfers between devices, cyclic(): lax.ppermute(array, axis, [(i, (i + by) % size) for i in range(size)])  8.11 us
    ppermute x4, starting transfers between devices, exchange(): return lax.ppermute(array, axis, [(i, i ^ flip) for i in range(size)])  3.78 us
    pallas_call x2, Pallas kernels, place(): pl.pallas_call(functools.partial(place_kernel, spots, columns), in_specs=...  2.7 us
    pallas_call x1, Pallas kernels, prepare(): pl.pallas_call(prepare_kernel, in_specs=[pl.BlockSpec(memory_space=pltpu....  1.62 us
    pallas_call x1, Pallas kernels, load(): pl.pallas_call(load_kernel, in_specs=[pl.BlockSpec(memory_space=pltpu.HBM...  1.6 us
  transfers between devices with their start and end apart: 10, of which 3 were waited for; matrix products, arithmetic and copies ran while one was open for 1% of the time, Pallas kernels for 35%

profile of v3, /device:TPU:0, one launch (start us, length us, event | category | flops | bytes accessed | tf_op | source)
XLA Modules:
  0.0 58.5 jit_solution(3853317604815844218)
XLA Ops:
  0.0 1.4 %pool.1 = (bf16[1024,128]{1,0:T(8,128)(2,1)S(1)}, bf16[1024,128]{1,0:T(8,128)(2,1)S(1)}, bf16[16,128]{1,0:T(8,128)(2,1)S(1)}, bf16[256,128]{1,0:T(8,128)(2,1)S(1...) custom-call(bf16[1024,128]{1,0:T(8,128)(2,1)} %keys_hbm.3, bf16[1024,128]{1,0:T(8,128)(2,1)} %values_hbm.3, ...), custom_call_target="tpu_custom_call" | custom-call | flops 20971520 | bytes 786432 | tf_op jit(solution)/shard_map/pool/pallas_call | solution.py:109
  1.4 3.0 %collective-permute-start.3 = (bf16[16,128]{1,0:T(8,128)(2,1)S(1)}, bf16[16,128]{1,0:T(8,128)(2,1)S(1)}, u32[]{:S(2)}, u32[]{:S(2)}) collective-permute-start(bf16[16,128]{1,0:T(8,128)(2,1)S(1)} %get-tuple-element.16.one_ref), channel_id=1, source_target_pairs={{0,4},{4,8},{8,12},{12,16},{16,20},{20,24},{24,28},{28,0},{1,5},{5... | collective-permute-start | bytes 12296 | tf_op jit(solution)/shard_map/ppermute | solution.py:35
  4.5 1.6 %collective-permute-start.1 = (bf16[256,128]{1,0:T(8,128)(2,1)S(1)}, bf16[256,128]{1,0:T(8,128)(2,1)S(1)}, u32[]{:S(2)}, u32[]{:S(2)}) collective-permute-start(bf16[256,128]{1,0:T(8,128)(2,1)S(1)} %get-tuple-element.14.refs_5_.rest_5_), channel_id=1, source_target_pairs={{0,8},{4,12},{8,16},{12,20},{16,24},{20,28},{24,0},{28,4},{1,9},{5... | collective-permute-start | bytes 196616 | tf_op jit(solution)/shard_map/ppermute | solution.py:35
  6.0 1.5 %collective-permute-start = (bf16[768,128]{1,0:T(8,128)(2,1)S(1)}, bf16[768,128]{1,0:T(8,128)(2,1)S(1)}, u32[]{:S(2)}, u32[]{:S(2)}) collective-permute-start(bf16[768,128]{1,0:T(8,128)(2,1)S(1)} %get-tuple-element.13), channel_id=1, source_target_pairs={{0,4},{4,8},{8,12},{12,16},{16,20},{20,24},{24,28},{28,0},{1,5},{5... | collective-permute-start | bytes 589832 | tf_op jit(solution)/shard_map/ppermute | solution.py:35
  7.6 2.5 %collective-permute-start.2 = (bf16[64,128]{1,0:T(8,128)(2,1)S(1)}, bf16[64,128]{1,0:T(8,128)(2,1)S(1)}, u32[]{:S(2)}, u32[]{:S(2)}) collective-permute-start(bf16[64,128]{1,0:T(8,128)(2,1)S(1)} %get-tuple-element.15), channel_id=1, source_target_pairs={{0,12},{4,16},{8,20},{12,24},{16,28},{20,0},{24,4},{28,8},{1,13},{... | collective-permute-start | bytes 49160 | tf_op jit(solution)/shard_map/ppermute | solution.py:35
  10.1 0.1 add_add_fusion.2.info_ref
  10.2 1.6 %prepare.1 = bf16[256,1280]{1,0:T(8,128)(2,1)S(1)} custom-call(s32[3]{0:T(128)S(1)} %add_add_fusion.2.info_ref, bf16[1024,1024]{1,0:T(8,128)(2,1)} %queries_hbm.1, bf16[1024,128]{1,0:T(8,128)(2,1)} %keys_hbm.3, bf16[1024,128]{1,0:T(8,128)(2,1)} %values_hbm.3), custom_call_target="tpu_custom_call" | custom-call | flops 327680 | bytes 1310720 | tf_op jit(solution)/shard_map/prepare/pallas_call | solution.py:440
  11.8 1.6 %collective-permute-start.8 = (bf16[256,1280]{1,0:T(8,128)(2,1)S(1)}, bf16[256,1280]{1,0:T(8,128)(2,1)S(1)}, u32[]{:S(2)}, u32[]{:S(2)}) collective-permute-start(bf16[256,1280]{1,0:T(8,128)(2,1)S(1)} %prepare.1), channel_id=1, source_target_pairs={{0,2},{1,3},{2,0},{3,1},{4,6},{5,7},{6,4},{7,5},{8,10},{9,11},{10,... | collective-permute-start | bytes 1966088 | tf_op jit(solution)/shard_map/ppermute | solution.py:44
  13.4 0.0 collective-permute-done.3.two_ref
  13.4 0.2 collective-permute-start.4
  13.6 0.1 add_add_fusion.1.info_ref
  13.7 5.2 %collective-permute-done.4.two_ref = bf16[32,128]{1,0:T(8,128)(2,1)S(1)} collective-permute-done((bf16[32,128]{1,0:T(8,128)(2,1)S(1)}, bf16[32,128]{1,0:T(8,128)(2,1)S(1)}, u32[]{:S(2)}, u32[]{:S(2)}) %collective-permute-start.4) | collective-permute-done | bytes 8224 | tf_op jit(solution)/shard_map/ppermute | solution.py:35
  18.8 0.0 collective-permute-start.5
  18.8 0.1 add_add_fusion.3.info_ref
  18.9 1.6 %load.1.q_ref = bf16[1024,1024]{1,0:T(8,128)(2,1)S(1)} custom-call(bf16[1024,1024]{1,0:T(8,128)(2,1)} %queries_hbm.1), custom_call_target="tpu_custom_call" | custom-call | flops 2097152 | bytes 4194304 | tf_op jit(solution)/shard_map/load/pallas_call | solution.py:154
  20.5 3.0 %collective-permute-done.5.two_ref = bf16[64,128]{1,0:T(8,128)(2,1)S(1)} collective-permute-done((bf16[64,128]{1,0:T(8,128)(2,1)S(1)}, bf16[64,128]{1,0:T(8,128)(2,1)S(1)}, u32[]{:S(2)}, u32[]{:S(2)}) %collective-permute-start.5) | collective-permute-done | bytes 16416 | tf_op jit(solution)/shard_map/ppermute | solution.py:35
  23.5 0.0 collective-permute-done.2.refs_4_.rest_4_
  23.5 0.0 collective-permute-done.1.refs_3_.rest_3_
  23.5 0.0 collective-permute-done.refs_2_.rest_2_
  23.5 0.6 %pack.1.rest_7_ = bf16[576,256]{1,0:T(8,128)(2,1)S(1)} custom-call(s32[3]{0:T(128)S(1)} %add_add_fusion.2.info_ref, bf16[1024,128]{1,0:T(8,128)(2,1)S(1)} %get-tuple-element.11.refs_0_.rest_0_, bf16[1024,128]{1,0:T(8,128)(2,1)S(1)} %get-tuple-element.12.refs_1_.rest_1_, bf16[768,128]{1,0:T(8,128)(2,1)S(1)} %collective-permute-done.refs_2_.rest_2_, ...), custom_call_target="tpu_custom_call" | custom-call | flops 73728 | bytes 589824 | tf_op jit(solution)/shard_map/pack/pallas_call | solution.py:223
  24.1 3.3 %attend.4.rest_7_ = bf16[256,1024]{1,0:T(8,128)(2,1)S(1)} custom-call(s32[3]{0:T(128)S(1)} %add_add_fusion.1.info_ref, bf16[1024,1024]{1,0:T(8,128)(2,1)S(1)} %load.1.q_ref, bf16[1024,128]{1,0:T(8,128)(2,1)S(1)} %get-tuple-element.11.refs_0_.rest_0_, bf16[1024,128]{1,0:T(8,128)(2,1)S(1)} %get-tuple-element.12.refs_1_.rest_1_, ...), custom_call_target="tpu_custom_call" | custom-call | flops 1409286144 | bytes 2097152 | tf_op jit(solution)/shard_map/attend/pallas_call | solution.py:363
  27.4 3.3 %attend.5.rest_7_ = bf16[256,1024]{1,0:T(8,128)(2,1)S(1)} custom-call(s32[3]{0:T(128)S(1)} %add_add_fusion.3.info_ref, bf16[1024,1024]{1,0:T(8,128)(2,1)S(1)} %load.1.q_ref, bf16[1024,128]{1,0:T(8,128)(2,1)S(1)} %get-tuple-element.11.refs_0_.rest_0_, bf16[1024,128]{1,0:T(8,128)(2,1)S(1)} %get-tuple-element.12.refs_1_.rest_1_, ...), custom_call_target="tpu_custom_call" | custom-call | flops 1409286144 | bytes 2097152 | tf_op jit(solution)/shard_map/attend/pallas_call | solution.py:363
  30.8 0.1 collective-permute-start.7
  30.8 0.6 %collective-permute-start.6 = (bf16[256,1024]{1,0:T(8,128)(2,1)S(1)}, bf16[256,1024]{1,0:T(8,128)(2,1)S(1)}, u32[]{:S(2)}, u32[]{:S(2)}) collective-permute-start(bf16[256,1024]{1,0:T(8,128)(2,1)S(1)} %attend.4.rest_7_), channel_id=1, source_target_pairs={{0,3},{1,2},{2,1},{3,0},{4,7},{5,6},{6,5},{7,4},{8,11},{9,10},{10,... | collective-permute-start | bytes 1572872 | tf_op jit(solution)/shard_map/ppermute | solution.py:44
  31.5 1.5 %collective-permute-start.9 = (bf16[576,256]{1,0:T(8,128)(2,1)S(1)}, bf16[576,256]{1,0:T(8,128)(2,1)S(1)}, u32[]{:S(2)}, u32[]{:S(2)}) collective-permute-start(bf16[576,256]{1,0:T(8,128)(2,1)S(1)} %pack.1.rest_7_), channel_id=1, source_target_pairs={{0,2},{1,3},{2,0},{3,1},{4,6},{5,7},{6,4},{7,5},{8,10},{9,11},{10,... | collective-permute-start | bytes 884744 | tf_op jit(solution)/shard_map/ppermute | solution.py:44
  33.0 0.1 add_add_fusion.info_ref
  33.0 4.3 %attend.6._ = bf16[256,4096]{1,0:T(8,128)(2,1)} custom-call(s32[3]{0:T(128)S(1)} %add_add_fusion.info_ref, bf16[1024,1024]{1,0:T(8,128)(2,1)S(1)} %load.1.q_ref, bf16[1024,128]{1,0:T(8,128)(2,1)S(1)} %get-tuple-element.11.refs_0_.rest_0_, bf16[1024,128]{1,0:T(8,128)(2,1)S(1)} %get-tuple-element.12.refs_1_.rest_1_, ...), custom_call_target="tpu_custom_call" | custom-call | flops 1409286144 | bytes 2097152 | tf_op jit(solution)/shard_map/attend/pallas_call | solution.py:363
  37.3 14.1 %collective-permute-done.9.late_ref = bf16[576,256]{1,0:T(8,128)(2,1)S(1)} collective-permute-done((bf16[576,256]{1,0:T(8,128)(2,1)S(1)}, bf16[576,256]{1,0:T(8,128)(2,1)S(1)}, u32[]{:S(2)}, u32[]{:S(2)}) %collective-permute-start.9) | collective-permute-done | bytes 294944 | tf_op jit(solution)/shard_map/ppermute | solution.py:44
  51.4 0.0 collective-permute-done.8.early_ref
  51.4 4.2 %attend.7.refs_1_ = bf16[256,4096]{1,0:T(8,128)(2,1)} custom-call(s32[3]{0:T(128)S(1)} %add_add_fusion.info_ref, bf16[256,1280]{1,0:T(8,128)(2,1)S(1)} %collective-permute-done.8.early_ref, bf16[576,256]{1,0:T(8,128)(2,1)S(1)} %collective-permute-done.9.late_ref, bf16[256,4096]{1,0:T(8,128)(2,1)} %attend.6._), custom_call_target="tpu_custom_call", output_to_operand_aliasing={{}: (3, {})} | custom-call | flops 1409286144 | bytes 2097152 | tf_op jit(solution)/shard_map/attend/pallas_call | solution.py:363
  55.6 0.0 collective-permute-done.7.refs_0_
  55.6 1.3 %place.2.refs_1_ = bf16[256,4096]{1,0:T(8,128)(2,1)} custom-call(s32[3]{0:T(128)S(1)} %add_add_fusion.info_ref, bf16[256,1024]{1,0:T(8,128)(2,1)S(1)} %collective-permute-done.7.refs_0_, bf16[256,4096]{1,0:T(8,128)(2,1)} %attend.7.refs_1_), custom_call_target="tpu_custom_call", output_to_operand_aliasing={{}: (2, {})} | custom-call | flops 262144 | bytes 1048576 | tf_op jit(solution)/shard_map/place/pallas_call | solution.py:471
  57.0 0.0 collective-permute-done.6.refs_0_
  57.0 1.4 %place.3 = bf16[256,4096]{1,0:T(8,128)(2,1)} custom-call(s32[3]{0:T(128)S(1)} %add_add_fusion.info_ref, bf16[256,1024]{1,0:T(8,128)(2,1)S(1)} %collective-permute-done.6.refs_0_, bf16[256,4096]{1,0:T(8,128)(2,1)} %place.2.refs_1_), custom_call_target="tpu_custom_call", output_to_operand_aliasing={{}: (2, {})} | custom-call | flops 262144 | bytes 1048576 | tf_op jit(solution)/shard_map/place/pallas_call | solution.py:471
  (3 shorter events, 0.0 us)
Async XLA Ops:
  1.4 11.9 %collective-permute-start.3 = (bf16[16,128]{1,0:T(8,128)(2,1)S(1)}, bf16[16,128]{1,0:T(8,128)(2,1)S(1)}, u32[]{:S(2)}, u32[]{:S(2)}) collective-permute-start(bf16[16,128]{1,0:T(8,128)(2,1)S(1)} %get-tuple-element.16.one_ref), channel_id=1, source_target_pairs={{0,4},{4,8},{8,12},{12,16},{16,20},{20,24},{24,28},{28,0},{1,5},{5... | collective-permute-start | bytes 12296 | tf_op jit(solution)/shard_map/ppermute | solution.py:35
  4.5 19.0 %collective-permute-start.1 = (bf16[256,128]{1,0:T(8,128)(2,1)S(1)}, bf16[256,128]{1,0:T(8,128)(2,1)S(1)}, u32[]{:S(2)}, u32[]{:S(2)}) collective-permute-start(bf16[256,128]{1,0:T(8,128)(2,1)S(1)} %get-tuple-element.14.refs_5_.rest_5_), channel_id=1, source_target_pairs={{0,8},{4,12},{8,16},{12,20},{16,24},{20,28},{24,0},{28,4},{1,9},{5... | collective-permute-start | bytes 196616 | tf_op jit(solution)/shard_map/ppermute | solution.py:35
  6.0 17.5 %collective-permute-start = (bf16[768,128]{1,0:T(8,128)(2,1)S(1)}, bf16[768,128]{1,0:T(8,128)(2,1)S(1)}, u32[]{:S(2)}, u32[]{:S(2)}) collective-permute-start(bf16[768,128]{1,0:T(8,128)(2,1)S(1)} %get-tuple-element.13), channel_id=1, source_target_pairs={{0,4},{4,8},{8,12},{12,16},{16,20},{20,24},{24,28},{28,0},{1,5},{5... | collective-permute-start | bytes 589832 | tf_op jit(solution)/shard_map/ppermute | solution.py:35
  7.6 15.9 %collective-permute-start.2 = (bf16[64,128]{1,0:T(8,128)(2,1)S(1)}, bf16[64,128]{1,0:T(8,128)(2,1)S(1)}, u32[]{:S(2)}, u32[]{:S(2)}) collective-permute-start(bf16[64,128]{1,0:T(8,128)(2,1)S(1)} %get-tuple-element.15), channel_id=1, source_target_pairs={{0,12},{4,16},{8,20},{12,24},{16,28},{20,0},{24,4},{28,8},{1,13},{... | collective-permute-start | bytes 49160 | tf_op jit(solution)/shard_map/ppermute | solution.py:35
  11.8 39.7 %collective-permute-start.8 = (bf16[256,1280]{1,0:T(8,128)(2,1)S(1)}, bf16[256,1280]{1,0:T(8,128)(2,1)S(1)}, u32[]{:S(2)}, u32[]{:S(2)}) collective-permute-start(bf16[256,1280]{1,0:T(8,128)(2,1)S(1)} %prepare.1), channel_id=1, source_target_pairs={{0,2},{1,3},{2,0},{3,1},{4,6},{5,7},{6,4},{7,5},{8,10},{9,11},{10,... | collective-permute-start | bytes 1966088 | tf_op jit(solution)/shard_map/ppermute | solution.py:44
  13.4 5.4 %collective-permute-start.4 = (bf16[32,128]{1,0:T(8,128)(2,1)S(1)}, bf16[32,128]{1,0:T(8,128)(2,1)S(1)}, u32[]{:S(2)}, u32[]{:S(2)}) collective-permute-start(bf16[32,128]{1,0:T(8,128)(2,1)S(1)} %join.3.one_ref), channel_id=1, source_target_pairs={{0,8},{4,12},{8,16},{12,20},{16,24},{20,28},{24,0},{28,4},{1,9},{5... | collective-permute-start | bytes 24584 | tf_op jit(solution)/shard_map/ppermute | solution.py:35
  18.8 4.6 %collective-permute-start.5 = (bf16[64,128]{1,0:T(8,128)(2,1)S(1)}, bf16[64,128]{1,0:T(8,128)(2,1)S(1)}, u32[]{:S(2)}, u32[]{:S(2)}) collective-permute-start(bf16[64,128]{1,0:T(8,128)(2,1)S(1)} %join.4.one_ref), channel_id=1, source_target_pairs={{0,16},{4,20},{8,24},{12,28},{16,0},{20,4},{24,8},{28,12},{1,17},{... | collective-permute-start | bytes 49160 | tf_op jit(solution)/shard_map/ppermute | solution.py:35
  30.8 24.9 %collective-permute-start.7 = (bf16[256,1024]{1,0:T(8,128)(2,1)S(1)}, bf16[256,1024]{1,0:T(8,128)(2,1)S(1)}, u32[]{:S(2)}, u32[]{:S(2)}) collective-permute-start(bf16[256,1024]{1,0:T(8,128)(2,1)S(1)} %attend.5.rest_7_), channel_id=1, source_target_pairs={{0,1},{1,0},{2,3},{3,2},{4,5},{5,4},{6,7},{7,6},{8,9},{9,8},{10,11... | collective-permute-start | bytes 1572872 | tf_op jit(solution)/shard_map/ppermute | solution.py:44
  30.8 26.1 %collective-permute-start.6 = (bf16[256,1024]{1,0:T(8,128)(2,1)S(1)}, bf16[256,1024]{1,0:T(8,128)(2,1)S(1)}, u32[]{:S(2)}, u32[]{:S(2)}) collective-permute-start(bf16[256,1024]{1,0:T(8,128)(2,1)S(1)} %attend.4.rest_7_), channel_id=1, source_target_pairs={{0,3},{1,2},{2,1},{3,0},{4,7},{5,6},{6,5},{7,4},{8,11},{9,10},{10,... | collective-permute-start | bytes 1572872 | tf_op jit(solution)/shard_map/ppermute | solution.py:44
  31.5 20.0 %collective-permute-start.9 = (bf16[576,256]{1,0:T(8,128)(2,1)S(1)}, bf16[576,256]{1,0:T(8,128)(2,1)S(1)}, u32[]{:S(2)}, u32[]{:S(2)}) collective-permute-start(bf16[576,256]{1,0:T(8,128)(2,1)S(1)} %pack.1.rest_7_), channel_id=1, source_target_pairs={{0,2},{1,3},{2,0},{3,1},{4,6},{5,7},{6,4},{7,5},{8,10},{9,11},{10,... | collective-permute-start | bytes 884744 | tf_op jit(solution)/shard_map/ppermute | solution.py:44

commit v4 on v3

v4 whole, which is shorter than its diff:
```python
import functools
import math

import jax
import jax.numpy as jnp
from jax import lax
from jax.experimental import pallas as pl
from jax.experimental.pallas import tpu as pltpu
from jax.sharding import PartitionSpec as P


HEAD_DIM = 128
BLK = 256
GROUP = 8
MIDS = 256
MIDB = 8
PER_GROUP = BLK // GROUP
LANES = 128
NEG = -1e30
HALF = BLK // 2
CHUNK = 32
SHARED = 7
VMEM_LIMIT = 16 * 1024 * 1024
ATTEND_LIMIT = 28 * 1024 * 1024
EXP_SCALE = math.log2(math.e) / math.sqrt(HEAD_DIM)
BF16 = jnp.bfloat16
F32 = jnp.float32


def round_up(value, multiple):
    return -(-value // multiple) * multiple


def cyclic(array, axis, by):
    size = lax.axis_size(axis)
    return lax.ppermute(array, axis, [(i, (i + by) % size) for i in range(size)])


def off_chip(*arrays):
    return [pltpu.with_memory_space_constraint(a, pltpu.HBM) for a in arrays]


def exchange(array, axis, flip):
    size = lax.axis_size(axis)
    return lax.ppermute(array, axis, [(i, i ^ flip) for i in range(size)])


def pool_kernel(block_count, slot, info_ref, queries_hbm, keys_hbm, values_hbm, mid_hbm, coarse_hbm,
                early_out, keys_ref, values_ref, near_out, tails_out, mid_ref, coarse_ref, arrived):
    wanted = pl.ds(pl.multiple_of(info_ref[0] * BLK, BLK), BLK)
    moves = [
        (mid_hbm, mid_ref),
        (coarse_hbm, coarse_ref),
        (keys_hbm, keys_ref),
        (values_hbm, values_ref),
    ]
    at = 0
    for source in (queries_hbm, keys_hbm, values_hbm):
        columns = slice(at, at + source.shape[1])
        moves.append((source.at[wanted, :], early_out.at[:, columns]))
        at += source.shape[1]
    copies = [
        pltpu.make_async_copy(source, target, arrived.at[i])
        for i, (source, target) in enumerate(moves)
    ]
    for copy in copies:
        copy.start()
    for copy in copies[:4]:
        copy.wait()
    rows = block_count * PER_GROUP
    repeat = (
        lax.broadcasted_iota(jnp.int32, (GROUP, BLK), 1) % GROUP
        == lax.broadcasted_iota(jnp.int32, (GROUP, BLK), 0)
    ).astype(BF16)
    tiled = jnp.dot(mid_ref[...], repeat, preferred_element_type=F32)
    owner = lax.broadcasted_iota(jnp.int32, (PER_GROUP, BLK), 1) // GROUP
    mine = owner == lax.broadcasted_iota(jnp.int32, (PER_GROUP, BLK), 0)
    mid_weights = jnp.where(mine, jnp.broadcast_to(tiled, (PER_GROUP, BLK)), 0.0)
    coarse_weights = coarse_ref[...].astype(F32)
    row = lax.broadcasted_iota(jnp.int32, (slot, BLK), 0)
    for which, source in enumerate((keys_ref, values_ref)):
        total = jnp.zeros((slot, HEAD_DIM), F32)
        for block in range(block_count):
            here = source[block * BLK : (block + 1) * BLK, :]
            weights = jnp.concatenate(
                [mid_weights, jnp.where(row == block, jnp.broadcast_to(coarse_weights, (slot, BLK)), 0.0)]
            ).astype(BF16)
            pooled = jnp.dot(weights, here, preferred_element_type=F32)
            total = total + pooled[PER_GROUP:]
            start = 2 * slot + which * rows + block * PER_GROUP
            near_out[start : start + PER_GROUP, :] = pooled[:PER_GROUP].astype(BF16)
        near_out[which * slot : (which + 1) * slot, :] = total.astype(BF16)
        edge = (block_count - 1) * BLK
        tails_out[which * BLK : (which + 1) * BLK, :] = source[edge : edge + BLK, :]
    for copy in copies[4:]:
        copy.wait()


def pool(info, queries, keys, values, mid_pool, coarse_pool, block_count, slot):
    shapes = (
        (BLK, queries.shape[1] + 2 * HEAD_DIM),
        keys.shape,
        values.shape,
        (2 * slot + 2 * block_count * PER_GROUP, HEAD_DIM),
        (2 * BLK, HEAD_DIM),
    )
    return pl.pallas_call(
        functools.partial(pool_kernel, block_count, slot),
        in_specs=[pl.BlockSpec(memory_space=pltpu.SMEM)]
        + [pl.BlockSpec(memory_space=pltpu.HBM)] * 5,
        out_specs=[pl.BlockSpec(memory_space=pltpu.VMEM) for _ in shapes],
        out_shape=[jax.ShapeDtypeStruct(shape, BF16) for shape in shapes],
        scratch_shapes=[
            pltpu.VMEM(mid_pool.shape, BF16),
            pltpu.VMEM(coarse_pool.shape, BF16),
            pltpu.SemaphoreType.DMA((7,)),
        ],
        cost_estimate=pl.CostEstimate(
            flops=4 * keys.size * (PER_GROUP + slot), bytes_accessed=6 * keys.size, transcendentals=0
        ),
        compiler_params=pltpu.CompilerParams(vmem_limit_bytes=VMEM_LIMIT),
        name="pool",
    )(info, *off_chip(queries, keys, values, mid_pool, coarse_pool))


def select_kernel(parts, *refs):
    out_ref, at = refs[-1], 0
    for index, start, size in parts:
        out_ref[at : at + size, :] = refs[index][start : start + size, :]
        at += size


def select(parts, *arrays):
    rows = sum(size for _, _, size in parts)
    return pl.pallas_call(
        functools.partial(select_kernel, parts),
        in_specs=[pl.BlockSpec(memory_space=pltpu.VMEM)] * len(arrays),
        out_specs=pl.BlockSpec(memory_space=pltpu.VMEM),
        out_shape=jax.ShapeDtypeStruct((rows, arrays[0].shape[1]), arrays[0].dtype),
        compiler_params=pltpu.CompilerParams(vmem_limit_bytes=VMEM_LIMIT),
        name="select",
    )(*arrays)


def load_kernel(*refs):
    count = len(refs) // 2
    copies = [
        pltpu.make_async_copy(refs[i], refs[count + i], refs[-1].at[i]) for i in range(count)
    ]
    for copy in copies:
        copy.start()
    for copy in copies:
        copy.wait()


def load(*arrays):
    return pl.pallas_call(
        load_kernel,
        in_specs=[pl.BlockSpec(memory_space=pltpu.HBM) for _ in arrays],
        out_specs=[pl.BlockSpec(memory_space=pltpu.VMEM) for _ in arrays],
        out_shape=[jax.ShapeDtypeStruct(a.shape, a.dtype) for a in arrays],
        scratch_shapes=[pltpu.SemaphoreType.DMA((len(arrays),))],
        compiler_params=pltpu.CompilerParams(vmem_limit_bytes=VMEM_LIMIT),
        cost_estimate=pl.CostEstimate(
            flops=2 * sum(a.size for a in arrays),
            bytes_accessed=4 * sum(a.size for a in arrays),
            transcendentals=0,
        ),
        name="load",
    )(*off_chip(*arrays))


def fill_summaries(geometry, target, width, sources, mid_scratch, which, write):
    block_count, last_blocks, slot, reach = geometry
    source = sources[which]
    tails_ref, near_ref, far_ref, mine_ref, coarse_ref = sources[2:]
    rows = block_count * PER_GROUP
    late = last_blocks * PER_GROUP
    at = 0
    for ref, start, size in (
        (far_ref, 2 * rows + which * late, late),
        (far_ref, which * rows, rows),
        (near_ref, 2 * slot + which * rows, rows),
        (mine_ref, 2 * slot + which * rows, rows),
    ):
        mid_scratch[at : at + size, :] = ref[start : start + size, :]
        at += size
    window = pl.ds(pl.multiple_of(target * PER_GROUP, PER_GROUP), MIDS)
    write(0, mid_scratch[window, :])
    wide = coarse_ref[...].astype(F32).reshape(reach, 2, slot, HEAD_DIM)[:, which]
    wide = wide.reshape(reach * slot, HEAD_DIM)
    if width > reach * slot:
        wide = jnp.concatenate([wide, jnp.zeros((width - reach * slot, HEAD_DIM), F32)])
    write(MIDS, wide.astype(BF16))
    before = pl.ds(pl.multiple_of(jnp.maximum(target - 1, 0) * BLK, BLK), BLK)
    write(MIDS + width, source[before, :])

    @pl.when(target == 0)
    def _():
        write(MIDS + width, tails_ref[which * BLK : (which + 1) * BLK, :])


def pack_kernel(geometry, info_ref, *refs):
    sources, (_, out_ref, mid_scratch) = refs[:-3], refs[-3:]
    _, _, slot, reach = geometry
    for which in range(2):
        columns = slice(which * HEAD_DIM, (which + 1) * HEAD_DIM)

        def write(at, value):
            out_ref[at : at + value.shape[0], columns] = value

        fill_summaries(geometry, info_ref[0], reach * slot, sources, mid_scratch, which, write)


def whole_in_vmem(count):
    return [pl.BlockSpec(memory_space=pltpu.VMEM)] * count


def mid_rows(geometry):
    block_count, last_blocks = geometry[:2]
    return (3 * block_count + last_blocks) * PER_GROUP


def pack(info, shared, after, geometry):
    _, _, slot, reach = geometry
    rows = MIDS + reach * slot + BLK
    return pl.pallas_call(
        functools.partial(pack_kernel, geometry),
        in_specs=[pl.BlockSpec(memory_space=pltpu.SMEM)]
        + whole_in_vmem(len(shared))
        + [pl.BlockSpec(memory_space=pl.ANY)],
        out_specs=pl.BlockSpec(memory_space=pltpu.VMEM),
        out_shape=jax.ShapeDtypeStruct((rows, 2 * HEAD_DIM), BF16),
        scratch_shapes=[pltpu.VMEM((mid_rows(geometry), HEAD_DIM), BF16)],
        compiler_params=pltpu.CompilerParams(vmem_limit_bytes=VMEM_LIMIT),
        cost_estimate=pl.CostEstimate(
            flops=rows * HEAD_DIM, bytes_accessed=8 * rows * HEAD_DIM, transcendentals=0
        ),
        name="pack",
    )(info, *shared, after)


def fill_bias(geometry, target, device, width, bias):
    block_count, _, slot, reach = geometry
    block = device * block_count + target
    coarse_at = MIDS
    prev_at = MIDS + width
    lane = lax.broadcasted_iota(jnp.int32, bias.shape, 1)
    mid_ok = lane >= (MIDB + 1 - block) * PER_GROUP
    far = (lane - coarse_at) // slot
    nth = (lane - coarse_at) % slot
    coarse_ok = (
        (nth < block_count)
        & (far < reach)
        & (far <= device)
        & (far * block_count - nth + target >= MIDB + 2)
    )
    mid_bias = jnp.where(mid_ok, 0.0, NEG)
    coarse_bias = jnp.where(coarse_ok, 0.0, NEG)
    prev_bias = jnp.where(block * (lane + 1) >= 1, 0.0, NEG)
    bias[...] = jnp.where(
        lane < coarse_at, mid_bias, jnp.where(lane < prev_at, coarse_bias, prev_bias)
    )


def attend_jobs(jobs, heads, scores, weights):
    group = max(1, heads // 2)
    units = [
        (job, first, half) for job in jobs for first in range(0, heads, group) for half in range(2)
    ]
    row = lax.broadcasted_iota(jnp.int32, (CHUNK, HALF), 0)
    column = lax.broadcasted_iota(jnp.int32, (CHUNK, HALF), 1)

    def score(unit):
        (q_ref, row_start, keys, _, bias, _), first, half = units[unit]
        seen = bias.shape[1] + (half + 1) * HALF
        rows_here = pl.ds(pl.multiple_of(row_start + half * HALF, HALF), HALF)
        stacked = jnp.concatenate([q_ref[rows_here, head_columns(first + i)] for i in range(group)])
        scores[unit % 2, :, :seen] = lax.dot_general(
            stacked, keys[:seen, :], (((1,), (1,)), ((), ())), preferred_element_type=F32
        )

    def weigh(unit):
        (_, _, _, _, bias, _), first, half = units[unit]
        own_at = bias.shape[1]
        seen = own_at + (half + 1) * HALF
        for at in range(0, group * HALF, CHUNK):
            here = slice(at, at + CHUNK)
            parts = [scores[unit % 2, here, :own_at] + bias[0:1, :]]
            if half:
                parts.append(scores[unit % 2, here, own_at : own_at + HALF])
            edge = scores[unit % 2, here, seen - HALF : seen]
            parts.append(jnp.where(row + at % HALF >= column, edge, NEG))
            chunk = jnp.concatenate(parts, axis=1)
            top = jnp.max(chunk, axis=-1, keepdims=True)
            weights[unit % 2, here, :seen] = jnp.exp2((chunk - top) * EXP_SCALE).astype(BF16)

    def mix(unit):
        (_, _, _, values, bias, emit), first, half = units[unit]
        seen = bias.shape[1] + (half + 1) * HALF
        mixed = jnp.dot(weights[unit % 2, :, :seen], values[:seen, :], preferred_element_type=F32)
        emit(first, group, half, (mixed[:, :HEAD_DIM] / mixed[:, HEAD_DIM:]).astype(BF16))

    for unit in range(len(units) + 2):
        if unit < len(units):
            score(unit)
        if 1 <= unit <= len(units):
            weigh(unit - 1)
        if unit >= 2:
            mix(unit - 2)


def head_columns(head):
    return slice(head * HEAD_DIM, (head + 1) * HEAD_DIM)


def store(ref, first_head, first, group, half, mixed):
    for i in range(group):
        ref[half * HALF : (half + 1) * HALF, head_columns(first_head + first + i)] = mixed[
            i * HALF : (i + 1) * HALF
        ]


def fill_local(geometry, width, info_ref, target, sources, mid_scratch, scratch):
    own_at = MIDS + width + BLK
    for which in range(2):
        everything = scratch[which]

        def write(at, value):
            everything[at : at + value.shape[0], :HEAD_DIM] = value

        fill_summaries(geometry, target, width, sources, mid_scratch, which, write)
        own = pl.ds(pl.multiple_of(target * BLK, BLK), BLK)
        write(own_at, sources[which][own, :])
    scratch[1][:, HEAD_DIM:] = jnp.ones((own_at + BLK, HEAD_DIM), BF16)
    fill_bias(geometry, target, info_ref[1], width, scratch[2])


def fill_shipped(geometry, width, info_ref, target, early_ref, late_ref, scratch):
    _, _, slot, reach = geometry
    used = MIDS + reach * slot
    own_at = MIDS + width + BLK
    for which in range(2):
        everything = scratch[which]
        columns = head_columns(which)
        everything[:used, :HEAD_DIM] = late_ref[:used, columns]
        if width > reach * slot:
            everything[used : MIDS + width, :HEAD_DIM] = jnp.zeros(
                (MIDS + width - used, HEAD_DIM), BF16
            )
        everything[MIDS + width : own_at, :HEAD_DIM] = late_ref[used:, columns]
        at = early_ref.shape[1] - (2 - which) * HEAD_DIM
        everything[own_at:, :HEAD_DIM] = early_ref[:, at : at + HEAD_DIM]
    scratch[1][:, HEAD_DIM:] = jnp.ones((own_at + BLK, HEAD_DIM), BF16)
    fill_bias(geometry, target, info_ref[1], width, scratch[2])


def attend_kernel(geometry, width, heads, info_ref, q_ref, *rest):
    sources, (_, out_ref, mid_scratch) = rest[:SHARED], rest[SHARED : SHARED + 3]
    scratch, (scores, weights) = rest[SHARED + 3 : SHARED + 6], rest[SHARED + 6 :]
    target = info_ref[0]
    fill_local(geometry, width, info_ref, target, sources, mid_scratch, scratch)
    emit = functools.partial(store, out_ref, 0)
    attend_jobs([(q_ref, target * BLK, *scratch, emit)], heads, scores, weights)


def finish_kernel(flip, geometry, width, heads, info_ref, q_ref, *rest):
    sources, rest = rest[:SHARED], rest[SHARED:]
    early_ref, late_ref, _, output, mid_scratch = rest[:5]
    rest = rest[2:]
    ours, theirs = rest[3:6], rest[6:9]
    scores, weights, results, sent = rest[9:]
    member = info_ref[2]
    copies = []

    fill_local(geometry, width, info_ref, info_ref[0], sources, mid_scratch, ours)
    fill_shipped(geometry, width, info_ref, info_ref[0], early_ref, late_ref, theirs)

    def emit(job, owner):
        def put(first, group, half, mixed):
            store(results, job * heads, first, group, half, mixed)
            if half:
                start = (job * heads + first) * HEAD_DIM
                size = group * HEAD_DIM
                at = pl.multiple_of((owner * heads + first) * HEAD_DIM, HEAD_DIM)
                copy = pltpu.make_async_copy(
                    results.at[:, start : start + size],
                    output.at[:, pl.ds(at, size)],
                    sent.at[len(copies)],
                )
                copies.append(copy)
                copy.start()

        return put

    attend_jobs(
        [
            (q_ref, info_ref[0] * BLK, *ours, emit(0, member)),
            (early_ref, 0, *theirs, emit(1, member ^ flip)),
        ],
        heads,
        scores,
        weights,
    )
    for copy in copies:
        copy.wait()


def context_scratch(total):
    return [
        pltpu.VMEM((total, HEAD_DIM), BF16),
        pltpu.VMEM((total, 2 * HEAD_DIM), BF16),
        pltpu.VMEM((8, total - BLK), F32),
    ]


def attend_call(kernel, operands, jobs, heads, geometry, out_columns, out_spec, extra):
    width = coarse_width(geometry)
    total = MIDS + width + 2 * BLK
    unit_rows = max(1, heads // 2) * HALF
    return pl.pallas_call(
        functools.partial(kernel, geometry, width, heads),
        in_specs=[pl.BlockSpec(memory_space=pltpu.SMEM)]
        + whole_in_vmem(len(operands) - 2)
        + [pl.BlockSpec(memory_space=pl.ANY)],
        out_specs=out_spec,
        scratch_shapes=[pltpu.VMEM((mid_rows(geometry), HEAD_DIM), BF16)]
        + context_scratch(total) * jobs
        + [
            pltpu.VMEM((2, unit_rows, total), F32),
            pltpu.VMEM((2, unit_rows, total), BF16),
        ]
        + extra,
        out_shape=jax.ShapeDtypeStruct((BLK, out_columns), BF16),
        compiler_params=pltpu.CompilerParams(vmem_limit_bytes=ATTEND_LIMIT),
        cost_estimate=pl.CostEstimate(
            flops=6 * jobs * BLK * heads * total * HEAD_DIM,
            bytes_accessed=4 * BLK * heads * HEAD_DIM + 1024 * 1024,
            transcendentals=jobs * BLK * heads * total,
        ),
        name="attend",
    )(*operands)


def coarse_width(geometry):
    return round_up(geometry[3] * geometry[2], LANES)


def attend(info, queries, shared, after, heads, geometry):
    return attend_call(
        attend_kernel,
        (info, queries, *shared, after),
        1,
        heads,
        geometry,
        heads * HEAD_DIM,
        pl.BlockSpec(memory_space=pltpu.VMEM),
        [],
    )


def finish(info, queries, shared, early, late, after, flip, heads, geometry, out_columns):
    kernel = functools.partial(finish_kernel, flip)
    groups = heads // max(1, heads // 2)
    return attend_call(
        kernel,
        (info, queries, *shared, early, late, after),
        2,
        heads,
        geometry,
        out_columns,
        pl.BlockSpec(memory_space=pl.ANY),
        [
            pltpu.VMEM((BLK, 2 * heads * HEAD_DIM), BF16),
            pltpu.SemaphoreType.DMA((2 * groups,)),
        ],
    )


def place_kernel(spots, columns, info_ref, *refs):
    pieces, out_ref, done = refs[: len(spots)], refs[-2], refs[-1]
    copies = []
    for i, (flip, at) in enumerate(spots):
        start = pl.multiple_of((info_ref[2] ^ flip) * columns + at, HEAD_DIM)
        target = out_ref.at[:, pl.ds(start, pieces[i].shape[1])]
        copies.append(pltpu.make_async_copy(pieces[i], target, done.at[i]))
    for copy in copies:
        copy.start()
    for copy in copies:
        copy.wait()


def place(info, output, pieces, columns):
    spots = [(flip, start * HEAD_DIM) for flip, start, _ in pieces]
    size = sum(piece.size for _, _, piece in pieces)
    return pl.pallas_call(
        functools.partial(place_kernel, spots, columns),
        in_specs=[pl.BlockSpec(memory_space=pltpu.SMEM)]
        + [pl.BlockSpec(memory_space=pltpu.VMEM)] * len(pieces)
        + [pl.BlockSpec(memory_space=pl.ANY)],
        out_specs=pl.BlockSpec(memory_space=pl.ANY),
        scratch_shapes=[pltpu.SemaphoreType.DMA((len(pieces),))],
        out_shape=jax.ShapeDtypeStruct(output.shape, output.dtype),
        input_output_aliases={len(pieces) + 1: 0},
        compiler_params=pltpu.CompilerParams(vmem_limit_bytes=VMEM_LIMIT),
        cost_estimate=pl.CostEstimate(flops=size, bytes_accessed=4 * size, transcendentals=0),
        name="place",
    )(info, *[piece for _, _, piece in pieces], output)


def body(queries, keys, values, mid_pool, coarse_pool):
    tokens_here, columns = queries.shape
    heads_here = columns // HEAD_DIM
    block_count = tokens_here // BLK
    members = lax.axis_size("head")
    length = lax.axis_size("seq")
    assert keys.shape[1] == HEAD_DIM and block_count == members
    assert block_count <= MIDB and members & (members - 1) == 0
    assert 2 * block_count <= MIDB < 3 * block_count
    device = lax.axis_index("seq")
    member = lax.axis_index("head")
    last_blocks = MIDB + 1 - 2 * block_count
    slot = round_up(block_count, 8)
    rows = block_count * PER_GROUP
    late_rows = last_blocks * PER_GROUP
    away = members // 2

    def info(flip):
        return jnp.stack([member ^ flip, device, member]).astype(jnp.int32)

    early, keys, values, mine, tails = pool(
        info(away), queries, keys, values, mid_pool, coarse_pool, block_count, slot
    )
    near = cyclic(mine, "seq", 1)
    early = exchange(early, "head", away)
    ends = [2 * slot + (i + 1) * rows - late_rows for i in range(2)]
    passing = select(
        [
            (0, 2 * slot, 2 * rows),
            *[(1, end, late_rows) for end in ends],
            (0, 0, 2 * slot),
            (1, 0, 2 * slot),
        ],
        mine,
        near,
    )
    far = cyclic(passing, "seq", 2)
    tails = cyclic(tails, "seq", 1)
    (queries,) = load(queries)
    summaries = 2 * rows + 2 * late_rows
    coarse = select([(0, summaries, 4 * slot), (1, summaries, 4 * slot)], passing, far)
    reach = 4
    while reach < length:
        arriving = cyclic(coarse, "seq", reach)
        size = coarse.shape[0]
        coarse = select([(0, 0, size), (1, 0, size)], coarse, arriving)
        reach *= 2
    geometry = (block_count, last_blocks, slot, reach)
    shared = (keys, values, tails, near, far, mine, coarse)

    late = pack(info(away), shared, coarse, geometry)
    after = late
    late = exchange(late, "head", away)
    arrived = []
    for flip in sent_flips(members):
        after = attend(info(flip), queries, shared, after, heads_here, geometry)
        arrived.append((flip, 0, exchange(after, "head", flip)))
    output = finish(
        info(0),
        queries,
        shared,
        early,
        late,
        after,
        away,
        heads_here,
        geometry,
        members * columns,
    )
    return place(info(0), output, arrived, columns)


def sent_flips(members):
    return [*range(members // 2 + 1, members), *range(1, members // 2)]


def solution(mesh):
    return jax.shard_map(
        body,
        mesh=mesh,
        in_specs=(
            P("seq", "head"),
            P("seq", "head"),
            P("seq", "head"),
            P("head", None),
            P("head", None),
        ),
        out_specs=P(("seq", "head"), None),
        check_vma=False,
    )
```

time: 58.7 us -> 46.6 us (0.79)
  starting transfers between devices: 12.7 us -> 8.56 us
  Pallas kernels: 23.1 us -> 19.2 us
  waiting for transfers between devices: 22.2 us -> 18.3 us
    ppermute x4, waiting for transfers between devices: 14.1 us -> 6.38 us  [exchange(): return lax.ppermute(array, axis, [(i, i ^ flip) for i in range(size)])]
    ppermute x6 -> x4, starting transfers between devices: 8.87 us -> 4.78 us  [cyclic(): lax.ppermute(array, axis, [(i, (i + by) % size) for i in range(size)])]
    ppermute x6 -> x4, waiting for transfers between devices: 8.11 us -> 12 us  [cyclic(): lax.ppermute(array, axis, [(i, (i + by) % size) for i in range(size)])]
    pallas_call x9 -> x7, Pallas kernels: 18.1 us -> 15.4 us  [the longest x3 13.4 us: attend_call(): pl.pallas_call(functools.partial(kernel, geometry, width, heads), in_spec...]
    pallas_call x2 -> x1, Pallas kernels: 2.7 us -> 1.53 us  [place(): pl.pallas_call(functools.partial(place_kernel, spots, columns), in_specs=...]
  transfers between devices with their start and end apart: 10 -> 8, of which waited for: 3 -> 4; matrix products, arithmetic and copies ran while one was open for 1% -> 0% of each run, Pallas kernels for 35% -> 34%
where the time goes in v4:
time: 46.6 us; the launch traced here: 46.5 us
  Pallas kernels  19.2 us (41%)
  waiting for transfers between devices  18.3 us (39%)
  starting transfers between devices  8.56 us (18%)
    pallas_call x3, Pallas kernels, attend_call(): pl.pallas_call(functools.partial(kernel, geometry, width, heads), in_spec...  13.4 us
    ppermute x4, waiting for transfers between devices, cyclic(): lax.ppermute(array, axis, [(i, (i + by) % size) for i in range(size)])  12 us
    ppermute x4, waiting for transfers between devices, exchange(): return lax.ppermute(array, axis, [(i, i ^ flip) for i in range(size)])  6.38 us
    ppermute x4, starting transfers between devices, cyclic(): lax.ppermute(array, axis, [(i, (i + by) % size) for i in range(size)])  4.78 us
    ppermute x4, starting transfers between devices, exchange(): return lax.ppermute(array, axis, [(i, i ^ flip) for i in range(size)])  3.78 us
    pallas_call x1, Pallas kernels, pool(): pl.pallas_call(functools.partial(pool_kernel, block_count, slot), in_spec...  2 us
    pallas_call x1, Pallas kernels, load(): pl.pallas_call(load_kernel, in_specs=[pl.BlockSpec(memory_space=pltpu.HBM...  1.6 us
    pallas_call x1, Pallas kernels, place(): pl.pallas_call(functools.partial(place_kernel, spots, columns), in_specs=...  1.53 us
  transfers between devices with their start and end apart: 8, of which 4 were waited for; matrix products, arithmetic and copies ran while one was open for 0% of the time, Pallas kernels for 34%

profile of v4, /device:TPU:0, one launch (start us, length us, event | category | flops | bytes accessed | tf_op | source)
XLA Modules:
  0.0 46.5 jit_solution(13455956363267674820)
XLA Ops:
  0.0 0.1 add_add_fusion.2.info_ref
  0.1 2.0 %pool.1 = (bf16[256,1280]{1,0:T(8,128)(2,1)S(1)}, bf16[1024,128]{1,0:T(8,128)(2,1)S(1)}, bf16[1024,128]{1,0:T(8,128)(2,1)S(1)}, bf16[272,128]{1,0:T(8,128)(2,1)S(1)}, bf16[512,128]{1,0:T(8,128)(2,1)S(1)}) custom-call(s32[3]{0:T(128)S(1)} %add_add_fusion.2.info_ref, bf16[1024,1024]{1,0:T(8,128)(2,1)} %queries_hbm.1, bf16[1024,128]{1,0:T(8,128)(2,1)} %keys_hbm.1, ...), custom_call_target="tpu_custom_call" | custom-call | flops 20971520 | bytes 786432 | tf_op jit(solution)/shard_map/pool/pallas_call | solution.py:107
  2.1 3.0 %collective-permute-start.1 = (bf16[272,128]{1,0:T(8,128)(2,1)S(1)}, bf16[272,128]{1,0:T(8,128)(2,1)S(1)}, u32[]{:S(2)}, u32[]{:S(2)}) collective-permute-start(bf16[272,128]{1,0:T(8,128)(2,1)S(1)} %get-tuple-element.13.refs_0_.refs_5_.rest_5_), channel_id=1, source_target_pairs={{0,4},{4,8},{8,12},{12,16},{16,20},{20,24},{24,28},{28,0},{1,5},{5... | collective-permute-start | bytes 208904 | tf_op jit(solution)/shard_map/ppermute | solution.py:36
  5.1 1.5 %collective-permute-start = (bf16[512,128]{1,0:T(8,128)(2,1)S(1)}, bf16[512,128]{1,0:T(8,128)(2,1)S(1)}, u32[]{:S(2)}, u32[]{:S(2)}) collective-permute-start(bf16[512,128]{1,0:T(8,128)(2,1)S(1)} %get-tuple-element.12), channel_id=1, source_target_pairs={{0,4},{4,8},{8,12},{12,16},{16,20},{20,24},{24,28},{28,0},{1,5},{5... | collective-permute-start | bytes 393224 | tf_op jit(solution)/shard_map/ppermute | solution.py:36
  6.7 1.5 %collective-permute-start.6 = (bf16[256,1280]{1,0:T(8,128)(2,1)S(1)}, bf16[256,1280]{1,0:T(8,128)(2,1)S(1)}, u32[]{:S(2)}, u32[]{:S(2)}) collective-permute-start(bf16[256,1280]{1,0:T(8,128)(2,1)S(1)} %get-tuple-element.14), channel_id=1, source_target_pairs={{0,2},{1,3},{2,0},{3,1},{4,6},{5,7},{6,4},{7,5},{8,10},{9,11},{10,... | collective-permute-start | bytes 1966088 | tf_op jit(solution)/shard_map/ppermute | solution.py:45
  8.2 2.7 %collective-permute-done.1.refs_1_.refs_3_.rest_3_ = bf16[272,128]{1,0:T(8,128)(2,1)S(1)} collective-permute-done((bf16[272,128]{1,0:T(8,128)(2,1)S(1)}, bf16[272,128]{1,0:T(8,128)(2,1)S(1)}, u32[]{:S(2)}, u32[]{:S(2)}) %collective-permute-start.1) | collective-permute-done | bytes 69664 | tf_op jit(solution)/shard_map/ppermute | solution.py:36
  10.9 0.2 collective-permute-start.2
  11.1 0.1 add_add_fusion.3.info_ref
  11.2 6.3 %collective-permute-done.2.refs_1_.refs_4_.rest_4_ = bf16[352,128]{1,0:T(8,128)(2,1)S(1)} collective-permute-done((bf16[352,128]{1,0:T(8,128)(2,1)S(1)}, bf16[352,128]{1,0:T(8,128)(2,1)S(1)}, u32[]{:S(2)}, u32[]{:S(2)}) %collective-permute-start.2) | collective-permute-done | bytes 90144 | tf_op jit(solution)/shard_map/ppermute | solution.py:36
  17.5 0.0 collective-permute-start.3
  17.5 0.1 add_add_fusion.1.info_ref
  17.6 1.6 %load.1.q_ref = bf16[1024,1024]{1,0:T(8,128)(2,1)S(1)} custom-call(bf16[1024,1024]{1,0:T(8,128)(2,1)} %queries_hbm.1), custom_call_target="tpu_custom_call" | custom-call | flops 2097152 | bytes 4194304 | tf_op jit(solution)/shard_map/load/pallas_call | solution.py:157
  19.2 3.0 %collective-permute-done.3.refs_1_ = bf16[64,128]{1,0:T(8,128)(2,1)S(1)} collective-permute-done((bf16[64,128]{1,0:T(8,128)(2,1)S(1)}, bf16[64,128]{1,0:T(8,128)(2,1)S(1)}, u32[]{:S(2)}, u32[]{:S(2)}) %collective-permute-start.3) | collective-permute-done | bytes 16416 | tf_op jit(solution)/shard_map/ppermute | solution.py:36
  22.1 0.0 collective-permute-done.refs_2_.rest_2_
  22.1 0.6 %pack.1.rest_7_ = bf16[576,256]{1,0:T(8,128)(2,1)S(1)} custom-call(s32[3]{0:T(128)S(1)} %add_add_fusion.2.info_ref, bf16[1024,128]{1,0:T(8,128)(2,1)S(1)} %get-tuple-element.10.refs_0_.rest_0_, bf16[1024,128]{1,0:T(8,128)(2,1)S(1)} %get-tuple-element.11.refs_1_.rest_1_, bf16[512,128]{1,0:T(8,128)(2,1)S(1)} %collective-permute-done.refs_2_.rest_2_, ...), custom_call_target="tpu_custom_call" | custom-call | flops 73728 | bytes 589824 | tf_op jit(solution)/shard_map/pack/pallas_call | solution.py:227
  22.7 1.8 %collective-permute-start.7 = (bf16[576,256]{1,0:T(8,128)(2,1)S(1)}, bf16[576,256]{1,0:T(8,128)(2,1)S(1)}, u32[]{:S(2)}, u32[]{:S(2)}) collective-permute-start(bf16[576,256]{1,0:T(8,128)(2,1)S(1)} %pack.1.rest_7_), channel_id=1, source_target_pairs={{0,2},{1,3},{2,0},{3,1},{4,6},{5,7},{6,4},{7,5},{8,10},{9,11},{10,... | collective-permute-start | bytes 884744 | tf_op jit(solution)/shard_map/ppermute | solution.py:45
  24.5 3.3 %attend.3.rest_7_ = bf16[256,1024]{1,0:T(8,128)(2,1)S(1)} custom-call(s32[3]{0:T(128)S(1)} %add_add_fusion.1.info_ref, bf16[1024,1024]{1,0:T(8,128)(2,1)S(1)} %load.1.q_ref, bf16[1024,128]{1,0:T(8,128)(2,1)S(1)} %get-tuple-element.10.refs_0_.rest_0_, bf16[1024,128]{1,0:T(8,128)(2,1)S(1)} %get-tuple-element.11.refs_1_.rest_1_, ...), custom_call_target="tpu_custom_call" | custom-call | flops 1409286144 | bytes 2097152 | tf_op jit(solution)/shard_map/attend/pallas_call | solution.py:421
  27.9 3.3 %attend.4.rest_9_ = bf16[256,1024]{1,0:T(8,128)(2,1)S(1)} custom-call(s32[3]{0:T(128)S(1)} %add_add_fusion.3.info_ref, bf16[1024,1024]{1,0:T(8,128)(2,1)S(1)} %load.1.q_ref, bf16[1024,128]{1,0:T(8,128)(2,1)S(1)} %get-tuple-element.10.refs_0_.rest_0_, bf16[1024,128]{1,0:T(8,128)(2,1)S(1)} %get-tuple-element.11.refs_1_.rest_1_, ...), custom_call_target="tpu_custom_call" | custom-call | flops 1409286144 | bytes 2097152 | tf_op jit(solution)/shard_map/attend/pallas_call | solution.py:421
  31.2 0.1 collective-permute-start.5
  31.2 0.4 collective-permute-start.4
  31.6 0.1 add_add_fusion.info_ref
  31.7 0.0 collective-permute-done.7.rest_8_
  31.7 0.0 collective-permute-done.6.rest_7_
  31.7 6.8 %attend.5.refs_2_ = bf16[256,4096]{1,0:T(8,128)(2,1)} custom-call(s32[3]{0:T(128)S(1)} %add_add_fusion.info_ref, bf16[1024,1024]{1,0:T(8,128)(2,1)S(1)} %load.1.q_ref, bf16[1024,128]{1,0:T(8,128)(2,1)S(1)} %get-tuple-element.10.refs_0_.rest_0_, bf16[1024,128]{1,0:T(8,128)(2,1)S(1)} %get-tuple-element.11.refs_1_.rest_1_, ...), custom_call_target="tpu_custom_call" | custom-call | flops 2818572288 | bytes 2097152 | tf_op jit(solution)/shard_map/attend/pallas_call | solution.py:421
  38.5 0.0 collective-permute-done.5.refs_1_
  38.5 6.4 %collective-permute-done.4.refs_0_ = bf16[256,1024]{1,0:T(8,128)(2,1)S(1)} collective-permute-done((bf16[256,1024]{1,0:T(8,128)(2,1)S(1)}, bf16[256,1024]{1,0:T(8,128)(2,1)S(1)}, u32[]{:S(2)}, u32[]{:S(2)}) %collective-permute-start.4) | collective-permute-done | bytes 524320 | tf_op jit(solution)/shard_map/ppermute | solution.py:45
  44.9 1.5 %place.1 = bf16[256,4096]{1,0:T(8,128)(2,1)} custom-call(s32[3]{0:T(128)S(1)} %add_add_fusion.info_ref, bf16[256,1024]{1,0:T(8,128)(2,1)S(1)} %collective-permute-done.4.refs_0_, bf16[256,1024]{1,0:T(8,128)(2,1)S(1)} %collective-permute-done.5.refs_1_, bf16[256,4096]{1,0:T(8,128)(2,1)} %attend.5.refs_2_), custom_call_target="tpu_custom_call", output_to_operand_aliasing={{}: (3, {})} | custom-call | flops 524288 | bytes 2097152 | tf_op jit(solution)/shard_map/place/pallas_call | solution.py:496
  (3 shorter events, 0.0 us)
Async XLA Ops:
  2.1 8.8 %collective-permute-start.1 = (bf16[272,128]{1,0:T(8,128)(2,1)S(1)}, bf16[272,128]{1,0:T(8,128)(2,1)S(1)}, u32[]{:S(2)}, u32[]{:S(2)}) collective-permute-start(bf16[272,128]{1,0:T(8,128)(2,1)S(1)} %get-tuple-element.13.refs_0_.refs_5_.rest_5_), channel_id=1, source_target_pairs={{0,4},{4,8},{8,12},{12,16},{16,20},{20,24},{24,28},{28,0},{1,5},{5... | collective-permute-start | bytes 208904 | tf_op jit(solution)/shard_map/ppermute | solution.py:36
  5.1 17.0 %collective-permute-start = (bf16[512,128]{1,0:T(8,128)(2,1)S(1)}, bf16[512,128]{1,0:T(8,128)(2,1)S(1)}, u32[]{:S(2)}, u32[]{:S(2)}) collective-permute-start(bf16[512,128]{1,0:T(8,128)(2,1)S(1)} %get-tuple-element.12), channel_id=1, source_target_pairs={{0,4},{4,8},{8,12},{12,16},{16,20},{20,24},{24,28},{28,0},{1,5},{5... | collective-permute-start | bytes 393224 | tf_op jit(solution)/shard_map/ppermute | solution.py:36
  6.7 25.1 %collective-permute-start.6 = (bf16[256,1280]{1,0:T(8,128)(2,1)S(1)}, bf16[256,1280]{1,0:T(8,128)(2,1)S(1)}, u32[]{:S(2)}, u32[]{:S(2)}) collective-permute-start(bf16[256,1280]{1,0:T(8,128)(2,1)S(1)} %get-tuple-element.14), channel_id=1, source_target_pairs={{0,2},{1,3},{2,0},{3,1},{4,6},{5,7},{6,4},{7,5},{8,10},{9,11},{10,... | collective-permute-start | bytes 1966088 | tf_op jit(solution)/shard_map/ppermute | solution.py:45
  10.9 6.6 %collective-permute-start.2 = (bf16[352,128]{1,0:T(8,128)(2,1)S(1)}, bf16[352,128]{1,0:T(8,128)(2,1)S(1)}, u32[]{:S(2)}, u32[]{:S(2)}) collective-permute-start(bf16[352,128]{1,0:T(8,128)(2,1)S(1)} %select.3.refs_0_), channel_id=1, source_target_pairs={{0,8},{4,12},{8,16},{12,20},{16,24},{20,28},{24,0},{28,4},{1,9},{5... | collective-permute-start | bytes 270344 | tf_op jit(solution)/shard_map/ppermute | solution.py:36
  17.5 4.6 %collective-permute-start.3 = (bf16[64,128]{1,0:T(8,128)(2,1)S(1)}, bf16[64,128]{1,0:T(8,128)(2,1)S(1)}, u32[]{:S(2)}, u32[]{:S(2)}) collective-permute-start(bf16[64,128]{1,0:T(8,128)(2,1)S(1)} %select.4.refs_0_), channel_id=1, source_target_pairs={{0,16},{4,20},{8,24},{12,28},{16,0},{20,4},{24,8},{28,12},{1,17},{... | collective-permute-start | bytes 49160 | tf_op jit(solution)/shard_map/ppermute | solution.py:36
  22.7 9.0 %collective-permute-start.7 = (bf16[576,256]{1,0:T(8,128)(2,1)S(1)}, bf16[576,256]{1,0:T(8,128)(2,1)S(1)}, u32[]{:S(2)}, u32[]{:S(2)}) collective-permute-start(bf16[576,256]{1,0:T(8,128)(2,1)S(1)} %pack.1.rest_7_), channel_id=1, source_target_pairs={{0,2},{1,3},{2,0},{3,1},{4,6},{5,7},{6,4},{7,5},{8,10},{9,11},{10,... | collective-permute-start | bytes 884744 | tf_op jit(solution)/shard_map/ppermute | solution.py:45
  31.2 7.4 %collective-permute-start.5 = (bf16[256,1024]{1,0:T(8,128)(2,1)S(1)}, bf16[256,1024]{1,0:T(8,128)(2,1)S(1)}, u32[]{:S(2)}, u32[]{:S(2)}) collective-permute-start(bf16[256,1024]{1,0:T(8,128)(2,1)S(1)} %attend.4.rest_9_), channel_id=1, source_target_pairs={{0,1},{1,0},{2,3},{3,2},{4,5},{5,4},{6,7},{7,6},{8,9},{9,8},{10,11... | collective-permute-start | bytes 1572872 | tf_op jit(solution)/shard_map/ppermute | solution.py:45
  31.2 13.7 %collective-permute-start.4 = (bf16[256,1024]{1,0:T(8,128)(2,1)S(1)}, bf16[256,1024]{1,0:T(8,128)(2,1)S(1)}, u32[]{:S(2)}, u32[]{:S(2)}) collective-permute-start(bf16[256,1024]{1,0:T(8,128)(2,1)S(1)} %attend.3.rest_7_), channel_id=1, source_target_pairs={{0,3},{1,2},{2,1},{3,0},{4,7},{5,6},{6,5},{7,4},{8,11},{9,10},{10,... | collective-permute-start | bytes 1572872 | tf_op jit(solution)/shard_map/ppermute | solution.py:45

commit v5 on v4

--- a/solution.py
+++ b/solution.py
@@ -19,7 +19,7 @@
 NEG = -1e30
 HALF = BLK // 2
 CHUNK = 32
-SHARED = 7
+SHARED = 8
 VMEM_LIMIT = 16 * 1024 * 1024
 ATTEND_LIMIT = 28 * 1024 * 1024
 EXP_SCALE = math.log2(math.e) / math.sqrt(HEAD_DIM)
@@ -45,8 +45,9 @@
     return lax.ppermute(array, axis, [(i, i ^ flip) for i in range(size)])
 
 
-def pool_kernel(block_count, slot, info_ref, queries_hbm, keys_hbm, values_hbm, mid_hbm, coarse_hbm,
-                early_out, keys_ref, values_ref, near_out, tails_out, mid_ref, coarse_ref, arrived):
+def pool_kernel(block_count, last_blocks, slot, info_ref, queries_hbm, keys_hbm, values_hbm, mid_hbm, coarse_hbm,
+                early_out, keys_ref, values_ref, near_out, third_out, tails_out, mid_ref, coarse_ref,
+                arrived):
     wanted = pl.ds(pl.multiple_of(info_ref[0] * BLK, BLK), BLK)
     moves = [
         (mid_hbm, mid_ref),
@@ -88,24 +89,31 @@
             pooled = jnp.dot(weights, here, preferred_element_type=F32)
             total = total + pooled[PER_GROUP:]
             start = 2 * slot + which * rows + block * PER_GROUP
-            near_out[start : start + PER_GROUP, :] = pooled[:PER_GROUP].astype(BF16)
+            mids = pooled[:PER_GROUP].astype(BF16)
+            near_out[start : start + PER_GROUP, :] = mids
+            nth = block - (block_count - last_blocks)
+            if nth >= 0:
+                start = 2 * slot + (which * last_blocks + nth) * PER_GROUP
+                third_out[start : start + PER_GROUP, :] = mids
         near_out[which * slot : (which + 1) * slot, :] = total.astype(BF16)
+        third_out[which * slot : (which + 1) * slot, :] = total.astype(BF16)
         edge = (block_count - 1) * BLK
         tails_out[which * BLK : (which + 1) * BLK, :] = source[edge : edge + BLK, :]
     for copy in copies[4:]:
         copy.wait()
 
 
-def pool(info, queries, keys, values, mid_pool, coarse_pool, block_count, slot):
+def pool(info, queries, keys, values, mid_pool, coarse_pool, block_count, last_blocks, slot):
     shapes = (
         (BLK, queries.shape[1] + 2 * HEAD_DIM),
         keys.shape,
         values.shape,
         (2 * slot + 2 * block_count * PER_GROUP, HEAD_DIM),
+        (2 * slot + 2 * last_blocks * PER_GROUP, HEAD_DIM),
         (2 * BLK, HEAD_DIM),
     )
     return pl.pallas_call(
-        functools.partial(pool_kernel, block_count, slot),
+        functools.partial(pool_kernel, block_count, last_blocks, slot),
         in_specs=[pl.BlockSpec(memory_space=pltpu.SMEM)]
         + [pl.BlockSpec(memory_space=pltpu.HBM)] * 5,
         out_specs=[pl.BlockSpec(memory_space=pltpu.VMEM) for _ in shapes],
@@ -170,16 +178,16 @@
     )(*off_chip(*arrays))
 
 
-def fill_summaries(geometry, target, width, sources, mid_scratch, which, write):
-    block_count, last_blocks, slot, reach = geometry
+def fill_late(geometry, target, prev_at, sources, mid_scratch, which, write):
+    block_count, last_blocks, slot, _ = geometry
     source = sources[which]
-    tails_ref, near_ref, far_ref, mine_ref, coarse_ref = sources[2:]
+    tails_ref, near_ref, far_ref, third_ref, mine_ref = sources[2:7]
     rows = block_count * PER_GROUP
     late = last_blocks * PER_GROUP
     at = 0
     for ref, start, size in (
-        (far_ref, 2 * rows + which * late, late),
-        (far_ref, which * rows, rows),
+        (third_ref, 2 * slot + which * late, late),
+        (far_ref, 2 * slot + which * rows, rows),
         (near_ref, 2 * slot + which * rows, rows),
         (mine_ref, 2 * slot + which * rows, rows),
     ):
@@ -187,29 +195,29 @@
         at += size
     window = pl.ds(pl.multiple_of(target * PER_GROUP, PER_GROUP), MIDS)
     write(0, mid_scratch[window, :])
+    before = pl.ds(pl.multiple_of(jnp.maximum(target - 1, 0) * BLK, BLK), BLK)
+    tail = tails_ref[which * BLK : (which + 1) * BLK, :]
+    write(prev_at, jnp.where(target == 0, tail, source[before, :]))
+
+
+def fill_coarse(geometry, width, coarse_ref, which, write):
+    _, _, slot, reach = geometry
     wide = coarse_ref[...].astype(F32).reshape(reach, 2, slot, HEAD_DIM)[:, which]
     wide = wide.reshape(reach * slot, HEAD_DIM)
     if width > reach * slot:
         wide = jnp.concatenate([wide, jnp.zeros((width - reach * slot, HEAD_DIM), F32)])
     write(MIDS, wide.astype(BF16))
-    before = pl.ds(pl.multiple_of(jnp.maximum(target - 1, 0) * BLK, BLK), BLK)
-    write(MIDS + width, source[before, :])
-
-    @pl.when(target == 0)
-    def _():
-        write(MIDS + width, tails_ref[which * BLK : (which + 1) * BLK, :])
 
 
 def pack_kernel(geometry, info_ref, *refs):
     sources, (_, out_ref, mid_scratch) = refs[:-3], refs[-3:]
-    _, _, slot, reach = geometry
     for which in range(2):
-        columns = slice(which * HEAD_DIM, (which + 1) * HEAD_DIM)
+        columns = head_columns(which)
 
         def write(at, value):
             out_ref[at : at + value.shape[0], columns] = value
 
-        fill_summaries(geometry, info_ref[0], reach * slot, sources, mid_scratch, which, write)
+        fill_late(geometry, info_ref[0], MIDS, sources, mid_scratch, which, write)
 
 
 def whole_in_vmem(count):
@@ -222,8 +230,7 @@
 
 
 def pack(info, shared, after, geometry):
-    _, _, slot, reach = geometry
-    rows = MIDS + reach * slot + BLK
+    rows = MIDS + BLK
     return pl.pallas_call(
         functools.partial(pack_kernel, geometry),
         in_specs=[pl.BlockSpec(memory_space=pltpu.SMEM)]
@@ -329,28 +336,28 @@
         def write(at, value):
             everything[at : at + value.shape[0], :HEAD_DIM] = value
 
-        fill_summaries(geometry, target, width, sources, mid_scratch, which, write)
+        fill_late(geometry, target, MIDS + width, sources, mid_scratch, which, write)
+        fill_coarse(geometry, width, sources[-1], which, write)
         own = pl.ds(pl.multiple_of(target * BLK, BLK), BLK)
         write(own_at, sources[which][own, :])
     scratch[1][:, HEAD_DIM:] = jnp.ones((own_at + BLK, HEAD_DIM), BF16)
     fill_bias(geometry, target, info_ref[1], width, scratch[2])
 
 
-def fill_shipped(geometry, width, info_ref, target, early_ref, late_ref, scratch):
-    _, _, slot, reach = geometry
-    used = MIDS + reach * slot
+def fill_shipped(geometry, width, info_ref, target, early_ref, late_ref, coarse_ref, scratch):
     own_at = MIDS + width + BLK
     for which in range(2):
         everything = scratch[which]
         columns = head_columns(which)
-        everything[:used, :HEAD_DIM] = late_ref[:used, columns]
-        if width > reach * slot:
-            everything[used : MIDS + width, :HEAD_DIM] = jnp.zeros(
-                (MIDS + width - used, HEAD_DIM), BF16
-            )
-        everything[MIDS + width : own_at, :HEAD_DIM] = late_ref[used:, columns]
+
+        def write(at, value):
+            everything[at : at + value.shape[0], :HEAD_DIM] = value
+
+        write(0, late_ref[:MIDS, columns])
+        fill_coarse(geometry, width, coarse_ref, which, write)
+        write(MIDS + width, late_ref[MIDS:, columns])
         at = early_ref.shape[1] - (2 - which) * HEAD_DIM
-        everything[own_at:, :HEAD_DIM] = early_ref[:, at : at + HEAD_DIM]
+        write(own_at, early_ref[:, at : at + HEAD_DIM])
     scratch[1][:, HEAD_DIM:] = jnp.ones((own_at + BLK, HEAD_DIM), BF16)
     fill_bias(geometry, target, info_ref[1], width, scratch[2])
 
@@ -366,15 +373,15 @@
 
 def finish_kernel(flip, geometry, width, heads, info_ref, q_ref, *rest):
     sources, rest = rest[:SHARED], rest[SHARED:]
-    early_ref, late_ref, _, output, mid_scratch = rest[:5]
-    rest = rest[2:]
+    early_ref, late_ref, coarse_ref, _, output, mid_scratch = rest[:6]
+    rest = rest[3:]
     ours, theirs = rest[3:6], rest[6:9]
     scores, weights, results, sent = rest[9:]
     member = info_ref[2]
     copies = []
 
     fill_local(geometry, width, info_ref, info_ref[0], sources, mid_scratch, ours)
-    fill_shipped(geometry, width, info_ref, info_ref[0], early_ref, late_ref, theirs)
+    fill_shipped(geometry, width, info_ref, info_ref[0], early_ref, late_ref, coarse_ref, theirs)
 
     def emit(job, owner):
         def put(first, group, half, mixed):
@@ -459,12 +466,12 @@
     )
 
 
-def finish(info, queries, shared, early, late, after, flip, heads, geometry, out_columns):
+def finish(info, queries, shared, shipped, after, flip, heads, geometry, out_columns):
     kernel = functools.partial(finish_kernel, flip)
     groups = heads // max(1, heads // 2)
     return attend_call(
         kernel,
-        (info, queries, *shared, early, late, after),
+        (info, queries, *shared, *shipped, after),
         2,
         heads,
         geometry,
@@ -521,34 +528,21 @@
     member = lax.axis_index("head")
     last_blocks = MIDB + 1 - 2 * block_count
     slot = round_up(block_count, 8)
-    rows = block_count * PER_GROUP
-    late_rows = last_blocks * PER_GROUP
     away = members // 2
 
     def info(flip):
         return jnp.stack([member ^ flip, device, member]).astype(jnp.int32)
 
-    early, keys, values, mine, tails = pool(
-        info(away), queries, keys, values, mid_pool, coarse_pool, block_count, slot
+    early, keys, values, mine, third, tails = pool(
+        info(away), queries, keys, values, mid_pool, coarse_pool, block_count, last_blocks, slot
     )
     near = cyclic(mine, "seq", 1)
     early = exchange(early, "head", away)
-    ends = [2 * slot + (i + 1) * rows - late_rows for i in range(2)]
-    passing = select(
-        [
-            (0, 2 * slot, 2 * rows),
-            *[(1, end, late_rows) for end in ends],
-            (0, 0, 2 * slot),
-            (1, 0, 2 * slot),
-        ],
-        mine,
-        near,
-    )
-    far = cyclic(passing, "seq", 2)
+    far = cyclic(mine, "seq", 2)
+    third = cyclic(third, "seq", 3)
     tails = cyclic(tails, "seq", 1)
     (queries,) = load(queries)
-    summaries = 2 * rows + 2 * late_rows
-    coarse = select([(0, summaries, 4 * slot), (1, summaries, 4 * slot)], passing, far)
+    coarse = select([(i, 0, 2 * slot) for i in range(4)], mine, near, far, third)
     reach = 4
     while reach < length:
         arriving = cyclic(coarse, "seq", reach)
@@ -556,11 +550,12 @@
         coarse = select([(0, 0, size), (1, 0, size)], coarse, arriving)
         reach *= 2
     geometry = (block_count, last_blocks, slot, reach)
-    shared = (keys, values, tails, near, far, mine, coarse)
-
-    late = pack(info(away), shared, coarse, geometry)
-    after = late
+    late = pack(info(away), (keys, values, tails, near, far, third, mine), far, geometry)
     late = exchange(late, "head", away)
+    shipped = (early, late, exchange(coarse, "head", away))
+
+    shared = (keys, values, tails, near, far, third, mine, coarse)
+    after = coarse
     arrived = []
     for flip in sent_flips(members):
         after = attend(info(flip), queries, shared, after, heads_here, geometry)
@@ -569,8 +564,7 @@
         info(0),
         queries,
         shared,
-        early,
-        late,
+        shipped,
         after,
         away,
         heads_here,

time: 46.6 us -> 52.4 us (1.12)
  starting transfers between devices: 8.56 us -> 16.2 us
  waiting for transfers between devices: 18.3 us -> 16.2 us
    ppermute x4 -> x5, waiting for transfers between devices: 12 us -> 1.28 us  [cyclic(): lax.ppermute(array, axis, [(i, (i + by) % size) for i in range(size)])]
    ppermute x4 -> x5, waiting for transfers between devices: 6.38 us -> 14.9 us  [exchange(): return lax.ppermute(array, axis, [(i, i ^ flip) for i in range(size)])]
    ppermute x4 -> x5, starting transfers between devices: 4.78 us -> 10.9 us  [cyclic(): lax.ppermute(array, axis, [(i, (i + by) % size) for i in range(size)])]
    ppermute x4 -> x5, starting transfers between devices: 3.78 us -> 5.3 us  [exchange(): return lax.ppermute(array, axis, [(i, i ^ flip) for i in range(size)])]
  transfers between devices with their start and end apart: 8 -> 10, of which waited for: 4 -> 3; matrix products, arithmetic and copies ran while one was open for 0% -> 0% of each run, Pallas kernels for 34% -> 31%
where the time goes in v5:
time: 52.4 us; the launch traced here: 52.3 us
  Pallas kernels  19.5 us (37%)
  starting transfers between devices  16.2 us (31%)
  waiting for transfers between devices  16.2 us (31%)
    ppermute x5, waiting for transfers between devices, exchange(): return lax.ppermute(array, axis, [(i, i ^ flip) for i in range(size)])  14.9 us
    pallas_call x3, Pallas kernels, attend_call(): pl.pallas_call(functools.partial(kernel, geometry, width, heads), in_spec...  13.8 us
    ppermute x5, starting transfers between devices, cyclic(): lax.ppermute(array, axis, [(i, (i + by) % size) for i in range(size)])  10.9 us
    ppermute x5, starting transfers between devices, exchange(): return lax.ppermute(array, axis, [(i, i ^ flip) for i in range(size)])  5.3 us
    pallas_call x1, Pallas kernels, pool(): pl.pallas_call(functools.partial(pool_kernel, block_count, last_blocks, s...  2 us
    pallas_call x1, Pallas kernels, load(): pl.pallas_call(load_kernel, in_specs=[pl.BlockSpec(memory_space=pltpu.HBM...  1.6 us
    pallas_call x1, Pallas kernels, place(): pl.pallas_call(functools.partial(place_kernel, spots, columns), in_specs=...  1.53 us
    ppermute x5, waiting for transfers between devices, cyclic(): lax.ppermute(array, axis, [(i, (i + by) % size) for i in range(size)])  1.28 us
  transfers between devices with their start and end apart: 10, of which 3 were waited for; matrix products, arithmetic and copies ran while one was open for 0% of the time, Pallas kernels for 31%

profile of v5, /device:TPU:0, one launch (start us, length us, event | category | flops | bytes accessed | tf_op | source)
XLA Modules:
  0.0 52.3 jit_solution(17102886257310486853)
XLA Ops:
  0.0 0.1 add_add_fusion.2.info_ref
  0.1 2.0 %pool.1 = (bf16[256,1280]{1,0:T(8,128)(2,1)S(1)}, bf16[1024,128]{1,0:T(8,128)(2,1)S(1)}, bf16[1024,128]{1,0:T(8,128)(2,1)S(1)}, bf16[272,128]{1,0:T(8,128)(2,1)S...) custom-call(s32[3]{0:T(128)S(1)} %add_add_fusion.2.info_ref, bf16[1024,1024]{1,0:T(8,128)(2,1)} %queries_hbm.1, ...), custom_call_target="tpu_custom_call" | custom-call | flops 20971520 | bytes 786432 | tf_op jit(solution)/shard_map/pool/pallas_call | solution.py:115
  2.1 3.1 %collective-permute-start.2 = (bf16[272,128]{1,0:T(8,128)(2,1)S(1)}, bf16[272,128]{1,0:T(8,128)(2,1)S(1)}, u32[]{:S(2)}, u32[]{:S(2)}) collective-permute-start(bf16[272,128]{1,0:T(8,128)(2,1)S(1)} %get-tuple-element.14.refs_0_.rest_6_.refs_6_), channel_id=1, source_target_pairs={{0,8},{4,12},{8,16},{12,20},{16,24},{20,28},{24,0},{28,4},{1,9},{5... | collective-permute-start | bytes 208904 | tf_op jit(solution)/shard_map/ppermute | solution.py:36
  5.2 1.5 %collective-permute-start.1 = (bf16[272,128]{1,0:T(8,128)(2,1)S(1)}, bf16[272,128]{1,0:T(8,128)(2,1)S(1)}, u32[]{:S(2)}, u32[]{:S(2)}) collective-permute-start(bf16[272,128]{1,0:T(8,128)(2,1)S(1)} %get-tuple-element.14.refs_0_.rest_6_.refs_6_), channel_id=1, source_target_pairs={{0,4},{4,8},{8,12},{12,16},{16,20},{20,24},{24,28},{28,0},{1,5},{5... | collective-permute-start | bytes 208904 | tf_op jit(solution)/shard_map/ppermute | solution.py:36
  6.7 2.6 %collective-permute-start.3 = (bf16[80,128]{1,0:T(8,128)(2,1)S(1)}, bf16[80,128]{1,0:T(8,128)(2,1)S(1)}, u32[]{:S(2)}, u32[]{:S(2)}) collective-permute-start(bf16[80,128]{1,0:T(8,128)(2,1)S(1)} %get-tuple-element.15), channel_id=1, source_target_pairs={{0,12},{4,16},{8,20},{12,24},{16,28},{20,0},{24,4},{28,8},{1,13},{... | collective-permute-start | bytes 61448 | tf_op jit(solution)/shard_map/ppermute | solution.py:36
  9.2 1.5 %collective-permute-start = (bf16[512,128]{1,0:T(8,128)(2,1)S(1)}, bf16[512,128]{1,0:T(8,128)(2,1)S(1)}, u32[]{:S(2)}, u32[]{:S(2)}) collective-permute-start(bf16[512,128]{1,0:T(8,128)(2,1)S(1)} %get-tuple-element.13), channel_id=1, source_target_pairs={{0,4},{4,8},{8,12},{12,16},{16,20},{20,24},{24,28},{28,0},{1,5},{5... | collective-permute-start | bytes 393224 | tf_op jit(solution)/shard_map/ppermute | solution.py:36
  10.7 1.5 %collective-permute-start.7 = (bf16[256,1280]{1,0:T(8,128)(2,1)S(1)}, bf16[256,1280]{1,0:T(8,128)(2,1)S(1)}, u32[]{:S(2)}, u32[]{:S(2)}) collective-permute-start(bf16[256,1280]{1,0:T(8,128)(2,1)S(1)} %get-tuple-element.16), channel_id=1, source_target_pairs={{0,2},{1,3},{2,0},{3,1},{4,6},{5,7},{6,4},{7,5},{8,10},{9,11},{10,... | collective-permute-start | bytes 1966088 | tf_op jit(solution)/shard_map/ppermute | solution.py:45
  12.3 0.1 add_add_fusion.3.info_ref
  12.3 0.5 collective-permute-done.3.refs_3_.rest_5_.refs_5_
  12.8 0.0 collective-permute-done.2.refs_2_.rest_4_.refs_4_.refs_7_
  12.8 0.0 collective-permute-done.1.refs_1_.rest_3_.refs_3_
  12.8 2.2 %collective-permute-start.4 = (bf16[64,128]{1,0:T(8,128)(2,1)S(1)}, bf16[64,128]{1,0:T(8,128)(2,1)S(1)}, u32[]{:S(2)}, u32[]{:S(2)}) collective-permute-start(bf16[64,128]{1,0:T(8,128)(2,1)S(1)} %select.2.refs_0_), channel_id=1, source_target_pairs={{0,16},{4,20},{8,24},{12,28},{16,0},{20,4},{24,8},{28,12},{1,17},{... | collective-permute-start | bytes 49160 | tf_op jit(solution)/shard_map/ppermute | solution.py:36
  15.0 0.1 add_add_fusion.1.info_ref
  15.1 1.6 %load.1.q_ref = bf16[1024,1024]{1,0:T(8,128)(2,1)S(1)} custom-call(bf16[1024,1024]{1,0:T(8,128)(2,1)} %queries_hbm.1), custom_call_target="tpu_custom_call" | custom-call | flops 2097152 | bytes 4194304 | tf_op jit(solution)/shard_map/load/pallas_call | solution.py:165
  16.7 0.8 %collective-permute-done.4.refs_1_ = bf16[64,128]{1,0:T(8,128)(2,1)S(1)} collective-permute-done((bf16[64,128]{1,0:T(8,128)(2,1)S(1)}, bf16[64,128]{1,0:T(8,128)(2,1)S(1)}, u32[]{:S(2)}, u32[]{:S(2)}) %collective-permute-start.4) | collective-permute-done | bytes 16416 | tf_op jit(solution)/shard_map/ppermute | solution.py:36
  17.5 0.0 collective-permute-done.rest_2_.refs_2_
  17.5 0.6 %pack.1 = bf16[512,256]{1,0:T(8,128)(2,1)S(1)} custom-call(s32[3]{0:T(128)S(1)} %add_add_fusion.2.info_ref, bf16[1024,128]{1,0:T(8,128)(2,1)S(1)} %get-tuple-element.11.rest_0_.refs_0_, bf16[1024,128]{1,0:T(8,128)(2,1)S(1)} %get-tuple-element.12.rest_1_.refs_1_, bf16[512,128]{1,0:T(8,128)(2,1)S(1)} %collective-permute-done.rest_2_.refs_2_, ...), custom_call_target="tpu_custom_call" | custom-call | flops 65536 | bytes 524288 | tf_op jit(solution)/shard_map/pack/pallas_call | solution.py:234
  18.1 1.6 %collective-permute-start.8 = (bf16[512,256]{1,0:T(8,128)(2,1)S(1)}, bf16[512,256]{1,0:T(8,128)(2,1)S(1)}, u32[]{:S(2)}, u32[]{:S(2)}) collective-permute-start(bf16[512,256]{1,0:T(8,128)(2,1)S(1)} %pack.1), channel_id=1, source_target_pairs={{0,2},{1,3},{2,0},{3,1},{4,6},{5,7},{6,4},{7,5},{8,10},{9,11},{10,... | collective-permute-start | bytes 786440 | tf_op jit(solution)/shard_map/ppermute | solution.py:45
  19.7 3.4 %attend.3.rest_8_ = bf16[256,1024]{1,0:T(8,128)(2,1)S(1)} custom-call(s32[3]{0:T(128)S(1)} %add_add_fusion.1.info_ref, bf16[1024,1024]{1,0:T(8,128)(2,1)S(1)} %load.1.q_ref, bf16[1024,128]{1,0:T(8,128)(2,1)S(1)} %get-tuple-element.11.rest_0_.refs_0_, bf16[1024,128]{1,0:T(8,128)(2,1)S(1)} %get-tuple-element.12.rest_1_.refs_1_, ...), custom_call_target="tpu_custom_call" | custom-call | flops 1409286144 | bytes 2097152 | tf_op jit(solution)/shard_map/attend/pallas_call | solution.py:428
  23.1 3.4 %attend.4.rest_11_ = bf16[256,1024]{1,0:T(8,128)(2,1)S(1)} custom-call(s32[3]{0:T(128)S(1)} %add_add_fusion.3.info_ref, bf16[1024,1024]{1,0:T(8,128)(2,1)S(1)} %load.1.q_ref, bf16[1024,128]{1,0:T(8,128)(2,1)S(1)} %get-tuple-element.11.rest_0_.refs_0_, bf16[1024,128]{1,0:T(8,128)(2,1)S(1)} %get-tuple-element.12.rest_1_.refs_1_, ...), custom_call_target="tpu_custom_call" | custom-call | flops 1409286144 | bytes 2097152 | tf_op jit(solution)/shard_map/attend/pallas_call | solution.py:428
  26.4 0.1 collective-permute-start.6
  26.5 0.6 %collective-permute-start.5 = (bf16[256,1024]{1,0:T(8,128)(2,1)S(1)}, bf16[256,1024]{1,0:T(8,128)(2,1)S(1)}, u32[]{:S(2)}, u32[]{:S(2)}) collective-permute-start(bf16[256,1024]{1,0:T(8,128)(2,1)S(1)} %attend.3.rest_8_), channel_id=1, source_target_pairs={{0,3},{1,2},{2,1},{3,0},{4,7},{5,6},{6,5},{7,4},{8,11},{9,10},{10,... | collective-permute-start | bytes 1572872 | tf_op jit(solution)/shard_map/ppermute | solution.py:45
  27.1 1.5 %collective-permute-start.9 = (bf16[128,128]{1,0:T(8,128)(2,1)S(1)}, bf16[128,128]{1,0:T(8,128)(2,1)S(1)}, u32[]{:S(2)}, u32[]{:S(2)}) collective-permute-start(bf16[128,128]{1,0:T(8,128)(2,1)S(1)} %select.3.rest_7_.rest_8_), channel_id=1, source_target_pairs={{0,2},{1,3},{2,0},{3,1},{4,6},{5,7},{6,4},{7,5},{8,10},{9,11},{10,... | collective-permute-start | bytes 98312 | tf_op jit(solution)/shard_map/ppermute | solution.py:45
  28.7 0.1 add_add_fusion.info_ref
  28.7 14.9 %collective-permute-done.9.rest_10_ = bf16[128,128]{1,0:T(8,128)(2,1)S(1)} collective-permute-done((bf16[128,128]{1,0:T(8,128)(2,1)S(1)}, bf16[128,128]{1,0:T(8,128)(2,1)S(1)}, u32[]{:S(2)}, u32[]{:S(2)}) %collective-permute-start.9) | collective-permute-done | bytes 32800 | tf_op jit(solution)/shard_map/ppermute | solution.py:45
  43.6 0.0 collective-permute-done.8.rest_9_
  43.6 0.0 collective-permute-done.7.rest_8_
  43.6 7.0 %attend.5.refs_2_ = bf16[256,4096]{1,0:T(8,128)(2,1)} custom-call(s32[3]{0:T(128)S(1)} %add_add_fusion.info_ref, bf16[1024,1024]{1,0:T(8,128)(2,1)S(1)} %load.1.q_ref, bf16[1024,128]{1,0:T(8,128)(2,1)S(1)} %get-tuple-element.11.rest_0_.refs_0_, bf16[1024,128]{1,0:T(8,128)(2,1)S(1)} %get-tuple-element.12.rest_1_.refs_1_, ...), custom_call_target="tpu_custom_call" | custom-call | flops 2818572288 | bytes 2097152 | tf_op jit(solution)/shard_map/attend/pallas_call | solution.py:428
  50.7 0.0 collective-permute-done.6.refs_1_
  50.7 0.0 collective-permute-done.5.refs_0_
  50.7 1.5 %place.1 = bf16[256,4096]{1,0:T(8,128)(2,1)} custom-call(s32[3]{0:T(128)S(1)} %add_add_fusion.info_ref, bf16[256,1024]{1,0:T(8,128)(2,1)S(1)} %collective-permute-done.5.refs_0_, bf16[256,1024]{1,0:T(8,128)(2,1)S(1)} %collective-permute-done.6.refs_1_, bf16[256,4096]{1,0:T(8,128)(2,1)} %attend.5.refs_2_), custom_call_target="tpu_custom_call", output_to_operand_aliasing={{}: (3, {})} | custom-call | flops 524288 | bytes 2097152 | tf_op jit(solution)/shard_map/place/pallas_call | solution.py:503
  (2 shorter events, 0.0 us)
Async XLA Ops:
  2.1 10.7 %collective-permute-start.2 = (bf16[272,128]{1,0:T(8,128)(2,1)S(1)}, bf16[272,128]{1,0:T(8,128)(2,1)S(1)}, u32[]{:S(2)}, u32[]{:S(2)}) collective-permute-start(bf16[272,128]{1,0:T(8,128)(2,1)S(1)} %get-tuple-element.14.refs_0_.rest_6_.refs_6_), channel_id=1, source_target_pairs={{0,8},{4,12},{8,16},{12,20},{16,24},{20,28},{24,0},{28,4},{1,9},{5... | collective-permute-start | bytes 208904 | tf_op jit(solution)/shard_map/ppermute | solution.py:36
  5.2 7.6 %collective-permute-start.1 = (bf16[272,128]{1,0:T(8,128)(2,1)S(1)}, bf16[272,128]{1,0:T(8,128)(2,1)S(1)}, u32[]{:S(2)}, u32[]{:S(2)}) collective-permute-start(bf16[272,128]{1,0:T(8,128)(2,1)S(1)} %get-tuple-element.14.refs_0_.rest_6_.refs_6_), channel_id=1, source_target_pairs={{0,4},{4,8},{8,12},{12,16},{16,20},{20,24},{24,28},{28,0},{1,5},{5... | collective-permute-start | bytes 208904 | tf_op jit(solution)/shard_map/ppermute | solution.py:36
  6.7 6.1 %collective-permute-start.3 = (bf16[80,128]{1,0:T(8,128)(2,1)S(1)}, bf16[80,128]{1,0:T(8,128)(2,1)S(1)}, u32[]{:S(2)}, u32[]{:S(2)}) collective-permute-start(bf16[80,128]{1,0:T(8,128)(2,1)S(1)} %get-tuple-element.15), channel_id=1, source_target_pairs={{0,12},{4,16},{8,20},{12,24},{16,28},{20,0},{24,4},{28,8},{1,13},{... | collective-permute-start | bytes 61448 | tf_op jit(solution)/shard_map/ppermute | solution.py:36
  9.2 8.3 %collective-permute-start = (bf16[512,128]{1,0:T(8,128)(2,1)S(1)}, bf16[512,128]{1,0:T(8,128)(2,1)S(1)}, u32[]{:S(2)}, u32[]{:S(2)}) collective-permute-start(bf16[512,128]{1,0:T(8,128)(2,1)S(1)} %get-tuple-element.13), channel_id=1, source_target_pairs={{0,4},{4,8},{8,12},{12,16},{16,20},{20,24},{24,28},{28,0},{1,5},{5... | collective-permute-start | bytes 393224 | tf_op jit(solution)/shard_map/ppermute | solution.py:36
  10.7 32.9 %collective-permute-start.7 = (bf16[256,1280]{1,0:T(8,128)(2,1)S(1)}, bf16[256,1280]{1,0:T(8,128)(2,1)S(1)}, u32[]{:S(2)}, u32[]{:S(2)}) collective-permute-start(bf16[256,1280]{1,0:T(8,128)(2,1)S(1)} %get-tuple-element.16), channel_id=1, source_target_pairs={{0,2},{1,3},{2,0},{3,1},{4,6},{5,7},{6,4},{7,5},{8,10},{9,11},{10,... | collective-permute-start | bytes 1966088 | tf_op jit(solution)/shard_map/ppermute | solution.py:45
  12.8 4.7 %collective-permute-start.4 = (bf16[64,128]{1,0:T(8,128)(2,1)S(1)}, bf16[64,128]{1,0:T(8,128)(2,1)S(1)}, u32[]{:S(2)}, u32[]{:S(2)}) collective-permute-start(bf16[64,128]{1,0:T(8,128)(2,1)S(1)} %select.2.refs_0_), channel_id=1, source_target_pairs={{0,16},{4,20},{8,24},{12,28},{16,0},{20,4},{24,8},{28,12},{1,17},{... | collective-permute-start | bytes 49160 | tf_op jit(solution)/shard_map/ppermute | solution.py:36
  18.1 25.5 %collective-permute-start.8 = (bf16[512,256]{1,0:T(8,128)(2,1)S(1)}, bf16[512,256]{1,0:T(8,128)(2,1)S(1)}, u32[]{:S(2)}, u32[]{:S(2)}) collective-permute-start(bf16[512,256]{1,0:T(8,128)(2,1)S(1)} %pack.1), channel_id=1, source_target_pairs={{0,2},{1,3},{2,0},{3,1},{4,6},{5,7},{6,4},{7,5},{8,10},{9,11},{10,... | collective-permute-start | bytes 786440 | tf_op jit(solution)/shard_map/ppermute | solution.py:45
  26.4 24.3 %collective-permute-start.6 = (bf16[256,1024]{1,0:T(8,128)(2,1)S(1)}, bf16[256,1024]{1,0:T(8,128)(2,1)S(1)}, u32[]{:S(2)}, u32[]{:S(2)}) collective-permute-start(bf16[256,1024]{1,0:T(8,128)(2,1)S(1)} %attend.4.rest_11_), channel_id=1, source_target_pairs={{0,1},{1,0},{2,3},{3,2},{4,5},{5,4},{6,7},{7,6},{8,9},{9,8},{10,11... | collective-permute-start | bytes 1572872 | tf_op jit(solution)/shard_map/ppermute | solution.py:45
  26.5 24.2 %collective-permute-start.5 = (bf16[256,1024]{1,0:T(8,128)(2,1)S(1)}, bf16[256,1024]{1,0:T(8,128)(2,1)S(1)}, u32[]{:S(2)}, u32[]{:S(2)}) collective-permute-start(bf16[256,1024]{1,0:T(8,128)(2,1)S(1)} %attend.3.rest_8_), channel_id=1, source_target_pairs={{0,3},{1,2},{2,1},{3,0},{4,7},{5,6},{6,5},{7,4},{8,11},{9,10},{10,... | collective-permute-start | bytes 1572872 | tf_op jit(solution)/shard_map/ppermute | solution.py:45
  27.1 16.5 %collective-permute-start.9 = (bf16[128,128]{1,0:T(8,128)(2,1)S(1)}, bf16[128,128]{1,0:T(8,128)(2,1)S(1)}, u32[]{:S(2)}, u32[]{:S(2)}) collective-permute-start(bf16[128,128]{1,0:T(8,128)(2,1)S(1)} %select.3.rest_7_.rest_8_), channel_id=1, source_target_pairs={{0,2},{1,3},{2,0},{3,1},{4,6},{5,7},{6,4},{7,5},{8,10},{9,11},{10,... | collective-permute-start | bytes 98312 | tf_op jit(solution)/shard_map/ppermute | solution.py:45

commit v6 on v5

--- a/solution.py
+++ b/solution.py
@@ -45,10 +45,14 @@
     return lax.ppermute(array, axis, [(i, i ^ flip) for i in range(size)])
 
 
-def pool_kernel(block_count, last_blocks, slot, info_ref, queries_hbm, keys_hbm, values_hbm, mid_hbm, coarse_hbm,
+def block_of(flip):
+    return lax.axis_index("head") ^ flip
+
+
+def pool_kernel(block_count, last_blocks, slot, flip, queries_hbm, keys_hbm, values_hbm, mid_hbm, coarse_hbm,
                 early_out, keys_ref, values_ref, near_out, third_out, tails_out, mid_ref, coarse_ref,
                 arrived):
-    wanted = pl.ds(pl.multiple_of(info_ref[0] * BLK, BLK), BLK)
+    wanted = pl.ds(pl.multiple_of(block_of(flip) * BLK, BLK), BLK)
     moves = [
         (mid_hbm, mid_ref),
         (coarse_hbm, coarse_ref),
@@ -103,7 +107,7 @@
         copy.wait()
 
 
-def pool(info, queries, keys, values, mid_pool, coarse_pool, block_count, last_blocks, slot):
+def pool(flip, queries, keys, values, mid_pool, coarse_pool, block_count, last_blocks, slot):
     shapes = (
         (BLK, queries.shape[1] + 2 * HEAD_DIM),
         keys.shape,
@@ -113,9 +117,8 @@
         (2 * BLK, HEAD_DIM),
     )
     return pl.pallas_call(
-        functools.partial(pool_kernel, block_count, last_blocks, slot),
-        in_specs=[pl.BlockSpec(memory_space=pltpu.SMEM)]
-        + [pl.BlockSpec(memory_space=pltpu.HBM)] * 5,
+        functools.partial(pool_kernel, block_count, last_blocks, slot, flip),
+        in_specs=[pl.BlockSpec(memory_space=pltpu.HBM)] * 5,
         out_specs=[pl.BlockSpec(memory_space=pltpu.VMEM) for _ in shapes],
         out_shape=[jax.ShapeDtypeStruct(shape, BF16) for shape in shapes],
         scratch_shapes=[
@@ -128,7 +131,7 @@
         ),
         compiler_params=pltpu.CompilerParams(vmem_limit_bytes=VMEM_LIMIT),
         name="pool",
-    )(info, *off_chip(queries, keys, values, mid_pool, coarse_pool))
+    )(*off_chip(queries, keys, values, mid_pool, coarse_pool))
 
 
 def select_kernel(parts, *refs):
@@ -209,7 +212,7 @@
     write(MIDS, wide.astype(BF16))
 
 
-def pack_kernel(geometry, info_ref, *refs):
+def pack_kernel(geometry, flip, *refs):
     sources, (_, out_ref, mid_scratch) = refs[:-3], refs[-3:]
     for which in range(2):
         columns = head_columns(which)
@@ -217,7 +220,7 @@
         def write(at, value):
             out_ref[at : at + value.shape[0], columns] = value
 
-        fill_late(geometry, info_ref[0], MIDS, sources, mid_scratch, which, write)
+        fill_late(geometry, block_of(flip), MIDS, sources, mid_scratch, which, write)
 
 
 def whole_in_vmem(count):
@@ -229,12 +232,11 @@
     return (3 * block_count + last_blocks) * PER_GROUP
 
 
-def pack(info, shared, after, geometry):
+def pack(flip, shared, after, geometry):
     rows = MIDS + BLK
     return pl.pallas_call(
-        functools.partial(pack_kernel, geometry),
-        in_specs=[pl.BlockSpec(memory_space=pltpu.SMEM)]
-        + whole_in_vmem(len(shared))
+        functools.partial(pack_kernel, geometry, flip),
+        in_specs=whole_in_vmem(len(shared))
         + [pl.BlockSpec(memory_space=pl.ANY)],
         out_specs=pl.BlockSpec(memory_space=pltpu.VMEM),
         out_shape=jax.ShapeDtypeStruct((rows, 2 * HEAD_DIM), BF16),
@@ -244,7 +246,7 @@
             flops=rows * HEAD_DIM, bytes_accessed=8 * rows * HEAD_DIM, transcendentals=0
         ),
         name="pack",
-    )(info, *shared, after)
+    )(*shared, after)
 
 
 def fill_bias(geometry, target, device, width, bias):
@@ -328,7 +330,7 @@
         ]
 
 
-def fill_local(geometry, width, info_ref, target, sources, mid_scratch, scratch):
+def fill_local(geometry, width, target, sources, mid_scratch, scratch):
     own_at = MIDS + width + BLK
     for which in range(2):
         everything = scratch[which]
@@ -341,10 +343,10 @@
         own = pl.ds(pl.multiple_of(target * BLK, BLK), BLK)
         write(own_at, sources[which][own, :])
     scratch[1][:, HEAD_DIM:] = jnp.ones((own_at + BLK, HEAD_DIM), BF16)
-    fill_bias(geometry, target, info_ref[1], width, scratch[2])
-
-
-def fill_shipped(geometry, width, info_ref, target, early_ref, late_ref, coarse_ref, scratch):
+    fill_bias(geometry, target, lax.axis_index("seq"), width, scratch[2])
+
+
+def fill_shipped(geometry, width, target, early_ref, late_ref, coarse_ref, scratch):
     own_at = MIDS + width + BLK
     for which in range(2):
         everything = scratch[which]
@@ -359,29 +361,29 @@
         at = early_ref.shape[1] - (2 - which) * HEAD_DIM
         write(own_at, early_ref[:, at : at + HEAD_DIM])
     scratch[1][:, HEAD_DIM:] = jnp.ones((own_at + BLK, HEAD_DIM), BF16)
-    fill_bias(geometry, target, info_ref[1], width, scratch[2])
-
-
-def attend_kernel(geometry, width, heads, info_ref, q_ref, *rest):
+    fill_bias(geometry, target, lax.axis_index("seq"), width, scratch[2])
+
+
+def attend_kernel(flip, geometry, width, heads, q_ref, *rest):
     sources, (_, out_ref, mid_scratch) = rest[:SHARED], rest[SHARED : SHARED + 3]
     scratch, (scores, weights) = rest[SHARED + 3 : SHARED + 6], rest[SHARED + 6 :]
-    target = info_ref[0]
-    fill_local(geometry, width, info_ref, target, sources, mid_scratch, scratch)
+    target = block_of(flip)
+    fill_local(geometry, width, target, sources, mid_scratch, scratch)
     emit = functools.partial(store, out_ref, 0)
     attend_jobs([(q_ref, target * BLK, *scratch, emit)], heads, scores, weights)
 
 
-def finish_kernel(flip, geometry, width, heads, info_ref, q_ref, *rest):
+def finish_kernel(flip, geometry, width, heads, q_ref, *rest):
     sources, rest = rest[:SHARED], rest[SHARED:]
     early_ref, late_ref, coarse_ref, _, output, mid_scratch = rest[:6]
     rest = rest[3:]
     ours, theirs = rest[3:6], rest[6:9]
     scores, weights, results, sent = rest[9:]
-    member = info_ref[2]
+    member = block_of(0)
     copies = []
 
-    fill_local(geometry, width, info_ref, info_ref[0], sources, mid_scratch, ours)
-    fill_shipped(geometry, width, info_ref, info_ref[0], early_ref, late_ref, coarse_ref, theirs)
+    fill_local(geometry, width, member, sources, mid_scratch, ours)
+    fill_shipped(geometry, width, member, early_ref, late_ref, coarse_ref, theirs)
 
     def emit(job, owner):
         def put(first, group, half, mixed):
@@ -402,7 +404,7 @@
 
     attend_jobs(
         [
-            (q_ref, info_ref[0] * BLK, *ours, emit(0, member)),
+            (q_ref, member * BLK, *ours, emit(0, member)),
             (early_ref, 0, *theirs, emit(1, member ^ flip)),
         ],
         heads,
@@ -427,8 +429,7 @@
     unit_rows = max(1, heads // 2) * HALF
     return pl.pallas_call(
         functools.partial(kernel, geometry, width, heads),
-        in_specs=[pl.BlockSpec(memory_space=pltpu.SMEM)]
-        + whole_in_vmem(len(operands) - 2)
+        in_specs=whole_in_vmem(len(operands) - 1)
         + [pl.BlockSpec(memory_space=pl.ANY)],
         out_specs=out_spec,
         scratch_shapes=[pltpu.VMEM((mid_rows(geometry), HEAD_DIM), BF16)]
@@ -453,10 +454,10 @@
     return round_up(geometry[3] * geometry[2], LANES)
 
 
-def attend(info, queries, shared, after, heads, geometry):
+def attend(flip, queries, shared, after, heads, geometry):
     return attend_call(
-        attend_kernel,
-        (info, queries, *shared, after),
+        functools.partial(attend_kernel, flip),
+        (queries, *shared, after),
         1,
         heads,
         geometry,
@@ -466,12 +467,12 @@
     )
 
 
-def finish(info, queries, shared, shipped, after, flip, heads, geometry, out_columns):
+def finish(queries, shared, shipped, after, flip, heads, geometry, out_columns):
     kernel = functools.partial(finish_kernel, flip)
     groups = heads // max(1, heads // 2)
     return attend_call(
         kernel,
-        (info, queries, *shared, *shipped, after),
+        (queries, *shared, *shipped, after),
         2,
         heads,
         geometry,
@@ -484,11 +485,11 @@
     )
 
 
-def place_kernel(spots, columns, info_ref, *refs):
+def place_kernel(spots, columns, *refs):
     pieces, out_ref, done = refs[: len(spots)], refs[-2], refs[-1]
     copies = []
     for i, (flip, at) in enumerate(spots):
-        start = pl.multiple_of((info_ref[2] ^ flip) * columns + at, HEAD_DIM)
+        start = pl.multiple_of(block_of(flip) * columns + at, HEAD_DIM)
         target = out_ref.at[:, pl.ds(start, pieces[i].shape[1])]
         copies.append(pltpu.make_async_copy(pieces[i], target, done.at[i]))
     for copy in copies:
@@ -497,22 +498,21 @@
         copy.wait()
 
 
-def place(info, output, pieces, columns):
+def place(output, pieces, columns):
     spots = [(flip, start * HEAD_DIM) for flip, start, _ in pieces]
     size = sum(piece.size for _, _, piece in pieces)
     return pl.pallas_call(
         functools.partial(place_kernel, spots, columns),
-        in_specs=[pl.BlockSpec(memory_space=pltpu.SMEM)]
-        + [pl.BlockSpec(memory_space=pltpu.VMEM)] * len(pieces)
+        in_specs=[pl.BlockSpec(memory_space=pltpu.VMEM)] * len(pieces)
         + [pl.BlockSpec(memory_space=pl.ANY)],
         out_specs=pl.BlockSpec(memory_space=pl.ANY),
         scratch_shapes=[pltpu.SemaphoreType.DMA((len(pieces),))],
         out_shape=jax.ShapeDtypeStruct(output.shape, output.dtype),
-        input_output_aliases={len(pieces) + 1: 0},
+        input_output_aliases={len(pieces): 0},
         compiler_params=pltpu.CompilerParams(vmem_limit_bytes=VMEM_LIMIT),
         cost_estimate=pl.CostEstimate(flops=size, bytes_accessed=4 * size, transcendentals=0),
         name="place",
-    )(info, *[piece for _, _, piece in pieces], output)
+    )(*[piece for _, _, piece in pieces], output)
 
 
 def body(queries, keys, values, mid_pool, coarse_pool):
@@ -524,17 +524,12 @@
     assert keys.shape[1] == HEAD_DIM and block_count == members
     assert block_count <= MIDB and members & (members - 1) == 0
     assert 2 * block_count <= MIDB < 3 * block_count
-    device = lax.axis_index("seq")
-    member = lax.axis_index("head")
     last_blocks = MIDB + 1 - 2 * block_count
     slot = round_up(block_count, 8)
     away = members // 2
 
-    def info(flip):
-        return jnp.stack([member ^ flip, device, member]).astype(jnp.int32)
-
     early, keys, values, mine, third, tails = pool(
-        info(away), queries, keys, values, mid_pool, coarse_pool, block_count, last_blocks, slot
+        away, queries, keys, values, mid_pool, coarse_pool, block_count, last_blocks, slot
     )
     near = cyclic(mine, "seq", 1)
     early = exchange(early, "head", away)
@@ -550,7 +545,7 @@
         coarse = select([(0, 0, size), (1, 0, size)], coarse, arriving)
         reach *= 2
     geometry = (block_count, last_blocks, slot, reach)
-    late = pack(info(away), (keys, values, tails, near, far, third, mine), far, geometry)
+    late = pack(away, (keys, values, tails, near, far, third, mine), far, geometry)
     late = exchange(late, "head", away)
     shipped = (early, late, exchange(coarse, "head", away))
 
@@ -558,20 +553,10 @@
     after = coarse
     arrived = []
     for flip in sent_flips(members):
-        after = attend(info(flip), queries, shared, after, heads_here, geometry)
+        after = attend(flip, queries, shared, after, heads_here, geometry)
         arrived.append((flip, 0, exchange(after, "head", flip)))
-    output = finish(
-        info(0),
-        queries,
-        shared,
-        shipped,
-        after,
-        away,
-        heads_here,
-        geometry,
-        members * columns,
-    )
-    return place(info(0), output, arrived, columns)
+    output = finish(queries, shared, shipped, after, away, heads_here, geometry, members * columns)
+    return place(output, arrived, columns)
 
 
 def sent_flips(members):

time: 52.4 us -> 49.6 us (0.947)
  Pallas kernels: 19.5 us -> 16.2 us
  waiting for transfers between devices: 16.2 us -> 17.9 us
  starting transfers between devices: 16.2 us -> 15.2 us
    ppermute x5, waiting for transfers between devices: 1.28 us -> 5.07 us  [cyclic(): lax.ppermute(array, axis, [(i, (i + by) % size) for i in range(size)])]
    ppermute x5, waiting for transfers between devices: 14.9 us -> 12.9 us  [exchange(): return lax.ppermute(array, axis, [(i, i ^ flip) for i in range(size)])]
    pallas_call x3, Pallas kernels: 13.8 us -> 12.1 us  [attend_call(): pl.pallas_call(functools.partial(kernel, geometry, width, heads), in_spec...]
    ppermute x5, starting transfers between devices: 10.9 us -> 9.86 us  [cyclic(): lax.ppermute(array, axis, [(i, (i + by) % size) for i in range(size)])]
    pallas_call x1, Pallas kernels: 2 us -> 1.46 us  [pool(): pl.pallas_call(functools.partial(pool_kernel, block_count, last_blocks, s...]
    pallas_call x1, Pallas kernels: 0.61 us -> 0.07 us  [pack(): pl.pallas_call(functools.partial(pack_kernel, geometry, flip), in_specs=w...]
    pallas_call x1, Pallas kernels: 1.53 us -> 1 us  [place(): pl.pallas_call(functools.partial(place_kernel, spots, columns), in_specs=...]
  transfers between devices with their start and end apart: 10 -> 10, of which waited for: 3 -> 3; matrix products, arithmetic and copies ran while one was open for 0% -> 0% of each run, Pallas kernels for 31% -> 28%
where the time goes in v6:
time: 49.6 us; the launch traced here: 49.5 us
  waiting for transfers between devices  17.9 us (36%)
  Pallas kernels  16.2 us (33%)
  starting transfers between devices  15.2 us (31%)
    ppermute x5, waiting for transfers between devices, exchange(): return lax.ppermute(array, axis, [(i, i ^ flip) for i in range(size)])  12.9 us
    pallas_call x3, Pallas kernels, attend_call(): pl.pallas_call(functools.partial(kernel, geometry, width, heads), in_spec...  12.1 us
    ppermute x5, starting transfers between devices, cyclic(): lax.ppermute(array, axis, [(i, (i + by) % size) for i in range(size)])  9.86 us
    ppermute x5, starting transfers between devices, exchange(): return lax.ppermute(array, axis, [(i, i ^ flip) for i in range(size)])  5.38 us
    ppermute x5, waiting for transfers between devices, cyclic(): lax.ppermute(array, axis, [(i, (i + by) % size) for i in range(size)])  5.07 us
    pallas_call x1, Pallas kernels, load(): pl.pallas_call(load_kernel, in_specs=[pl.BlockSpec(memory_space=pltpu.HBM...  1.6 us
    pallas_call x1, Pallas kernels, pool(): pl.pallas_call(functools.partial(pool_kernel, block_count, last_blocks, s...  1.46 us
    pallas_call x1, Pallas kernels, place(): pl.pallas_call(functools.partial(place_kernel, spots, columns), in_specs=...  1 us
  transfers between devices with their start and end apart: 10, of which 3 were waited for; matrix products, arithmetic and copies ran while one was open for 0% of the time, Pallas kernels for 28%

profile of v6, /device:TPU:0, one launch (start us, length us, event | category | flops | bytes accessed | tf_op | source)
XLA Modules:
  0.0 49.5 jit_solution(1693388857478550736)
XLA Ops:
  0.0 1.5 %pool.1 = (bf16[256,1280]{1,0:T(8,128)(2,1)S(1)}, bf16[1024,128]{1,0:T(8,128)(2,1)S(1)}, bf16[1024,128]{1,0:T(8,128)(2,1)S(1)}, bf16[272,128]{1,0:T(8,128)(2,1)S...) custom-call(bf16[1024,1024]{1,0:T(8,128)(2,1)} %queries_hbm.1, bf16[1024,128]{1,0:T(8,128)(2,1)} %keys_hbm.1, ...), custom_call_target="tpu_custom_call" | custom-call | flops 20971520 | bytes 786432 | tf_op jit(solution)/shard_map/pool/pallas_call | solution.py:119
  1.5 3.0 %collective-permute-start = (bf16[512,128]{1,0:T(8,128)(2,1)S(1)}, bf16[512,128]{1,0:T(8,128)(2,1)S(1)}, u32[]{:S(2)}, u32[]{:S(2)}) collective-permute-start(bf16[512,128]{1,0:T(8,128)(2,1)S(1)} %get-tuple-element.13), channel_id=1, source_target_pairs={{0,4},{4,8},{8,12},{12,16},{16,20},{20,24},{24,28},{28,0},{1,5},{5... | collective-permute-start | bytes 393224 | tf_op jit(solution)/shard_map/ppermute | solution.py:36
  4.5 1.5 %collective-permute-start.7 = (bf16[256,1280]{1,0:T(8,128)(2,1)S(1)}, bf16[256,1280]{1,0:T(8,128)(2,1)S(1)}, u32[]{:S(2)}, u32[]{:S(2)}) collective-permute-start(bf16[256,1280]{1,0:T(8,128)(2,1)S(1)} %get-tuple-element.16), channel_id=1, source_target_pairs={{0,2},{1,3},{2,0},{3,1},{4,6},{5,7},{6,4},{7,5},{8,10},{9,11},{10,... | collective-permute-start | bytes 1966088 | tf_op jit(solution)/shard_map/ppermute | solution.py:45
  6.0 1.6 %collective-permute-start.2 = (bf16[272,128]{1,0:T(8,128)(2,1)S(1)}, bf16[272,128]{1,0:T(8,128)(2,1)S(1)}, u32[]{:S(2)}, u32[]{:S(2)}) collective-permute-start(bf16[272,128]{1,0:T(8,128)(2,1)S(1)} %get-tuple-element.14.refs_0_.rest_6_.refs_6_), channel_id=1, source_target_pairs={{0,8},{4,12},{8,16},{12,20},{16,24},{20,28},{24,0},{28,4},{1,9},{5... | collective-permute-start | bytes 208904 | tf_op jit(solution)/shard_map/ppermute | solution.py:36
  7.6 1.5 %collective-permute-start.1 = (bf16[272,128]{1,0:T(8,128)(2,1)S(1)}, bf16[272,128]{1,0:T(8,128)(2,1)S(1)}, u32[]{:S(2)}, u32[]{:S(2)}) collective-permute-start(bf16[272,128]{1,0:T(8,128)(2,1)S(1)} %get-tuple-element.14.refs_0_.rest_6_.refs_6_), channel_id=1, source_target_pairs={{0,4},{4,8},{8,12},{12,16},{16,20},{20,24},{24,28},{28,0},{1,5},{5... | collective-permute-start | bytes 208904 | tf_op jit(solution)/shard_map/ppermute | solution.py:36
  9.1 2.5 %collective-permute-start.3 = (bf16[80,128]{1,0:T(8,128)(2,1)S(1)}, bf16[80,128]{1,0:T(8,128)(2,1)S(1)}, u32[]{:S(2)}, u32[]{:S(2)}) collective-permute-start(bf16[80,128]{1,0:T(8,128)(2,1)S(1)} %get-tuple-element.15), channel_id=1, source_target_pairs={{0,12},{4,16},{8,20},{12,24},{16,28},{20,0},{24,4},{28,8},{1,13},{... | collective-permute-start | bytes 61448 | tf_op jit(solution)/shard_map/ppermute | solution.py:36
  11.6 3.2 %collective-permute-done.3.refs_3_.rest_5_.refs_5_ = bf16[80,128]{1,0:T(8,128)(2,1)S(1)} collective-permute-done((bf16[80,128]{1,0:T(8,128)(2,1)S(1)}, bf16[80,128]{1,0:T(8,128)(2,1)S(1)}, u32[]{:S(2)}, u32[]{:S(2)}) %collective-permute-start.3) | collective-permute-done | bytes 20512 | tf_op jit(solution)/shard_map/ppermute | solution.py:36
  14.8 0.0 collective-permute-done.2.refs_2_.rest_4_.refs_4_.refs_7_
  14.8 0.0 collective-permute-done.1.refs_1_.rest_3_.refs_3_
  14.8 1.2 %collective-permute-start.4 = (bf16[64,128]{1,0:T(8,128)(2,1)S(1)}, bf16[64,128]{1,0:T(8,128)(2,1)S(1)}, u32[]{:S(2)}, u32[]{:S(2)}) collective-permute-start(bf16[64,128]{1,0:T(8,128)(2,1)S(1)} %select.2.refs_0_), channel_id=1, source_target_pairs={{0,16},{4,20},{8,24},{12,28},{16,0},{20,4},{24,8},{28,12},{1,17},{... | collective-permute-start | bytes 49160 | tf_op jit(solution)/shard_map/ppermute | solution.py:36
  16.0 1.6 %load.1.q_ref = bf16[1024,1024]{1,0:T(8,128)(2,1)S(1)} custom-call(bf16[1024,1024]{1,0:T(8,128)(2,1)} %queries_hbm.1), custom_call_target="tpu_custom_call" | custom-call | flops 2097152 | bytes 4194304 | tf_op jit(solution)/shard_map/load/pallas_call | solution.py:168
  17.6 1.9 %collective-permute-done.4.refs_1_ = bf16[64,128]{1,0:T(8,128)(2,1)S(1)} collective-permute-done((bf16[64,128]{1,0:T(8,128)(2,1)S(1)}, bf16[64,128]{1,0:T(8,128)(2,1)S(1)}, u32[]{:S(2)}, u32[]{:S(2)}) %collective-permute-start.4) | collective-permute-done | bytes 16416 | tf_op jit(solution)/shard_map/ppermute | solution.py:36
  19.5 0.0 collective-permute-done.rest_2_.refs_2_
  19.5 0.1 pack.1
  19.6 1.7 %collective-permute-start.8 = (bf16[512,256]{1,0:T(8,128)(2,1)S(1)}, bf16[512,256]{1,0:T(8,128)(2,1)S(1)}, u32[]{:S(2)}, u32[]{:S(2)}) collective-permute-start(bf16[512,256]{1,0:T(8,128)(2,1)S(1)} %pack.1), channel_id=1, source_target_pairs={{0,2},{1,3},{2,0},{3,1},{4,6},{5,7},{6,4},{7,5},{8,10},{9,11},{10,... | collective-permute-start | bytes 786440 | tf_op jit(solution)/shard_map/ppermute | solution.py:45
  21.3 2.8 %attend.3.rest_8_ = bf16[256,1024]{1,0:T(8,128)(2,1)S(1)} custom-call(bf16[1024,1024]{1,0:T(8,128)(2,1)S(1)} %load.1.q_ref, bf16[1024,128]{1,0:T(8,128)(2,1)S(1)} %get-tuple-element.11.rest_0_.refs_0_, bf16[1024,128]{1,0:T(8,128)(2,1)S(1)} %get-tuple-element.12.rest_1_.refs_1_, bf16[512,128]{1,0:T(8,128)(2,1)S(1)} %collective-permute-done.rest_2_.refs_2_, ...), custom_call_target="tpu_custom_call" | custom-call | flops 1409286144 | bytes 2097152 | tf_op jit(solution)/shard_map/attend/pallas_call | solution.py:430
  24.1 2.8 %attend.4.rest_11_ = bf16[256,1024]{1,0:T(8,128)(2,1)S(1)} custom-call(bf16[1024,1024]{1,0:T(8,128)(2,1)S(1)} %load.1.q_ref, bf16[1024,128]{1,0:T(8,128)(2,1)S(1)} %get-tuple-element.11.rest_0_.refs_0_, bf16[1024,128]{1,0:T(8,128)(2,1)S(1)} %get-tuple-element.12.rest_1_.refs_1_, bf16[512,128]{1,0:T(8,128)(2,1)S(1)} %collective-permute-done.rest_2_.refs_2_, ...), custom_call_target="tpu_custom_call" | custom-call | flops 1409286144 | bytes 2097152 | tf_op jit(solution)/shard_map/attend/pallas_call | solution.py:430
  26.9 0.1 collective-permute-start.6
  27.0 0.5 %collective-permute-start.5 = (bf16[256,1024]{1,0:T(8,128)(2,1)S(1)}, bf16[256,1024]{1,0:T(8,128)(2,1)S(1)}, u32[]{:S(2)}, u32[]{:S(2)}) collective-permute-start(bf16[256,1024]{1,0:T(8,128)(2,1)S(1)} %attend.3.rest_8_), channel_id=1, source_target_pairs={{0,3},{1,2},{2,1},{3,0},{4,7},{5,6},{6,5},{7,4},{8,11},{9,10},{10,... | collective-permute-start | bytes 1572872 | tf_op jit(solution)/shard_map/ppermute | solution.py:45
  27.5 1.6 %collective-permute-start.9 = (bf16[128,128]{1,0:T(8,128)(2,1)S(1)}, bf16[128,128]{1,0:T(8,128)(2,1)S(1)}, u32[]{:S(2)}, u32[]{:S(2)}) collective-permute-start(bf16[128,128]{1,0:T(8,128)(2,1)S(1)} %select.3.rest_7_.rest_8_), channel_id=1, source_target_pairs={{0,2},{1,3},{2,0},{3,1},{4,6},{5,7},{6,4},{7,5},{8,10},{9,11},{10,... | collective-permute-start | bytes 98312 | tf_op jit(solution)/shard_map/ppermute | solution.py:45
  29.1 12.9 %collective-permute-done.9.rest_10_ = bf16[128,128]{1,0:T(8,128)(2,1)S(1)} collective-permute-done((bf16[128,128]{1,0:T(8,128)(2,1)S(1)}, bf16[128,128]{1,0:T(8,128)(2,1)S(1)}, u32[]{:S(2)}, u32[]{:S(2)}) %collective-permute-start.9) | collective-permute-done | bytes 32800 | tf_op jit(solution)/shard_map/ppermute | solution.py:45
  42.0 0.0 collective-permute-done.8.rest_9_
  42.0 0.0 collective-permute-done.7.rest_8_
  42.0 6.5 %attend.5.refs_2_ = bf16[256,4096]{1,0:T(8,128)(2,1)} custom-call(bf16[1024,1024]{1,0:T(8,128)(2,1)S(1)} %load.1.q_ref, bf16[1024,128]{1,0:T(8,128)(2,1)S(1)} %get-tuple-element.11.rest_0_.refs_0_, bf16[1024,128]{1,0:T(8,128)(2,1)S(1)} %get-tuple-element.12.rest_1_.refs_1_, bf16[512,128]{1,0:T(8,128)(2,1)S(1)} %collective-permute-done.rest_2_.refs_2_, ...), custom_call_target="tpu_custom_call" | custom-call | flops 2818572288 | bytes 2097152 | tf_op jit(solution)/shard_map/attend/pallas_call | solution.py:430
  48.5 0.0 collective-permute-done.6.refs_1_
  48.5 0.0 collective-permute-done.5.refs_0_
  48.5 1.0 %place.1 = bf16[256,4096]{1,0:T(8,128)(2,1)} custom-call(bf16[256,1024]{1,0:T(8,128)(2,1)S(1)} %collective-permute-done.5.refs_0_, bf16[256,1024]{1,0:T(8,128)(2,1)S(1)} %collective-permute-done.6.refs_1_, bf16[256,4096]{1,0:T(8,128)(2,1)} %attend.5.refs_2_), custom_call_target="tpu_custom_call", output_to_operand_aliasing={{}: (2, {})} | custom-call | flops 524288 | bytes 2097152 | tf_op jit(solution)/shard_map/place/pallas_call | solution.py:504
  (2 shorter events, 0.0 us)
Async XLA Ops:
  1.5 18.1 %collective-permute-start = (bf16[512,128]{1,0:T(8,128)(2,1)S(1)}, bf16[512,128]{1,0:T(8,128)(2,1)S(1)}, u32[]{:S(2)}, u32[]{:S(2)}) collective-permute-start(bf16[512,128]{1,0:T(8,128)(2,1)S(1)} %get-tuple-element.13), channel_id=1, source_target_pairs={{0,4},{4,8},{8,12},{12,16},{16,20},{20,24},{24,28},{28,0},{1,5},{5... | collective-permute-start | bytes 393224 | tf_op jit(solution)/shard_map/ppermute | solution.py:36
  4.5 37.5 %collective-permute-start.7 = (bf16[256,1280]{1,0:T(8,128)(2,1)S(1)}, bf16[256,1280]{1,0:T(8,128)(2,1)S(1)}, u32[]{:S(2)}, u32[]{:S(2)}) collective-permute-start(bf16[256,1280]{1,0:T(8,128)(2,1)S(1)} %get-tuple-element.16), channel_id=1, source_target_pairs={{0,2},{1,3},{2,0},{3,1},{4,6},{5,7},{6,4},{7,5},{8,10},{9,11},{10,... | collective-permute-start | bytes 1966088 | tf_op jit(solution)/shard_map/ppermute | solution.py:45
  6.0 8.8 %collective-permute-start.2 = (bf16[272,128]{1,0:T(8,128)(2,1)S(1)}, bf16[272,128]{1,0:T(8,128)(2,1)S(1)}, u32[]{:S(2)}, u32[]{:S(2)}) collective-permute-start(bf16[272,128]{1,0:T(8,128)(2,1)S(1)} %get-tuple-element.14.refs_0_.rest_6_.refs_6_), channel_id=1, source_target_pairs={{0,8},{4,12},{8,16},{12,20},{16,24},{20,28},{24,0},{28,4},{1,9},{5... | collective-permute-start | bytes 208904 | tf_op jit(solution)/shard_map/ppermute | solution.py:36
  7.6 7.2 %collective-permute-start.1 = (bf16[272,128]{1,0:T(8,128)(2,1)S(1)}, bf16[272,128]{1,0:T(8,128)(2,1)S(1)}, u32[]{:S(2)}, u32[]{:S(2)}) collective-permute-start(bf16[272,128]{1,0:T(8,128)(2,1)S(1)} %get-tuple-element.14.refs_0_.rest_6_.refs_6_), channel_id=1, source_target_pairs={{0,4},{4,8},{8,12},{12,16},{16,20},{20,24},{24,28},{28,0},{1,5},{5... | collective-permute-start | bytes 208904 | tf_op jit(solution)/shard_map/ppermute | solution.py:36
  9.1 5.7 %collective-permute-start.3 = (bf16[80,128]{1,0:T(8,128)(2,1)S(1)}, bf16[80,128]{1,0:T(8,128)(2,1)S(1)}, u32[]{:S(2)}, u32[]{:S(2)}) collective-permute-start(bf16[80,128]{1,0:T(8,128)(2,1)S(1)} %get-tuple-element.15), channel_id=1, source_target_pairs={{0,12},{4,16},{8,20},{12,24},{16,28},{20,0},{24,4},{28,8},{1,13},{... | collective-permute-start | bytes 61448 | tf_op jit(solution)/shard_map/ppermute | solution.py:36
  14.8 4.7 %collective-permute-start.4 = (bf16[64,128]{1,0:T(8,128)(2,1)S(1)}, bf16[64,128]{1,0:T(8,128)(2,1)S(1)}, u32[]{:S(2)}, u32[]{:S(2)}) collective-permute-start(bf16[64,128]{1,0:T(8,128)(2,1)S(1)} %select.2.refs_0_), channel_id=1, source_target_pairs={{0,16},{4,20},{8,24},{12,28},{16,0},{20,4},{24,8},{28,12},{1,17},{... | collective-permute-start | bytes 49160 | tf_op jit(solution)/shard_map/ppermute | solution.py:36
  19.6 22.4 %collective-permute-start.8 = (bf16[512,256]{1,0:T(8,128)(2,1)S(1)}, bf16[512,256]{1,0:T(8,128)(2,1)S(1)}, u32[]{:S(2)}, u32[]{:S(2)}) collective-permute-start(bf16[512,256]{1,0:T(8,128)(2,1)S(1)} %pack.1), channel_id=1, source_target_pairs={{0,2},{1,3},{2,0},{3,1},{4,6},{5,7},{6,4},{7,5},{8,10},{9,11},{10,... | collective-permute-start | bytes 786440 | tf_op jit(solution)/shard_map/ppermute | solution.py:45
  26.9 21.6 %collective-permute-start.6 = (bf16[256,1024]{1,0:T(8,128)(2,1)S(1)}, bf16[256,1024]{1,0:T(8,128)(2,1)S(1)}, u32[]{:S(2)}, u32[]{:S(2)}) collective-permute-start(bf16[256,1024]{1,0:T(8,128)(2,1)S(1)} %attend.4.rest_11_), channel_id=1, source_target_pairs={{0,1},{1,0},{2,3},{3,2},{4,5},{5,4},{6,7},{7,6},{8,9},{9,8},{10,11... | collective-permute-start | bytes 1572872 | tf_op jit(solution)/shard_map/ppermute | solution.py:45
  27.0 21.5 %collective-permute-start.5 = (bf16[256,1024]{1,0:T(8,128)(2,1)S(1)}, bf16[256,1024]{1,0:T(8,128)(2,1)S(1)}, u32[]{:S(2)}, u32[]{:S(2)}) collective-permute-start(bf16[256,1024]{1,0:T(8,128)(2,1)S(1)} %attend.3.rest_8_), channel_id=1, source_target_pairs={{0,3},{1,2},{2,1},{3,0},{4,7},{5,6},{6,5},{7,4},{8,11},{9,10},{10,... | collective-permute-start | bytes 1572872 | tf_op jit(solution)/shard_map/ppermute | solution.py:45
  27.5 14.5 %collective-permute-start.9 = (bf16[128,128]{1,0:T(8,128)(2,1)S(1)}, bf16[128,128]{1,0:T(8,128)(2,1)S(1)}, u32[]{:S(2)}, u32[]{:S(2)}) collective-permute-start(bf16[128,128]{1,0:T(8,128)(2,1)S(1)} %select.3.rest_7_.rest_8_), channel_id=1, source_target_pairs={{0,2},{1,3},{2,0},{3,1},{4,6},{5,7},{6,4},{7,5},{8,10},{9,11},{10,... | collective-permute-start | bytes 98312 | tf_op jit(solution)/shard_map/ppermute | solution.py:45

commit v7 on v6

--- a/solution.py
+++ b/solution.py
@@ -81,28 +81,31 @@
     owner = lax.broadcasted_iota(jnp.int32, (PER_GROUP, BLK), 1) // GROUP
     mine = owner == lax.broadcasted_iota(jnp.int32, (PER_GROUP, BLK), 0)
     mid_weights = jnp.where(mine, jnp.broadcast_to(tiled, (PER_GROUP, BLK)), 0.0)
-    coarse_weights = coarse_ref[...].astype(F32)
+    coarse_weights = jnp.broadcast_to(coarse_ref[...].astype(F32), (slot, BLK))
     row = lax.broadcasted_iota(jnp.int32, (slot, BLK), 0)
+    total = jnp.zeros((slot, HEAD_DIM), F32)
     for which, source in enumerate((keys_ref, values_ref)):
-        total = jnp.zeros((slot, HEAD_DIM), F32)
         for block in range(block_count):
             here = source[block * BLK : (block + 1) * BLK, :]
             weights = jnp.concatenate(
-                [mid_weights, jnp.where(row == block, jnp.broadcast_to(coarse_weights, (slot, BLK)), 0.0)]
+                [
+                    mid_weights,
+                    jnp.where(row == which * block_count + block, coarse_weights, 0.0),
+                ]
             ).astype(BF16)
             pooled = jnp.dot(weights, here, preferred_element_type=F32)
             total = total + pooled[PER_GROUP:]
-            start = 2 * slot + which * rows + block * PER_GROUP
+            start = slot + which * rows + block * PER_GROUP
             mids = pooled[:PER_GROUP].astype(BF16)
             near_out[start : start + PER_GROUP, :] = mids
             nth = block - (block_count - last_blocks)
             if nth >= 0:
-                start = 2 * slot + (which * last_blocks + nth) * PER_GROUP
+                start = slot + (which * last_blocks + nth) * PER_GROUP
                 third_out[start : start + PER_GROUP, :] = mids
-        near_out[which * slot : (which + 1) * slot, :] = total.astype(BF16)
-        third_out[which * slot : (which + 1) * slot, :] = total.astype(BF16)
         edge = (block_count - 1) * BLK
         tails_out[which * BLK : (which + 1) * BLK, :] = source[edge : edge + BLK, :]
+    near_out[:slot, :] = total.astype(BF16)
+    third_out[:slot, :] = total.astype(BF16)
     for copy in copies[4:]:
         copy.wait()
 
@@ -112,8 +115,8 @@
         (BLK, queries.shape[1] + 2 * HEAD_DIM),
         keys.shape,
         values.shape,
-        (2 * slot + 2 * block_count * PER_GROUP, HEAD_DIM),
-        (2 * slot + 2 * last_blocks * PER_GROUP, HEAD_DIM),
+        (slot + 2 * block_count * PER_GROUP, HEAD_DIM),
+        (slot + 2 * last_blocks * PER_GROUP, HEAD_DIM),
         (2 * BLK, HEAD_DIM),
     )
     return pl.pallas_call(
@@ -189,10 +192,10 @@
     late = last_blocks * PER_GROUP
     at = 0
     for ref, start, size in (
-        (third_ref, 2 * slot + which * late, late),
-        (far_ref, 2 * slot + which * rows, rows),
-        (near_ref, 2 * slot + which * rows, rows),
-        (mine_ref, 2 * slot + which * rows, rows),
+        (third_ref, slot + which * late, late),
+        (far_ref, slot + which * rows, rows),
+        (near_ref, slot + which * rows, rows),
+        (mine_ref, slot + which * rows, rows),
     ):
         mid_scratch[at : at + size, :] = ref[start : start + size, :]
         at += size
@@ -204,9 +207,10 @@
 
 
 def fill_coarse(geometry, width, coarse_ref, which, write):
-    _, _, slot, reach = geometry
-    wide = coarse_ref[...].astype(F32).reshape(reach, 2, slot, HEAD_DIM)[:, which]
-    wide = wide.reshape(reach * slot, HEAD_DIM)
+    block_count, _, slot, reach = geometry
+    wide = coarse_ref[...].astype(F32)
+    if which:
+        wide = pltpu.roll(wide, reach * slot - block_count, 0)
     if width > reach * slot:
         wide = jnp.concatenate([wide, jnp.zeros((width - reach * slot, HEAD_DIM), F32)])
     write(MIDS, wide.astype(BF16))
@@ -525,7 +529,7 @@
     assert block_count <= MIDB and members & (members - 1) == 0
     assert 2 * block_count <= MIDB < 3 * block_count
     last_blocks = MIDB + 1 - 2 * block_count
-    slot = round_up(block_count, 8)
+    slot = round_up(2 * block_count, 8)
     away = members // 2
 
     early, keys, values, mine, third, tails = pool(
@@ -537,7 +541,7 @@
     third = cyclic(third, "seq", 3)
     tails = cyclic(tails, "seq", 1)
     (queries,) = load(queries)
-    coarse = select([(i, 0, 2 * slot) for i in range(4)], mine, near, far, third)
+    coarse = select([(i, 0, slot) for i in range(4)], mine, near, far, third)
     reach = 4
     while reach < length:
         arriving = cyclic(coarse, "seq", reach)

time: 49.6 us -> 49.1 us (0.990)
  waiting for transfers between devices: 17.9 us -> 17.4 us
where the time goes in v7:
time: 49.1 us; the launch traced here: 48.9 us
  waiting for transfers between devices  17.4 us (35%)
  Pallas kernels  16.2 us (33%)
  starting transfers between devices  15.2 us (31%)
    ppermute x5, waiting for transfers between devices, exchange(): return lax.ppermute(array, axis, [(i, i ^ flip) for i in range(size)])  12.5 us
    pallas_call x3, Pallas kernels, attend_call(): pl.pallas_call(functools.partial(kernel, geometry, width, heads), in_spec...  12.1 us
    ppermute x5, starting transfers between devices, cyclic(): lax.ppermute(array, axis, [(i, (i + by) % size) for i in range(size)])  9.88 us
    ppermute x5, starting transfers between devices, exchange(): return lax.ppermute(array, axis, [(i, i ^ flip) for i in range(size)])  5.32 us
    ppermute x5, waiting for transfers between devices, cyclic(): lax.ppermute(array, axis, [(i, (i + by) % size) for i in range(size)])  4.92 us
    pallas_call x1, Pallas kernels, load(): pl.pallas_call(load_kernel, in_specs=[pl.BlockSpec(memory_space=pltpu.HBM...  1.6 us
    pallas_call x1, Pallas kernels, pool(): pl.pallas_call(functools.partial(pool_kernel, block_count, last_blocks, s...  1.46 us
    pallas_call x1, Pallas kernels, place(): pl.pallas_call(functools.partial(place_kernel, spots, columns), in_specs=...  1 us
  transfers between devices with their start and end apart: 10, of which 3 were waited for; matrix products, arithmetic and copies ran while one was open for 0% of the time, Pallas kernels for 28%

profile of v7, /device:TPU:0, one launch (start us, length us, event | category | flops | bytes accessed | tf_op | source)
XLA Modules:
  0.0 48.9 jit_solution(13823520400821289749)
XLA Ops:
  0.0 1.5 %pool.1 = (bf16[256,1280]{1,0:T(8,128)(2,1)S(1)}, bf16[1024,128]{1,0:T(8,128)(2,1)S(1)}, bf16[1024,128]{1,0:T(8,128)(2,1)S(1)}, bf16[264,128]{1,0:T(8,128)(2,1)S...) custom-call(bf16[1024,1024]{1,0:T(8,128)(2,1)} %queries_hbm.1, bf16[1024,128]{1,0:T(8,128)(2,1)} %keys_hbm.1, ...), custom_call_target="tpu_custom_call" | custom-call | flops 20971520 | bytes 786432 | tf_op jit(solution)/shard_map/pool/pallas_call | solution.py:122
  1.5 3.0 %collective-permute-start = (bf16[512,128]{1,0:T(8,128)(2,1)S(1)}, bf16[512,128]{1,0:T(8,128)(2,1)S(1)}, u32[]{:S(2)}, u32[]{:S(2)}) collective-permute-start(bf16[512,128]{1,0:T(8,128)(2,1)S(1)} %get-tuple-element.13), channel_id=1, source_target_pairs={{0,4},{4,8},{8,12},{12,16},{16,20},{20,24},{24,28},{28,0},{1,5},{5... | collective-permute-start | bytes 393224 | tf_op jit(solution)/shard_map/ppermute | solution.py:36
  4.5 1.5 %collective-permute-start.7 = (bf16[256,1280]{1,0:T(8,128)(2,1)S(1)}, bf16[256,1280]{1,0:T(8,128)(2,1)S(1)}, u32[]{:S(2)}, u32[]{:S(2)}) collective-permute-start(bf16[256,1280]{1,0:T(8,128)(2,1)S(1)} %get-tuple-element.16), channel_id=1, source_target_pairs={{0,2},{1,3},{2,0},{3,1},{4,6},{5,7},{6,4},{7,5},{8,10},{9,11},{10,... | collective-permute-start | bytes 1966088 | tf_op jit(solution)/shard_map/ppermute | solution.py:45
  6.0 1.6 %collective-permute-start.2 = (bf16[264,128]{1,0:T(8,128)(2,1)S(1)}, bf16[264,128]{1,0:T(8,128)(2,1)S(1)}, u32[]{:S(2)}, u32[]{:S(2)}) collective-permute-start(bf16[264,128]{1,0:T(8,128)(2,1)S(1)} %get-tuple-element.14.refs_0_.rest_6_.refs_6_), channel_id=1, source_target_pairs={{0,8},{4,12},{8,16},{12,20},{16,24},{20,28},{24,0},{28,4},{1,9},{5... | collective-permute-start | bytes 202760 | tf_op jit(solution)/shard_map/ppermute | solution.py:36
  7.6 1.5 %collective-permute-start.1 = (bf16[264,128]{1,0:T(8,128)(2,1)S(1)}, bf16[264,128]{1,0:T(8,128)(2,1)S(1)}, u32[]{:S(2)}, u32[]{:S(2)}) collective-permute-start(bf16[264,128]{1,0:T(8,128)(2,1)S(1)} %get-tuple-element.14.refs_0_.rest_6_.refs_6_), channel_id=1, source_target_pairs={{0,4},{4,8},{8,12},{12,16},{16,20},{20,24},{24,28},{28,0},{1,5},{5... | collective-permute-start | bytes 202760 | tf_op jit(solution)/shard_map/ppermute | solution.py:36
  9.1 2.5 %collective-permute-start.3 = (bf16[72,128]{1,0:T(8,128)(2,1)S(1)}, bf16[72,128]{1,0:T(8,128)(2,1)S(1)}, u32[]{:S(2)}, u32[]{:S(2)}) collective-permute-start(bf16[72,128]{1,0:T(8,128)(2,1)S(1)} %get-tuple-element.15), channel_id=1, source_target_pairs={{0,12},{4,16},{8,20},{12,24},{16,28},{20,0},{24,4},{28,8},{1,13},{... | collective-permute-start | bytes 55304 | tf_op jit(solution)/shard_map/ppermute | solution.py:36
  11.6 3.1 %collective-permute-done.3.refs_3_.rest_5_.refs_5_ = bf16[72,128]{1,0:T(8,128)(2,1)S(1)} collective-permute-done((bf16[72,128]{1,0:T(8,128)(2,1)S(1)}, bf16[72,128]{1,0:T(8,128)(2,1)S(1)}, u32[]{:S(2)}, u32[]{:S(2)}) %collective-permute-start.3) | collective-permute-done | bytes 18464 | tf_op jit(solution)/shard_map/ppermute | solution.py:36
  14.8 0.0 collective-permute-done.2.refs_2_.rest_4_.refs_4_.refs_7_
  14.8 0.0 collective-permute-done.1.refs_1_.rest_3_.refs_3_
  14.8 1.2 %collective-permute-start.4 = (bf16[32,128]{1,0:T(8,128)(2,1)S(1)}, bf16[32,128]{1,0:T(8,128)(2,1)S(1)}, u32[]{:S(2)}, u32[]{:S(2)}) collective-permute-start(bf16[32,128]{1,0:T(8,128)(2,1)S(1)} %select.2.refs_0_), channel_id=1, source_target_pairs={{0,16},{4,20},{8,24},{12,28},{16,0},{20,4},{24,8},{28,12},{1,17},{... | collective-permute-start | bytes 24584 | tf_op jit(solution)/shard_map/ppermute | solution.py:36
  16.0 1.6 %load.1.q_ref = bf16[1024,1024]{1,0:T(8,128)(2,1)S(1)} custom-call(bf16[1024,1024]{1,0:T(8,128)(2,1)} %queries_hbm.1), custom_call_target="tpu_custom_call" | custom-call | flops 2097152 | bytes 4194304 | tf_op jit(solution)/shard_map/load/pallas_call | solution.py:171
  17.6 1.8 %collective-permute-done.4.refs_1_ = bf16[32,128]{1,0:T(8,128)(2,1)S(1)} collective-permute-done((bf16[32,128]{1,0:T(8,128)(2,1)S(1)}, bf16[32,128]{1,0:T(8,128)(2,1)S(1)}, u32[]{:S(2)}, u32[]{:S(2)}) %collective-permute-start.4) | collective-permute-done | bytes 8224 | tf_op jit(solution)/shard_map/ppermute | solution.py:36
  19.4 0.0 collective-permute-done.rest_2_.refs_2_
  19.4 0.1 pack.1
  19.5 1.6 %collective-permute-start.8 = (bf16[512,256]{1,0:T(8,128)(2,1)S(1)}, bf16[512,256]{1,0:T(8,128)(2,1)S(1)}, u32[]{:S(2)}, u32[]{:S(2)}) collective-permute-start(bf16[512,256]{1,0:T(8,128)(2,1)S(1)} %pack.1), channel_id=1, source_target_pairs={{0,2},{1,3},{2,0},{3,1},{4,6},{5,7},{6,4},{7,5},{8,10},{9,11},{10,... | collective-permute-start | bytes 786440 | tf_op jit(solution)/shard_map/ppermute | solution.py:45
  21.1 2.8 %attend.3.rest_8_ = bf16[256,1024]{1,0:T(8,128)(2,1)S(1)} custom-call(bf16[1024,1024]{1,0:T(8,128)(2,1)S(1)} %load.1.q_ref, bf16[1024,128]{1,0:T(8,128)(2,1)S(1)} %get-tuple-element.11.rest_0_.refs_0_, bf16[1024,128]{1,0:T(8,128)(2,1)S(1)} %get-tuple-element.12.rest_1_.refs_1_, bf16[512,128]{1,0:T(8,128)(2,1)S(1)} %collective-permute-done.rest_2_.refs_2_, ...), custom_call_target="tpu_custom_call" | custom-call | flops 1409286144 | bytes 2097152 | tf_op jit(solution)/shard_map/attend/pallas_call | solution.py:434
  23.9 2.8 %attend.4.rest_11_ = bf16[256,1024]{1,0:T(8,128)(2,1)S(1)} custom-call(bf16[1024,1024]{1,0:T(8,128)(2,1)S(1)} %load.1.q_ref, bf16[1024,128]{1,0:T(8,128)(2,1)S(1)} %get-tuple-element.11.rest_0_.refs_0_, bf16[1024,128]{1,0:T(8,128)(2,1)S(1)} %get-tuple-element.12.rest_1_.refs_1_, bf16[512,128]{1,0:T(8,128)(2,1)S(1)} %collective-permute-done.rest_2_.refs_2_, ...), custom_call_target="tpu_custom_call" | custom-call | flops 1409286144 | bytes 2097152 | tf_op jit(solution)/shard_map/attend/pallas_call | solution.py:434
  26.7 0.1 collective-permute-start.6
  26.8 0.6 %collective-permute-start.5 = (bf16[256,1024]{1,0:T(8,128)(2,1)S(1)}, bf16[256,1024]{1,0:T(8,128)(2,1)S(1)}, u32[]{:S(2)}, u32[]{:S(2)}) collective-permute-start(bf16[256,1024]{1,0:T(8,128)(2,1)S(1)} %attend.3.rest_8_), channel_id=1, source_target_pairs={{0,3},{1,2},{2,1},{3,0},{4,7},{5,6},{6,5},{7,4},{8,11},{9,10},{10,... | collective-permute-start | bytes 1572872 | tf_op jit(solution)/shard_map/ppermute | solution.py:45
  27.4 1.5 %collective-permute-start.9 = (bf16[64,128]{1,0:T(8,128)(2,1)S(1)}, bf16[64,128]{1,0:T(8,128)(2,1)S(1)}, u32[]{:S(2)}, u32[]{:S(2)}) collective-permute-start(bf16[64,128]{1,0:T(8,128)(2,1)S(1)} %select.3.rest_7_.rest_8_), channel_id=1, source_target_pairs={{0,2},{1,3},{2,0},{3,1},{4,6},{5,7},{6,4},{7,5},{8,10},{9,11},{10,... | collective-permute-start | bytes 49160 | tf_op jit(solution)/shard_map/ppermute | solution.py:45
  28.9 12.5 %collective-permute-done.9.rest_10_ = bf16[64,128]{1,0:T(8,128)(2,1)S(1)} collective-permute-done((bf16[64,128]{1,0:T(8,128)(2,1)S(1)}, bf16[64,128]{1,0:T(8,128)(2,1)S(1)}, u32[]{:S(2)}, u32[]{:S(2)}) %collective-permute-start.9) | collective-permute-done | bytes 16416 | tf_op jit(solution)/shard_map/ppermute | solution.py:45
  41.4 0.0 collective-permute-done.8.rest_9_
  41.4 0.0 collective-permute-done.7.rest_8_
  41.4 6.5 %attend.5.refs_2_ = bf16[256,4096]{1,0:T(8,128)(2,1)} custom-call(bf16[1024,1024]{1,0:T(8,128)(2,1)S(1)} %load.1.q_ref, bf16[1024,128]{1,0:T(8,128)(2,1)S(1)} %get-tuple-element.11.rest_0_.refs_0_, bf16[1024,128]{1,0:T(8,128)(2,1)S(1)} %get-tuple-element.12.rest_1_.refs_1_, bf16[512,128]{1,0:T(8,128)(2,1)S(1)} %collective-permute-done.rest_2_.refs_2_, ...), custom_call_target="tpu_custom_call" | custom-call | flops 2818572288 | bytes 2097152 | tf_op jit(solution)/shard_map/attend/pallas_call | solution.py:434
  47.9 0.0 collective-permute-done.6.refs_1_
  47.9 0.0 collective-permute-done.5.refs_0_
  47.9 1.0 %place.1 = bf16[256,4096]{1,0:T(8,128)(2,1)} custom-call(bf16[256,1024]{1,0:T(8,128)(2,1)S(1)} %collective-permute-done.5.refs_0_, bf16[256,1024]{1,0:T(8,128)(2,1)S(1)} %collective-permute-done.6.refs_1_, bf16[256,4096]{1,0:T(8,128)(2,1)} %attend.5.refs_2_), custom_call_target="tpu_custom_call", output_to_operand_aliasing={{}: (2, {})} | custom-call | flops 524288 | bytes 2097152 | tf_op jit(solution)/shard_map/place/pallas_call | solution.py:508
  (2 shorter events, 0.0 us)
Async XLA Ops:
  1.5 17.9 %collective-permute-start = (bf16[512,128]{1,0:T(8,128)(2,1)S(1)}, bf16[512,128]{1,0:T(8,128)(2,1)S(1)}, u32[]{:S(2)}, u32[]{:S(2)}) collective-permute-start(bf16[512,128]{1,0:T(8,128)(2,1)S(1)} %get-tuple-element.13), channel_id=1, source_target_pairs={{0,4},{4,8},{8,12},{12,16},{16,20},{20,24},{24,28},{28,0},{1,5},{5... | collective-permute-start | bytes 393224 | tf_op jit(solution)/shard_map/ppermute | solution.py:36
  4.5 36.9 %collective-permute-start.7 = (bf16[256,1280]{1,0:T(8,128)(2,1)S(1)}, bf16[256,1280]{1,0:T(8,128)(2,1)S(1)}, u32[]{:S(2)}, u32[]{:S(2)}) collective-permute-start(bf16[256,1280]{1,0:T(8,128)(2,1)S(1)} %get-tuple-element.16), channel_id=1, source_target_pairs={{0,2},{1,3},{2,0},{3,1},{4,6},{5,7},{6,4},{7,5},{8,10},{9,11},{10,... | collective-permute-start | bytes 1966088 | tf_op jit(solution)/shard_map/ppermute | solution.py:45
  6.0 8.8 %collective-permute-start.2 = (bf16[264,128]{1,0:T(8,128)(2,1)S(1)}, bf16[264,128]{1,0:T(8,128)(2,1)S(1)}, u32[]{:S(2)}, u32[]{:S(2)}) collective-permute-start(bf16[264,128]{1,0:T(8,128)(2,1)S(1)} %get-tuple-element.14.refs_0_.rest_6_.refs_6_), channel_id=1, source_target_pairs={{0,8},{4,12},{8,16},{12,20},{16,24},{20,28},{24,0},{28,4},{1,9},{5... | collective-permute-start | bytes 202760 | tf_op jit(solution)/shard_map/ppermute | solution.py:36
  7.6 7.2 %collective-permute-start.1 = (bf16[264,128]{1,0:T(8,128)(2,1)S(1)}, bf16[264,128]{1,0:T(8,128)(2,1)S(1)}, u32[]{:S(2)}, u32[]{:S(2)}) collective-permute-start(bf16[264,128]{1,0:T(8,128)(2,1)S(1)} %get-tuple-element.14.refs_0_.rest_6_.refs_6_), channel_id=1, source_target_pairs={{0,4},{4,8},{8,12},{12,16},{16,20},{20,24},{24,28},{28,0},{1,5},{5... | collective-permute-start | bytes 202760 | tf_op jit(solution)/shard_map/ppermute | solution.py:36
  9.1 5.6 %collective-permute-start.3 = (bf16[72,128]{1,0:T(8,128)(2,1)S(1)}, bf16[72,128]{1,0:T(8,128)(2,1)S(1)}, u32[]{:S(2)}, u32[]{:S(2)}) collective-permute-start(bf16[72,128]{1,0:T(8,128)(2,1)S(1)} %get-tuple-element.15), channel_id=1, source_target_pairs={{0,12},{4,16},{8,20},{12,24},{16,28},{20,0},{24,4},{28,8},{1,13},{... | collective-permute-start | bytes 55304 | tf_op jit(solution)/shard_map/ppermute | solution.py:36
  14.8 4.6 %collective-permute-start.4 = (bf16[32,128]{1,0:T(8,128)(2,1)S(1)}, bf16[32,128]{1,0:T(8,128)(2,1)S(1)}, u32[]{:S(2)}, u32[]{:S(2)}) collective-permute-start(bf16[32,128]{1,0:T(8,128)(2,1)S(1)} %select.2.refs_0_), channel_id=1, source_target_pairs={{0,16},{4,20},{8,24},{12,28},{16,0},{20,4},{24,8},{28,12},{1,17},{... | collective-permute-start | bytes 24584 | tf_op jit(solution)/shard_map/ppermute | solution.py:36
  19.5 21.9 %collective-permute-start.8 = (bf16[512,256]{1,0:T(8,128)(2,1)S(1)}, bf16[512,256]{1,0:T(8,128)(2,1)S(1)}, u32[]{:S(2)}, u32[]{:S(2)}) collective-permute-start(bf16[512,256]{1,0:T(8,128)(2,1)S(1)} %pack.1), channel_id=1, source_target_pairs={{0,2},{1,3},{2,0},{3,1},{4,6},{5,7},{6,4},{7,5},{8,10},{9,11},{10,... | collective-permute-start | bytes 786440 | tf_op jit(solution)/shard_map/ppermute | solution.py:45
  26.7 21.2 %collective-permute-start.6 = (bf16[256,1024]{1,0:T(8,128)(2,1)S(1)}, bf16[256,1024]{1,0:T(8,128)(2,1)S(1)}, u32[]{:S(2)}, u32[]{:S(2)}) collective-permute-start(bf16[256,1024]{1,0:T(8,128)(2,1)S(1)} %attend.4.rest_11_), channel_id=1, source_target_pairs={{0,1},{1,0},{2,3},{3,2},{4,5},{5,4},{6,7},{7,6},{8,9},{9,8},{10,11... | collective-permute-start | bytes 1572872 | tf_op jit(solution)/shard_map/ppermute | solution.py:45
  26.8 21.1 %collective-permute-start.5 = (bf16[256,1024]{1,0:T(8,128)(2,1)S(1)}, bf16[256,1024]{1,0:T(8,128)(2,1)S(1)}, u32[]{:S(2)}, u32[]{:S(2)}) collective-permute-start(bf16[256,1024]{1,0:T(8,128)(2,1)S(1)} %attend.3.rest_8_), channel_id=1, source_target_pairs={{0,3},{1,2},{2,1},{3,0},{4,7},{5,6},{6,5},{7,4},{8,11},{9,10},{10,... | collective-permute-start | bytes 1572872 | tf_op jit(solution)/shard_map/ppermute | solution.py:45
  27.4 14.0 %collective-permute-start.9 = (bf16[64,128]{1,0:T(8,128)(2,1)S(1)}, bf16[64,128]{1,0:T(8,128)(2,1)S(1)}, u32[]{:S(2)}, u32[]{:S(2)}) collective-permute-start(bf16[64,128]{1,0:T(8,128)(2,1)S(1)} %select.3.rest_7_.rest_8_), channel_id=1, source_target_pairs={{0,2},{1,3},{2,0},{3,1},{4,6},{5,7},{6,4},{7,5},{8,10},{9,11},{10,... | collective-permute-start | bytes 49160 | tf_op jit(solution)/shard_map/ppermute | solution.py:45

commit v8 on v7

--- a/solution.py
+++ b/solution.py
@@ -184,10 +184,9 @@
     )(*off_chip(*arrays))
 
 
-def fill_late(geometry, target, prev_at, sources, mid_scratch, which, write):
+def fill_mids(geometry, target, sources, mid_scratch, which, write):
     block_count, last_blocks, slot, _ = geometry
-    source = sources[which]
-    tails_ref, near_ref, far_ref, third_ref, mine_ref = sources[2:7]
+    near_ref, far_ref, third_ref, mine_ref = sources
     rows = block_count * PER_GROUP
     late = last_blocks * PER_GROUP
     at = 0
@@ -201,14 +200,17 @@
         at += size
     window = pl.ds(pl.multiple_of(target * PER_GROUP, PER_GROUP), MIDS)
     write(0, mid_scratch[window, :])
+
+
+def fill_previous(target, prev_at, source, tails_ref, which, write):
     before = pl.ds(pl.multiple_of(jnp.maximum(target - 1, 0) * BLK, BLK), BLK)
     tail = tails_ref[which * BLK : (which + 1) * BLK, :]
     write(prev_at, jnp.where(target == 0, tail, source[before, :]))
 
 
-def fill_coarse(geometry, width, coarse_ref, which, write):
+def fill_coarse(geometry, width, coarse, which, write):
     block_count, _, slot, reach = geometry
-    wide = coarse_ref[...].astype(F32)
+    wide = coarse.astype(F32)
     if which:
         wide = pltpu.roll(wide, reach * slot - block_count, 0)
     if width > reach * slot:
@@ -216,15 +218,25 @@
     write(MIDS, wide.astype(BF16))
 
 
-def pack_kernel(geometry, flip, *refs):
-    sources, (_, out_ref, mid_scratch) = refs[:-3], refs[-3:]
+def pack_mids_kernel(geometry, flip, *refs):
+    sources, (out_ref, mid_scratch) = refs[:-2], refs[-2:]
     for which in range(2):
-        columns = head_columns(which)
 
         def write(at, value):
-            out_ref[at : at + value.shape[0], columns] = value
-
-        fill_late(geometry, block_of(flip), MIDS, sources, mid_scratch, which, write)
+            out_ref[at : at + value.shape[0], head_columns(which)] = value
+
+        fill_mids(geometry, block_of(flip), sources, mid_scratch, which, write)
+
+
+def pack_rest_kernel(flip, keys_ref, values_ref, tails_ref, coarse_ref, out_ref):
+    half = coarse_ref.shape[0] // 2
+    for which, source in enumerate((keys_ref, values_ref)):
+
+        def write(at, value):
+            out_ref[at : at + value.shape[0], head_columns(which)] = value
+
+        fill_previous(block_of(flip), 0, source, tails_ref, which, write)
+        write(BLK, coarse_ref[which * half : (which + 1) * half, :])
 
 
 def whole_in_vmem(count):
@@ -236,21 +248,19 @@
     return (3 * block_count + last_blocks) * PER_GROUP
 
 
-def pack(flip, shared, after, geometry):
-    rows = MIDS + BLK
+def pack(kernel, rows, operands, scratch):
     return pl.pallas_call(
-        functools.partial(pack_kernel, geometry, flip),
-        in_specs=whole_in_vmem(len(shared))
-        + [pl.BlockSpec(memory_space=pl.ANY)],
+        kernel,
+        in_specs=whole_in_vmem(len(operands)),
         out_specs=pl.BlockSpec(memory_space=pltpu.VMEM),
         out_shape=jax.ShapeDtypeStruct((rows, 2 * HEAD_DIM), BF16),
-        scratch_shapes=[pltpu.VMEM((mid_rows(geometry), HEAD_DIM), BF16)],
+        scratch_shapes=scratch,
         compiler_params=pltpu.CompilerParams(vmem_limit_bytes=VMEM_LIMIT),
         cost_estimate=pl.CostEstimate(
             flops=rows * HEAD_DIM, bytes_accessed=8 * rows * HEAD_DIM, transcendentals=0
         ),
         name="pack",
-    )(*shared, after)
+    )(*operands)
 
 
 def fill_bias(geometry, target, device, width, bias):
@@ -342,15 +352,16 @@
         def write(at, value):
             everything[at : at + value.shape[0], :HEAD_DIM] = value
 
-        fill_late(geometry, target, MIDS + width, sources, mid_scratch, which, write)
-        fill_coarse(geometry, width, sources[-1], which, write)
+        fill_mids(geometry, target, sources[3:7], mid_scratch, which, write)
+        fill_previous(target, MIDS + width, sources[which], sources[2], which, write)
+        fill_coarse(geometry, width, sources[-1][...], which, write)
         own = pl.ds(pl.multiple_of(target * BLK, BLK), BLK)
         write(own_at, sources[which][own, :])
     scratch[1][:, HEAD_DIM:] = jnp.ones((own_at + BLK, HEAD_DIM), BF16)
     fill_bias(geometry, target, lax.axis_index("seq"), width, scratch[2])
 
 
-def fill_shipped(geometry, width, target, early_ref, late_ref, coarse_ref, scratch):
+def fill_shipped(geometry, width, target, early_ref, mids_ref, rest_ref, scratch):
     own_at = MIDS + width + BLK
     for which in range(2):
         everything = scratch[which]
@@ -359,9 +370,10 @@
         def write(at, value):
             everything[at : at + value.shape[0], :HEAD_DIM] = value
 
-        write(0, late_ref[:MIDS, columns])
-        fill_coarse(geometry, width, coarse_ref, which, write)
-        write(MIDS + width, late_ref[MIDS:, columns])
+        write(0, mids_ref[:, columns])
+        coarse = jnp.concatenate([rest_ref[BLK:, head_columns(i)] for i in range(2)])
+        fill_coarse(geometry, width, coarse, which, write)
+        write(MIDS + width, rest_ref[:BLK, columns])
         at = early_ref.shape[1] - (2 - which) * HEAD_DIM
         write(own_at, early_ref[:, at : at + HEAD_DIM])
     scratch[1][:, HEAD_DIM:] = jnp.ones((own_at + BLK, HEAD_DIM), BF16)
@@ -379,7 +391,7 @@
 
 def finish_kernel(flip, geometry, width, heads, q_ref, *rest):
     sources, rest = rest[:SHARED], rest[SHARED:]
-    early_ref, late_ref, coarse_ref, _, output, mid_scratch = rest[:6]
+    early_ref, mids_ref, rest_ref, _, output, mid_scratch = rest[:6]
     rest = rest[3:]
     ours, theirs = rest[3:6], rest[6:9]
     scores, weights, results, sent = rest[9:]
@@ -387,7 +399,7 @@
     copies = []
 
     fill_local(geometry, width, member, sources, mid_scratch, ours)
-    fill_shipped(geometry, width, member, early_ref, late_ref, coarse_ref, theirs)
+    fill_shipped(geometry, width, member, early_ref, mids_ref, rest_ref, theirs)
 
     def emit(job, owner):
         def put(first, group, half, mixed):
@@ -549,9 +561,20 @@
         coarse = select([(0, 0, size), (1, 0, size)], coarse, arriving)
         reach *= 2
     geometry = (block_count, last_blocks, slot, reach)
-    late = pack(away, (keys, values, tails, near, far, third, mine), far, geometry)
+    late = pack(
+        functools.partial(pack_mids_kernel, geometry, away),
+        MIDS,
+        (near, far, third, mine),
+        [pltpu.VMEM((mid_rows(geometry), HEAD_DIM), BF16)],
+    )
     late = exchange(late, "head", away)
-    shipped = (early, late, exchange(coarse, "head", away))
+    rest = pack(
+        functools.partial(pack_rest_kernel, away),
+        BLK + reach * slot // 2,
+        (keys, values, tails, coarse),
+        [],
+    )
+    shipped = (early, late, exchange(rest, "head", away))
 
     shared = (keys, values, tails, near, far, third, mine, coarse)
     after = coarse

time: 49.1 us -> 53 us (1.079)
  waiting for transfers between devices: 17.4 us -> 21.3 us
    ppermute x5, waiting for transfers between devices: 12.5 us -> 16.4 us  [exchange(): return lax.ppermute(array, axis, [(i, i ^ flip) for i in range(size)])]
  transfers between devices with their start and end apart: 10 -> 10, of which waited for: 3 -> 3; matrix products, arithmetic and copies ran while one was open for 0% -> 0% of each run, Pallas kernels for 28% -> 26%
where the time goes in v8:
time: 53 us; the launch traced here: 52.9 us
  waiting for transfers between devices  21.3 us (40%)
  Pallas kernels  16.2 us (31%)
  starting transfers between devices  15.3 us (29%)
    ppermute x5, waiting for transfers between devices, exchange(): return lax.ppermute(array, axis, [(i, i ^ flip) for i in range(size)])  16.4 us
    pallas_call x3, Pallas kernels, attend_call(): pl.pallas_call(functools.partial(kernel, geometry, width, heads), in_spec...  12.1 us
    ppermute x5, starting transfers between devices, cyclic(): lax.ppermute(array, axis, [(i, (i + by) % size) for i in range(size)])  9.88 us
    ppermute x5, starting transfers between devices, exchange(): return lax.ppermute(array, axis, [(i, i ^ flip) for i in range(size)])  5.38 us
    ppermute x5, waiting for transfers between devices, cyclic(): lax.ppermute(array, axis, [(i, (i + by) % size) for i in range(size)])  4.92 us
    pallas_call x1, Pallas kernels, load(): pl.pallas_call(load_kernel, in_specs=[pl.BlockSpec(memory_space=pltpu.HBM...  1.6 us
    pallas_call x1, Pallas kernels, pool(): pl.pallas_call(functools.partial(pool_kernel, block_count, last_blocks, s...  1.46 us
  transfers between devices with their start and end apart: 10, of which 3 were waited for; matrix products, arithmetic and copies ran while one was open for 0% of the time, Pallas kernels for 26%

profile of v8, /device:TPU:0, one launch (start us, length us, event | category | flops | bytes accessed | tf_op | source)
XLA Modules:
  0.0 52.9 jit_solution(11494028471399253865)
XLA Ops:
  0.0 1.5 %pool.1 = (bf16[256,1280]{1,0:T(8,128)(2,1)S(1)}, bf16[1024,128]{1,0:T(8,128)(2,1)S(1)}, bf16[1024,128]{1,0:T(8,128)(2,1)S(1)}, bf16[264,128]{1,0:T(8,128)(2,1)S...) custom-call(bf16[1024,1024]{1,0:T(8,128)(2,1)} %queries_hbm.1, bf16[1024,128]{1,0:T(8,128)(2,1)} %keys_hbm.1, ...), custom_call_target="tpu_custom_call" | custom-call | flops 20971520 | bytes 786432 | tf_op jit(solution)/shard_map/pool/pallas_call | solution.py:122
  1.5 3.0 %collective-permute-start = (bf16[512,128]{1,0:T(8,128)(2,1)S(1)}, bf16[512,128]{1,0:T(8,128)(2,1)S(1)}, u32[]{:S(2)}, u32[]{:S(2)}) collective-permute-start(bf16[512,128]{1,0:T(8,128)(2,1)S(1)} %get-tuple-element.13), channel_id=1, source_target_pairs={{0,4},{4,8},{8,12},{12,16},{16,20},{20,24},{24,28},{28,0},{1,5},{5... | collective-permute-start | bytes 393224 | tf_op jit(solution)/shard_map/ppermute | solution.py:36
  4.5 1.5 %collective-permute-start.7 = (bf16[256,1280]{1,0:T(8,128)(2,1)S(1)}, bf16[256,1280]{1,0:T(8,128)(2,1)S(1)}, u32[]{:S(2)}, u32[]{:S(2)}) collective-permute-start(bf16[256,1280]{1,0:T(8,128)(2,1)S(1)} %get-tuple-element.16), channel_id=1, source_target_pairs={{0,2},{1,3},{2,0},{3,1},{4,6},{5,7},{6,4},{7,5},{8,10},{9,11},{10,... | collective-permute-start | bytes 1966088 | tf_op jit(solution)/shard_map/ppermute | solution.py:45
  6.0 1.6 %collective-permute-start.2 = (bf16[264,128]{1,0:T(8,128)(2,1)S(1)}, bf16[264,128]{1,0:T(8,128)(2,1)S(1)}, u32[]{:S(2)}, u32[]{:S(2)}) collective-permute-start(bf16[264,128]{1,0:T(8,128)(2,1)S(1)} %get-tuple-element.14.refs_0_.rest_6_.refs_3_), channel_id=1, source_target_pairs={{0,8},{4,12},{8,16},{12,20},{16,24},{20,28},{24,0},{28,4},{1,9},{5... | collective-permute-start | bytes 202760 | tf_op jit(solution)/shard_map/ppermute | solution.py:36
  7.6 1.5 %collective-permute-start.1 = (bf16[264,128]{1,0:T(8,128)(2,1)S(1)}, bf16[264,128]{1,0:T(8,128)(2,1)S(1)}, u32[]{:S(2)}, u32[]{:S(2)}) collective-permute-start(bf16[264,128]{1,0:T(8,128)(2,1)S(1)} %get-tuple-element.14.refs_0_.rest_6_.refs_3_), channel_id=1, source_target_pairs={{0,4},{4,8},{8,12},{12,16},{16,20},{20,24},{24,28},{28,0},{1,5},{5... | collective-permute-start | bytes 202760 | tf_op jit(solution)/shard_map/ppermute | solution.py:36
  9.1 2.5 %collective-permute-start.3 = (bf16[72,128]{1,0:T(8,128)(2,1)S(1)}, bf16[72,128]{1,0:T(8,128)(2,1)S(1)}, u32[]{:S(2)}, u32[]{:S(2)}) collective-permute-start(bf16[72,128]{1,0:T(8,128)(2,1)S(1)} %get-tuple-element.15), channel_id=1, source_target_pairs={{0,12},{4,16},{8,20},{12,24},{16,28},{20,0},{24,4},{28,8},{1,13},{... | collective-permute-start | bytes 55304 | tf_op jit(solution)/shard_map/ppermute | solution.py:36
  11.6 3.1 %collective-permute-done.3.refs_3_.rest_5_.refs_2_ = bf16[72,128]{1,0:T(8,128)(2,1)S(1)} collective-permute-done((bf16[72,128]{1,0:T(8,128)(2,1)S(1)}, bf16[72,128]{1,0:T(8,128)(2,1)S(1)}, u32[]{:S(2)}, u32[]{:S(2)}) %collective-permute-start.3) | collective-permute-done | bytes 18464 | tf_op jit(solution)/shard_map/ppermute | solution.py:36
  14.8 0.0 collective-permute-done.2.refs_2_.rest_4_.refs_1_
  14.8 0.0 collective-permute-done.1.refs_1_.rest_3_.refs_0_
  14.8 1.2 %collective-permute-start.4 = (bf16[32,128]{1,0:T(8,128)(2,1)S(1)}, bf16[32,128]{1,0:T(8,128)(2,1)S(1)}, u32[]{:S(2)}, u32[]{:S(2)}) collective-permute-start(bf16[32,128]{1,0:T(8,128)(2,1)S(1)} %select.2.refs_0_), channel_id=1, source_target_pairs={{0,16},{4,20},{8,24},{12,28},{16,0},{20,4},{24,8},{28,12},{1,17},{... | collective-permute-start | bytes 24584 | tf_op jit(solution)/shard_map/ppermute | solution.py:36
  16.0 1.6 %load.1.q_ref = bf16[1024,1024]{1,0:T(8,128)(2,1)S(1)} custom-call(bf16[1024,1024]{1,0:T(8,128)(2,1)} %queries_hbm.1), custom_call_target="tpu_custom_call" | custom-call | flops 2097152 | bytes 4194304 | tf_op jit(solution)/shard_map/load/pallas_call | solution.py:171
  17.6 1.8 %collective-permute-done.4.refs_1_ = bf16[32,128]{1,0:T(8,128)(2,1)S(1)} collective-permute-done((bf16[32,128]{1,0:T(8,128)(2,1)S(1)}, bf16[32,128]{1,0:T(8,128)(2,1)S(1)}, u32[]{:S(2)}, u32[]{:S(2)}) %collective-permute-start.4) | collective-permute-done | bytes 8224 | tf_op jit(solution)/shard_map/ppermute | solution.py:36
  19.4 0.0 collective-permute-done.rest_2_.tails_ref
  19.4 2.8 %attend.3.rest_8_ = bf16[256,1024]{1,0:T(8,128)(2,1)S(1)} custom-call(bf16[1024,1024]{1,0:T(8,128)(2,1)S(1)} %load.1.q_ref, bf16[1024,128]{1,0:T(8,128)(2,1)S(1)} %get-tuple-element.11.rest_0_.keys_ref, bf16[1024,128]{1,0:T(8,128)(2,1)S(1)} %get-tuple-element.12.rest_1_.values_ref, bf16[512,128]{1,0:T(8,128)(2,1)S(1)} %collective-permute-done.rest_2_.tails_ref, ...), custom_call_target="tpu_custom_call" | custom-call | flops 1409286144 | bytes 2097152 | tf_op jit(solution)/shard_map/attend/pallas_call | solution.py:446
  22.2 2.8 %attend.4.rest_11_ = bf16[256,1024]{1,0:T(8,128)(2,1)S(1)} custom-call(bf16[1024,1024]{1,0:T(8,128)(2,1)S(1)} %load.1.q_ref, bf16[1024,128]{1,0:T(8,128)(2,1)S(1)} %get-tuple-element.11.rest_0_.keys_ref, bf16[1024,128]{1,0:T(8,128)(2,1)S(1)} %get-tuple-element.12.rest_1_.values_ref, bf16[512,128]{1,0:T(8,128)(2,1)S(1)} %collective-permute-done.rest_2_.tails_ref, ...), custom_call_target="tpu_custom_call" | custom-call | flops 1409286144 | bytes 2097152 | tf_op jit(solution)/shard_map/attend/pallas_call | solution.py:446
  25.0 0.1 collective-permute-start.6
  25.1 1.6 %collective-permute-start.5 = (bf16[256,1024]{1,0:T(8,128)(2,1)S(1)}, bf16[256,1024]{1,0:T(8,128)(2,1)S(1)}, u32[]{:S(2)}, u32[]{:S(2)}) collective-permute-start(bf16[256,1024]{1,0:T(8,128)(2,1)S(1)} %attend.3.rest_8_), channel_id=1, source_target_pairs={{0,3},{1,2},{2,1},{3,0},{4,7},{5,6},{6,5},{7,4},{8,11},{9,10},{10,... | collective-permute-start | bytes 1572872 | tf_op jit(solution)/shard_map/ppermute | solution.py:45
  26.8 0.6 %collective-permute-start.9 = (bf16[288,256]{1,0:T(8,128)(2,1)S(1)}, bf16[288,256]{1,0:T(8,128)(2,1)S(1)}, u32[]{:S(2)}, u32[]{:S(2)}) collective-permute-start(bf16[288,256]{1,0:T(8,128)(2,1)S(1)} %pack.3), channel_id=1, source_target_pairs={{0,2},{1,3},{2,0},{3,1},{4,6},{5,7},{6,4},{7,5},{8,10},{9,11},{10,... | collective-permute-start | bytes 442376 | tf_op jit(solution)/shard_map/ppermute | solution.py:45
  27.4 1.6 %collective-permute-start.8 = (bf16[256,256]{1,0:T(8,128)(2,1)S(1)}, bf16[256,256]{1,0:T(8,128)(2,1)S(1)}, u32[]{:S(2)}, u32[]{:S(2)}) collective-permute-start(bf16[256,256]{1,0:T(8,128)(2,1)S(1)} %pack.2), channel_id=1, source_target_pairs={{0,2},{1,3},{2,0},{3,1},{4,6},{5,7},{6,4},{7,5},{8,10},{9,11},{10,... | collective-permute-start | bytes 393224 | tf_op jit(solution)/shard_map/ppermute | solution.py:45
  29.0 16.4 %collective-permute-done.8.rest_9_ = bf16[256,256]{1,0:T(8,128)(2,1)S(1)} collective-permute-done((bf16[256,256]{1,0:T(8,128)(2,1)S(1)}, bf16[256,256]{1,0:T(8,128)(2,1)S(1)}, u32[]{:S(2)}, u32[]{:S(2)}) %collective-permute-start.8) | collective-permute-done | bytes 131104 | tf_op jit(solution)/shard_map/ppermute | solution.py:45
  45.4 0.0 collective-permute-done.9.rest_10_
  45.4 0.0 collective-permute-done.7.rest_8_
  45.4 6.5 %attend.5.refs_2_ = bf16[256,4096]{1,0:T(8,128)(2,1)} custom-call(bf16[1024,1024]{1,0:T(8,128)(2,1)S(1)} %load.1.q_ref, bf16[1024,128]{1,0:T(8,128)(2,1)S(1)} %get-tuple-element.11.rest_0_.keys_ref, bf16[1024,128]{1,0:T(8,128)(2,1)S(1)} %get-tuple-element.12.rest_1_.values_ref, bf16[512,128]{1,0:T(8,128)(2,1)S(1)} %collective-permute-done.rest_2_.tails_ref, ...), custom_call_target="tpu_custom_call" | custom-call | flops 2818572288 | bytes 2097152 | tf_op jit(solution)/shard_map/attend/pallas_call | solution.py:446
  51.8 0.0 collective-permute-done.6.refs_1_
  51.9 0.0 collective-permute-done.5.refs_0_
  51.9 1.0 %place.1 = bf16[256,4096]{1,0:T(8,128)(2,1)} custom-call(bf16[256,1024]{1,0:T(8,128)(2,1)S(1)} %collective-permute-done.5.refs_0_, bf16[256,1024]{1,0:T(8,128)(2,1)S(1)} %collective-permute-done.6.refs_1_, bf16[256,4096]{1,0:T(8,128)(2,1)} %attend.5.refs_2_), custom_call_target="tpu_custom_call", output_to_operand_aliasing={{}: (2, {})} | custom-call | flops 524288 | bytes 2097152 | tf_op jit(solution)/shard_map/place/pallas_call | solution.py:520
  (4 shorter events, 0.1 us)
Async XLA Ops:
  1.5 17.9 %collective-permute-start = (bf16[512,128]{1,0:T(8,128)(2,1)S(1)}, bf16[512,128]{1,0:T(8,128)(2,1)S(1)}, u32[]{:S(2)}, u32[]{:S(2)}) collective-permute-start(bf16[512,128]{1,0:T(8,128)(2,1)S(1)} %get-tuple-element.13), channel_id=1, source_target_pairs={{0,4},{4,8},{8,12},{12,16},{16,20},{20,24},{24,28},{28,0},{1,5},{5... | collective-permute-start | bytes 393224 | tf_op jit(solution)/shard_map/ppermute | solution.py:36
  4.5 40.9 %collective-permute-start.7 = (bf16[256,1280]{1,0:T(8,128)(2,1)S(1)}, bf16[256,1280]{1,0:T(8,128)(2,1)S(1)}, u32[]{:S(2)}, u32[]{:S(2)}) collective-permute-start(bf16[256,1280]{1,0:T(8,128)(2,1)S(1)} %get-tuple-element.16), channel_id=1, source_target_pairs={{0,2},{1,3},{2,0},{3,1},{4,6},{5,7},{6,4},{7,5},{8,10},{9,11},{10,... | collective-permute-start | bytes 1966088 | tf_op jit(solution)/shard_map/ppermute | solution.py:45
  6.0 8.8 %collective-permute-start.2 = (bf16[264,128]{1,0:T(8,128)(2,1)S(1)}, bf16[264,128]{1,0:T(8,128)(2,1)S(1)}, u32[]{:S(2)}, u32[]{:S(2)}) collective-permute-start(bf16[264,128]{1,0:T(8,128)(2,1)S(1)} %get-tuple-element.14.refs_0_.rest_6_.refs_3_), channel_id=1, source_target_pairs={{0,8},{4,12},{8,16},{12,20},{16,24},{20,28},{24,0},{28,4},{1,9},{5... | collective-permute-start | bytes 202760 | tf_op jit(solution)/shard_map/ppermute | solution.py:36
  7.6 7.2 %collective-permute-start.1 = (bf16[264,128]{1,0:T(8,128)(2,1)S(1)}, bf16[264,128]{1,0:T(8,128)(2,1)S(1)}, u32[]{:S(2)}, u32[]{:S(2)}) collective-permute-start(bf16[264,128]{1,0:T(8,128)(2,1)S(1)} %get-tuple-element.14.refs_0_.rest_6_.refs_3_), channel_id=1, source_target_pairs={{0,4},{4,8},{8,12},{12,16},{16,20},{20,24},{24,28},{28,0},{1,5},{5... | collective-permute-start | bytes 202760 | tf_op jit(solution)/shard_map/ppermute | solution.py:36
  9.1 5.6 %collective-permute-start.3 = (bf16[72,128]{1,0:T(8,128)(2,1)S(1)}, bf16[72,128]{1,0:T(8,128)(2,1)S(1)}, u32[]{:S(2)}, u32[]{:S(2)}) collective-permute-start(bf16[72,128]{1,0:T(8,128)(2,1)S(1)} %get-tuple-element.15), channel_id=1, source_target_pairs={{0,12},{4,16},{8,20},{12,24},{16,28},{20,0},{24,4},{28,8},{1,13},{... | collective-permute-start | bytes 55304 | tf_op jit(solution)/shard_map/ppermute | solution.py:36
  14.8 4.6 %collective-permute-start.4 = (bf16[32,128]{1,0:T(8,128)(2,1)S(1)}, bf16[32,128]{1,0:T(8,128)(2,1)S(1)}, u32[]{:S(2)}, u32[]{:S(2)}) collective-permute-start(bf16[32,128]{1,0:T(8,128)(2,1)S(1)} %select.2.refs_0_), channel_id=1, source_target_pairs={{0,16},{4,20},{8,24},{12,28},{16,0},{20,4},{24,8},{28,12},{1,17},{... | collective-permute-start | bytes 24584 | tf_op jit(solution)/shard_map/ppermute | solution.py:36
  25.0 26.8 %collective-permute-start.6 = (bf16[256,1024]{1,0:T(8,128)(2,1)S(1)}, bf16[256,1024]{1,0:T(8,128)(2,1)S(1)}, u32[]{:S(2)}, u32[]{:S(2)}) collective-permute-start(bf16[256,1024]{1,0:T(8,128)(2,1)S(1)} %attend.4.rest_11_), channel_id=1, source_target_pairs={{0,1},{1,0},{2,3},{3,2},{4,5},{5,4},{6,7},{7,6},{8,9},{9,8},{10,11... | collective-permute-start | bytes 1572872 | tf_op jit(solution)/shard_map/ppermute | solution.py:45
  25.1 26.8 %collective-permute-start.5 = (bf16[256,1024]{1,0:T(8,128)(2,1)S(1)}, bf16[256,1024]{1,0:T(8,128)(2,1)S(1)}, u32[]{:S(2)}, u32[]{:S(2)}) collective-permute-start(bf16[256,1024]{1,0:T(8,128)(2,1)S(1)} %attend.3.rest_8_), channel_id=1, source_target_pairs={{0,3},{1,2},{2,1},{3,0},{4,7},{5,6},{6,5},{7,4},{8,11},{9,10},{10,... | collective-permute-start | bytes 1572872 | tf_op jit(solution)/shard_map/ppermute | solution.py:45
  26.8 18.6 %collective-permute-start.9 = (bf16[288,256]{1,0:T(8,128)(2,1)S(1)}, bf16[288,256]{1,0:T(8,128)(2,1)S(1)}, u32[]{:S(2)}, u32[]{:S(2)}) collective-permute-start(bf16[288,256]{1,0:T(8,128)(2,1)S(1)} %pack.3), channel_id=1, source_target_pairs={{0,2},{1,3},{2,0},{3,1},{4,6},{5,7},{6,4},{7,5},{8,10},{9,11},{10,... | collective-permute-start | bytes 442376 | tf_op jit(solution)/shard_map/ppermute | solution.py:45
  27.4 18.0 %collective-permute-start.8 = (bf16[256,256]{1,0:T(8,128)(2,1)S(1)}, bf16[256,256]{1,0:T(8,128)(2,1)S(1)}, u32[]{:S(2)}, u32[]{:S(2)}) collective-permute-start(bf16[256,256]{1,0:T(8,128)(2,1)S(1)} %pack.2), channel_id=1, source_target_pairs={{0,2},{1,3},{2,0},{3,1},{4,6},{5,7},{6,4},{7,5},{8,10},{9,11},{10,... | collective-permute-start | bytes 393224 | tf_op jit(solution)/shard_map/ppermute | solution.py:45

commit v9 on v8

--- a/solution.py
+++ b/solution.py
@@ -49,29 +49,44 @@
     return lax.axis_index("head") ^ flip
 
 
-def pool_kernel(block_count, last_blocks, slot, flip, queries_hbm, keys_hbm, values_hbm, mid_hbm, coarse_hbm,
-                early_out, keys_ref, values_ref, near_out, third_out, tails_out, mid_ref, coarse_ref,
-                arrived):
+def prepare_kernel(flip, *refs):
+    sources, (early_out, *targets), arrived = refs[:5], refs[5:10], refs[10]
     wanted = pl.ds(pl.multiple_of(block_of(flip) * BLK, BLK), BLK)
-    moves = [
-        (mid_hbm, mid_ref),
-        (coarse_hbm, coarse_ref),
-        (keys_hbm, keys_ref),
-        (values_hbm, values_ref),
-    ]
-    at = 0
-    for source in (queries_hbm, keys_hbm, values_hbm):
+    moves, at = [], 0
+    for source in sources[:3]:
         columns = slice(at, at + source.shape[1])
         moves.append((source.at[wanted, :], early_out.at[:, columns]))
         at += source.shape[1]
+    moves += list(zip(sources[1:], targets))
     copies = [
         pltpu.make_async_copy(source, target, arrived.at[i])
         for i, (source, target) in enumerate(moves)
     ]
     for copy in copies:
         copy.start()
-    for copy in copies[:4]:
+    for copy in copies:
         copy.wait()
+
+
+def prepare(flip, *arrays):
+    early = jax.ShapeDtypeStruct((BLK, sum(a.shape[1] for a in arrays[:3])), BF16)
+    shapes = [early] + [jax.ShapeDtypeStruct(a.shape, a.dtype) for a in arrays[1:]]
+    return pl.pallas_call(
+        functools.partial(prepare_kernel, flip),
+        in_specs=[pl.BlockSpec(memory_space=pltpu.HBM) for _ in arrays],
+        out_specs=[pl.BlockSpec(memory_space=pltpu.VMEM) for _ in shapes],
+        out_shape=shapes,
+        scratch_shapes=[pltpu.SemaphoreType.DMA((7,))],
+        compiler_params=pltpu.CompilerParams(vmem_limit_bytes=VMEM_LIMIT),
+        cost_estimate=pl.CostEstimate(
+            flops=early.size, bytes_accessed=4 * early.size, transcendentals=0
+        ),
+        name="prepare",
+    )(*off_chip(*arrays))
+
+
+def pool_kernel(block_count, last_blocks, slot, keys_ref, values_ref, mid_ref, coarse_ref,
+                near_out, third_out, tails_out):
     rows = block_count * PER_GROUP
     repeat = (
         lax.broadcasted_iota(jnp.int32, (GROUP, BLK), 1) % GROUP
@@ -106,35 +121,25 @@
         tails_out[which * BLK : (which + 1) * BLK, :] = source[edge : edge + BLK, :]
     near_out[:slot, :] = total.astype(BF16)
     third_out[:slot, :] = total.astype(BF16)
-    for copy in copies[4:]:
-        copy.wait()
-
-
-def pool(flip, queries, keys, values, mid_pool, coarse_pool, block_count, last_blocks, slot):
+
+
+def pool(keys, values, mid_pool, coarse_pool, block_count, last_blocks, slot):
     shapes = (
-        (BLK, queries.shape[1] + 2 * HEAD_DIM),
-        keys.shape,
-        values.shape,
         (slot + 2 * block_count * PER_GROUP, HEAD_DIM),
         (slot + 2 * last_blocks * PER_GROUP, HEAD_DIM),
         (2 * BLK, HEAD_DIM),
     )
     return pl.pallas_call(
-        functools.partial(pool_kernel, block_count, last_blocks, slot, flip),
-        in_specs=[pl.BlockSpec(memory_space=pltpu.HBM)] * 5,
+        functools.partial(pool_kernel, block_count, last_blocks, slot),
+        in_specs=[pl.BlockSpec(memory_space=pltpu.VMEM)] * 4,
         out_specs=[pl.BlockSpec(memory_space=pltpu.VMEM) for _ in shapes],
         out_shape=[jax.ShapeDtypeStruct(shape, BF16) for shape in shapes],
-        scratch_shapes=[
-            pltpu.VMEM(mid_pool.shape, BF16),
-            pltpu.VMEM(coarse_pool.shape, BF16),
-            pltpu.SemaphoreType.DMA((7,)),
-        ],
         cost_estimate=pl.CostEstimate(
             flops=4 * keys.size * (PER_GROUP + slot), bytes_accessed=6 * keys.size, transcendentals=0
         ),
         compiler_params=pltpu.CompilerParams(vmem_limit_bytes=VMEM_LIMIT),
         name="pool",
-    )(*off_chip(queries, keys, values, mid_pool, coarse_pool))
+    )(keys, values, mid_pool, coarse_pool)
 
 
 def select_kernel(parts, *refs):
@@ -544,9 +549,10 @@
     slot = round_up(2 * block_count, 8)
     away = members // 2
 
-    early, keys, values, mine, third, tails = pool(
-        away, queries, keys, values, mid_pool, coarse_pool, block_count, last_blocks, slot
-    )
+    early, keys, values, mid_pool, coarse_pool = prepare(
+        away, queries, keys, values, mid_pool, coarse_pool
+    )
+    mine, third, tails = pool(keys, values, mid_pool, coarse_pool, block_count, last_blocks, slot)
     near = cyclic(mine, "seq", 1)
     early = exchange(early, "head", away)
     far = cyclic(mine, "seq", 2)
@@ -583,7 +589,8 @@
         after = attend(flip, queries, shared, after, heads_here, geometry)
         arrived.append((flip, 0, exchange(after, "head", flip)))
     output = finish(queries, shared, shipped, after, away, heads_here, geometry, members * columns)
-    return place(output, arrived, columns)
+    output = place(output, [p for p in arrived if p[0] < away], columns)
+    return place(output, [p for p in arrived if p[0] > away], columns)
 
 
 def sent_flips(members):

time: 53 us -> 53.8 us (1.015)
  Pallas kernels: 16.2 us -> 17 us
    pallas_call x0 -> x1, Pallas kernels: none -> 1.29 us  [prepare(): pl.pallas_call(functools.partial(prepare_kernel, flip), in_specs=[pl.Bloc...]
    pallas_call x1, Pallas kernels: 1.46 us -> 0.31 us  [pool(): pl.pallas_call(functools.partial(pool_kernel, block_count, last_blocks, s...]
    pallas_call x1 -> x2, Pallas kernels: 1 us -> 1.63 us  [place(): pl.pallas_call(functools.partial(place_kernel, spots, columns), in_specs=...]
  transfers between devices with their start and end apart: 10 -> 10, of which waited for: 3 -> 3; matrix products, arithmetic and copies ran while one was open for 0% -> 0% of each run, Pallas kernels for 26% -> 27%
where the time goes in v9:
time: 53.8 us; the launch traced here: 53.6 us
  waiting for transfers between devices  21.3 us (40%)
  Pallas kernels  17 us (32%)
  starting transfers between devices  15.3 us (28%)
    ppermute x5, waiting for transfers between devices, exchange(): return lax.ppermute(array, axis, [(i, i ^ flip) for i in range(size)])  16.4 us
    pallas_call x3, Pallas kernels, attend_call(): pl.pallas_call(functools.partial(kernel, geometry, width, heads), in_spec...  12 us
    ppermute x5, starting transfers between devices, cyclic(): lax.ppermute(array, axis, [(i, (i + by) % size) for i in range(size)])  9.88 us
    ppermute x5, starting transfers between devices, exchange(): return lax.ppermute(array, axis, [(i, i ^ flip) for i in range(size)])  5.37 us
    ppermute x5, waiting for transfers between devices, cyclic(): lax.ppermute(array, axis, [(i, (i + by) % size) for i in range(size)])  4.92 us
    pallas_call x2, Pallas kernels, place(): pl.pallas_call(functools.partial(place_kernel, spots, columns), in_specs=...  1.63 us
    pallas_call x1, Pallas kernels, load(): pl.pallas_call(load_kernel, in_specs=[pl.BlockSpec(memory_space=pltpu.HBM...  1.6 us
    pallas_call x1, Pallas kernels, prepare(): pl.pallas_call(functools.partial(prepare_kernel, flip), in_specs=[pl.Bloc...  1.29 us
  transfers between devices with their start and end apart: 10, of which 3 were waited for; matrix products, arithmetic and copies ran while one was open for 0% of the time, Pallas kernels for 27%

profile of v9, /device:TPU:0, one launch (start us, length us, event | category | flops | bytes accessed | tf_op | source)
XLA Modules:
  0.0 53.6 jit_solution(13967074106787518122)
XLA Ops:
  0.0 1.3 %prepare.1 = (bf16[256,1280]{1,0:T(8,128)(2,1)S(1)}, bf16[1024,128]{1,0:T(8,128)(2,1)S(1)}, bf16[1024,128]{1,0:T(8,128)(2,1)S(1)}, bf16[1,8]{1,0:T(2,128)(2,1)S(1)}, bf16[1,256]{1,0:T(2,128)(2,1)S(1)}) custom-call(bf16[1024,1024]{1,0:T(8,128)(2,1)} %refs_0_.3, bf16[1024,128]{1,0:T(8,128)(2,1)} %refs_1_.1, bf16[1024,128]{1,0:T(8,128)(2,1)} %refs_2_.1, ...), custom_call_target="tpu_custom_call" | custom-call | flops 327680 | bytes 1310720 | tf_op jit(solution)/shard_map/prepare/pallas_call | solution.py:74
  1.3 0.3 pool.1
  1.6 3.0 %collective-permute-start = (bf16[512,128]{1,0:T(8,128)(2,1)S(1)}, bf16[512,128]{1,0:T(8,128)(2,1)S(1)}, u32[]{:S(2)}, u32[]{:S(2)}) collective-permute-start(bf16[512,128]{1,0:T(8,128)(2,1)S(1)} %get-tuple-element.17), channel_id=1, source_target_pairs={{0,4},{4,8},{8,12},{12,16},{16,20},{20,24},{24,28},{28,0},{1,5},{5... | collective-permute-start | bytes 393224 | tf_op jit(solution)/shard_map/ppermute | solution.py:36
  4.6 1.5 %collective-permute-start.7 = (bf16[256,1280]{1,0:T(8,128)(2,1)S(1)}, bf16[256,1280]{1,0:T(8,128)(2,1)S(1)}, u32[]{:S(2)}, u32[]{:S(2)}) collective-permute-start(bf16[256,1280]{1,0:T(8,128)(2,1)S(1)} %get-tuple-element.20), channel_id=1, source_target_pairs={{0,2},{1,3},{2,0},{3,1},{4,6},{5,7},{6,4},{7,5},{8,10},{9,11},{10,... | collective-permute-start | bytes 1966088 | tf_op jit(solution)/shard_map/ppermute | solution.py:45
  6.2 1.6 %collective-permute-start.2 = (bf16[264,128]{1,0:T(8,128)(2,1)S(1)}, bf16[264,128]{1,0:T(8,128)(2,1)S(1)}, u32[]{:S(2)}, u32[]{:S(2)}) collective-permute-start(bf16[264,128]{1,0:T(8,128)(2,1)S(1)} %get-tuple-element.18.refs_0_.rest_6_.refs_3_), channel_id=1, source_target_pairs={{0,8},{4,12},{8,16},{12,20},{16,24},{20,28},{24,0},{28,4},{1,9},{5... | collective-permute-start | bytes 202760 | tf_op jit(solution)/shard_map/ppermute | solution.py:36
  7.7 1.5 %collective-permute-start.1 = (bf16[264,128]{1,0:T(8,128)(2,1)S(1)}, bf16[264,128]{1,0:T(8,128)(2,1)S(1)}, u32[]{:S(2)}, u32[]{:S(2)}) collective-permute-start(bf16[264,128]{1,0:T(8,128)(2,1)S(1)} %get-tuple-element.18.refs_0_.rest_6_.refs_3_), channel_id=1, source_target_pairs={{0,4},{4,8},{8,12},{12,16},{16,20},{20,24},{24,28},{28,0},{1,5},{5... | collective-permute-start | bytes 202760 | tf_op jit(solution)/shard_map/ppermute | solution.py:36
  9.3 2.5 %collective-permute-start.3 = (bf16[72,128]{1,0:T(8,128)(2,1)S(1)}, bf16[72,128]{1,0:T(8,128)(2,1)S(1)}, u32[]{:S(2)}, u32[]{:S(2)}) collective-permute-start(bf16[72,128]{1,0:T(8,128)(2,1)S(1)} %get-tuple-element.19), channel_id=1, source_target_pairs={{0,12},{4,16},{8,20},{12,24},{16,28},{20,0},{24,4},{28,8},{1,13},{... | collective-permute-start | bytes 55304 | tf_op jit(solution)/shard_map/ppermute | solution.py:36
  11.8 3.1 %collective-permute-done.3.refs_3_.rest_5_.refs_2_ = bf16[72,128]{1,0:T(8,128)(2,1)S(1)} collective-permute-done((bf16[72,128]{1,0:T(8,128)(2,1)S(1)}, bf16[72,128]{1,0:T(8,128)(2,1)S(1)}, u32[]{:S(2)}, u32[]{:S(2)}) %collective-permute-start.3) | collective-permute-done | bytes 18464 | tf_op jit(solution)/shard_map/ppermute | solution.py:36
  14.9 0.0 collective-permute-done.2.refs_2_.rest_4_.refs_1_
  14.9 0.0 collective-permute-done.1.refs_1_.rest_3_.refs_0_
  14.9 1.2 %collective-permute-start.4 = (bf16[32,128]{1,0:T(8,128)(2,1)S(1)}, bf16[32,128]{1,0:T(8,128)(2,1)S(1)}, u32[]{:S(2)}, u32[]{:S(2)}) collective-permute-start(bf16[32,128]{1,0:T(8,128)(2,1)S(1)} %select.2.refs_0_), channel_id=1, source_target_pairs={{0,16},{4,20},{8,24},{12,28},{16,0},{20,4},{24,8},{28,12},{1,17},{... | collective-permute-start | bytes 24584 | tf_op jit(solution)/shard_map/ppermute | solution.py:36
  16.2 1.6 %load.1.q_ref = bf16[1024,1024]{1,0:T(8,128)(2,1)S(1)} custom-call(bf16[1024,1024]{1,0:T(8,128)(2,1)} %refs_0_.3), custom_call_target="tpu_custom_call" | custom-call | flops 2097152 | bytes 4194304 | tf_op jit(solution)/shard_map/load/pallas_call | solution.py:176
  17.8 1.8 %collective-permute-done.4.refs_1_ = bf16[32,128]{1,0:T(8,128)(2,1)S(1)} collective-permute-done((bf16[32,128]{1,0:T(8,128)(2,1)S(1)}, bf16[32,128]{1,0:T(8,128)(2,1)S(1)}, u32[]{:S(2)}, u32[]{:S(2)}) %collective-permute-start.4) | collective-permute-done | bytes 8224 | tf_op jit(solution)/shard_map/ppermute | solution.py:36
  19.6 0.0 collective-permute-done.rest_2_.tails_ref
  19.6 2.8 %attend.3.rest_8_ = bf16[256,1024]{1,0:T(8,128)(2,1)S(1)} custom-call(bf16[1024,1024]{1,0:T(8,128)(2,1)S(1)} %load.1.q_ref, bf16[1024,128]{1,0:T(8,128)(2,1)S(1)} %get-tuple-element.13.keys_ref.rest_0_, bf16[1024,128]{1,0:T(8,128)(2,1)S(1)} %get-tuple-element.14.values_ref.rest_1_, bf16[512,128]{1,0:T(8,128)(2,1)S(1)} %collective-permute-done.rest_2_.tails_ref, ...), custom_call_target="tpu_custom_call" | custom-call | flops 1409286144 | bytes 2097152 | tf_op jit(solution)/shard_map/attend/pallas_call | solution.py:451
  22.4 2.8 %attend.4.rest_11_ = bf16[256,1024]{1,0:T(8,128)(2,1)S(1)} custom-call(bf16[1024,1024]{1,0:T(8,128)(2,1)S(1)} %load.1.q_ref, bf16[1024,128]{1,0:T(8,128)(2,1)S(1)} %get-tuple-element.13.keys_ref.rest_0_, bf16[1024,128]{1,0:T(8,128)(2,1)S(1)} %get-tuple-element.14.values_ref.rest_1_, bf16[512,128]{1,0:T(8,128)(2,1)S(1)} %collective-permute-done.rest_2_.tails_ref, ...), custom_call_target="tpu_custom_call" | custom-call | flops 1409286144 | bytes 2097152 | tf_op jit(solution)/shard_map/attend/pallas_call | solution.py:451
  25.2 0.1 collective-permute-start.6
  25.2 1.6 %collective-permute-start.5 = (bf16[256,1024]{1,0:T(8,128)(2,1)S(1)}, bf16[256,1024]{1,0:T(8,128)(2,1)S(1)}, u32[]{:S(2)}, u32[]{:S(2)}) collective-permute-start(bf16[256,1024]{1,0:T(8,128)(2,1)S(1)} %attend.3.rest_8_), channel_id=1, source_target_pairs={{0,3},{1,2},{2,1},{3,0},{4,7},{5,6},{6,5},{7,4},{8,11},{9,10},{10,... | collective-permute-start | bytes 1572872 | tf_op jit(solution)/shard_map/ppermute | solution.py:45
  26.9 0.6 %collective-permute-start.9 = (bf16[288,256]{1,0:T(8,128)(2,1)S(1)}, bf16[288,256]{1,0:T(8,128)(2,1)S(1)}, u32[]{:S(2)}, u32[]{:S(2)}) collective-permute-start(bf16[288,256]{1,0:T(8,128)(2,1)S(1)} %pack.3), channel_id=1, source_target_pairs={{0,2},{1,3},{2,0},{3,1},{4,6},{5,7},{6,4},{7,5},{8,10},{9,11},{10,... | collective-permute-start | bytes 442376 | tf_op jit(solution)/shard_map/ppermute | solution.py:45
  27.5 1.6 %collective-permute-start.8 = (bf16[256,256]{1,0:T(8,128)(2,1)S(1)}, bf16[256,256]{1,0:T(8,128)(2,1)S(1)}, u32[]{:S(2)}, u32[]{:S(2)}) collective-permute-start(bf16[256,256]{1,0:T(8,128)(2,1)S(1)} %pack.2), channel_id=1, source_target_pairs={{0,2},{1,3},{2,0},{3,1},{4,6},{5,7},{6,4},{7,5},{8,10},{9,11},{10,... | collective-permute-start | bytes 393224 | tf_op jit(solution)/shard_map/ppermute | solution.py:45
  29.1 16.4 %collective-permute-done.8.rest_9_ = bf16[256,256]{1,0:T(8,128)(2,1)S(1)} collective-permute-done((bf16[256,256]{1,0:T(8,128)(2,1)S(1)}, bf16[256,256]{1,0:T(8,128)(2,1)S(1)}, u32[]{:S(2)}, u32[]{:S(2)}) %collective-permute-start.8) | collective-permute-done | bytes 131104 | tf_op jit(solution)/shard_map/ppermute | solution.py:45
  45.5 0.0 collective-permute-done.9.rest_10_
  45.5 0.0 collective-permute-done.7.rest_8_
  45.5 6.5 %attend.5.refs_1_ = bf16[256,4096]{1,0:T(8,128)(2,1)} custom-call(bf16[1024,1024]{1,0:T(8,128)(2,1)S(1)} %load.1.q_ref, bf16[1024,128]{1,0:T(8,128)(2,1)S(1)} %get-tuple-element.13.keys_ref.rest_0_, bf16[1024,128]{1,0:T(8,128)(2,1)S(1)} %get-tuple-element.14.values_ref.rest_1_, bf16[512,128]{1,0:T(8,128)(2,1)S(1)} %collective-permute-done.rest_2_.tails_ref, ...), custom_call_target="tpu_custom_call" | custom-call | flops 2818572288 | bytes 2097152 | tf_op jit(solution)/shard_map/attend/pallas_call | solution.py:451
  52.0 0.0 collective-permute-done.6.refs_0_
  52.0 0.8 %place.2.refs_1_ = bf16[256,4096]{1,0:T(8,128)(2,1)} custom-call(bf16[256,1024]{1,0:T(8,128)(2,1)S(1)} %collective-permute-done.6.refs_0_, bf16[256,4096]{1,0:T(8,128)(2,1)} %attend.5.refs_1_), custom_call_target="tpu_custom_call", output_to_operand_aliasing={{}: (1, {})} | custom-call | flops 262144 | bytes 1048576 | tf_op jit(solution)/shard_map/place/pallas_call | solution.py:525
  52.8 0.0 collective-permute-done.5.refs_0_
  52.8 0.8 %place.3 = bf16[256,4096]{1,0:T(8,128)(2,1)} custom-call(bf16[256,1024]{1,0:T(8,128)(2,1)S(1)} %collective-permute-done.5.refs_0_, bf16[256,4096]{1,0:T(8,128)(2,1)} %place.2.refs_1_), custom_call_target="tpu_custom_call", output_to_operand_aliasing={{}: (1, {})} | custom-call | flops 262144 | bytes 1048576 | tf_op jit(solution)/shard_map/place/pallas_call | solution.py:525
  (4 shorter events, 0.1 us)
Async XLA Ops:
  1.6 17.9 %collective-permute-start = (bf16[512,128]{1,0:T(8,128)(2,1)S(1)}, bf16[512,128]{1,0:T(8,128)(2,1)S(1)}, u32[]{:S(2)}, u32[]{:S(2)}) collective-permute-start(bf16[512,128]{1,0:T(8,128)(2,1)S(1)} %get-tuple-element.17), channel_id=1, source_target_pairs={{0,4},{4,8},{8,12},{12,16},{16,20},{20,24},{24,28},{28,0},{1,5},{5... | collective-permute-start | bytes 393224 | tf_op jit(solution)/shard_map/ppermute | solution.py:36
  4.6 40.9 %collective-permute-start.7 = (bf16[256,1280]{1,0:T(8,128)(2,1)S(1)}, bf16[256,1280]{1,0:T(8,128)(2,1)S(1)}, u32[]{:S(2)}, u32[]{:S(2)}) collective-permute-start(bf16[256,1280]{1,0:T(8,128)(2,1)S(1)} %get-tuple-element.20), channel_id=1, source_target_pairs={{0,2},{1,3},{2,0},{3,1},{4,6},{5,7},{6,4},{7,5},{8,10},{9,11},{10,... | collective-permute-start | bytes 1966088 | tf_op jit(solution)/shard_map/ppermute | solution.py:45
  6.2 8.8 %collective-permute-start.2 = (bf16[264,128]{1,0:T(8,128)(2,1)S(1)}, bf16[264,128]{1,0:T(8,128)(2,1)S(1)}, u32[]{:S(2)}, u32[]{:S(2)}) collective-permute-start(bf16[264,128]{1,0:T(8,128)(2,1)S(1)} %get-tuple-element.18.refs_0_.rest_6_.refs_3_), channel_id=1, source_target_pairs={{0,8},{4,12},{8,16},{12,20},{16,24},{20,28},{24,0},{28,4},{1,9},{5... | collective-permute-start | bytes 202760 | tf_op jit(solution)/shard_map/ppermute | solution.py:36
  7.7 7.2 %collective-permute-start.1 = (bf16[264,128]{1,0:T(8,128)(2,1)S(1)}, bf16[264,128]{1,0:T(8,128)(2,1)S(1)}, u32[]{:S(2)}, u32[]{:S(2)}) collective-permute-start(bf16[264,128]{1,0:T(8,128)(2,1)S(1)} %get-tuple-element.18.refs_0_.rest_6_.refs_3_), channel_id=1, source_target_pairs={{0,4},{4,8},{8,12},{12,16},{16,20},{20,24},{24,28},{28,0},{1,5},{5... | collective-permute-start | bytes 202760 | tf_op jit(solution)/shard_map/ppermute | solution.py:36
  9.3 5.6 %collective-permute-start.3 = (bf16[72,128]{1,0:T(8,128)(2,1)S(1)}, bf16[72,128]{1,0:T(8,128)(2,1)S(1)}, u32[]{:S(2)}, u32[]{:S(2)}) collective-permute-start(bf16[72,128]{1,0:T(8,128)(2,1)S(1)} %get-tuple-element.19), channel_id=1, source_target_pairs={{0,12},{4,16},{8,20},{12,24},{16,28},{20,0},{24,4},{28,8},{1,13},{... | collective-permute-start | bytes 55304 | tf_op jit(solution)/shard_map/ppermute | solution.py:36
  14.9 4.6 %collective-permute-start.4 = (bf16[32,128]{1,0:T(8,128)(2,1)S(1)}, bf16[32,128]{1,0:T(8,128)(2,1)S(1)}, u32[]{:S(2)}, u32[]{:S(2)}) collective-permute-start(bf16[32,128]{1,0:T(8,128)(2,1)S(1)} %select.2.refs_0_), channel_id=1, source_target_pairs={{0,16},{4,20},{8,24},{12,28},{16,0},{20,4},{24,8},{28,12},{1,17},{... | collective-permute-start | bytes 24584 | tf_op jit(solution)/shard_map/ppermute | solution.py:36
  25.2 26.8 %collective-permute-start.6 = (bf16[256,1024]{1,0:T(8,128)(2,1)S(1)}, bf16[256,1024]{1,0:T(8,128)(2,1)S(1)}, u32[]{:S(2)}, u32[]{:S(2)}) collective-permute-start(bf16[256,1024]{1,0:T(8,128)(2,1)S(1)} %attend.4.rest_11_), channel_id=1, source_target_pairs={{0,1},{1,0},{2,3},{3,2},{4,5},{5,4},{6,7},{7,6},{8,9},{9,8},{10,11... | collective-permute-start | bytes 1572872 | tf_op jit(solution)/shard_map/ppermute | solution.py:45
  25.2 27.6 %collective-permute-start.5 = (bf16[256,1024]{1,0:T(8,128)(2,1)S(1)}, bf16[256,1024]{1,0:T(8,128)(2,1)S(1)}, u32[]{:S(2)}, u32[]{:S(2)}) collective-permute-start(bf16[256,1024]{1,0:T(8,128)(2,1)S(1)} %attend.3.rest_8_), channel_id=1, source_target_pairs={{0,3},{1,2},{2,1},{3,0},{4,7},{5,6},{6,5},{7,4},{8,11},{9,10},{10,... | collective-permute-start | bytes 1572872 | tf_op jit(solution)/shard_map/ppermute | solution.py:45
  26.9 18.6 %collective-permute-start.9 = (bf16[288,256]{1,0:T(8,128)(2,1)S(1)}, bf16[288,256]{1,0:T(8,128)(2,1)S(1)}, u32[]{:S(2)}, u32[]{:S(2)}) collective-permute-start(bf16[288,256]{1,0:T(8,128)(2,1)S(1)} %pack.3), channel_id=1, source_target_pairs={{0,2},{1,3},{2,0},{3,1},{4,6},{5,7},{6,4},{7,5},{8,10},{9,11},{10,... | collective-permute-start | bytes 442376 | tf_op jit(solution)/shard_map/ppermute | solution.py:45
  27.5 18.0 %collective-permute-start.8 = (bf16[256,256]{1,0:T(8,128)(2,1)S(1)}, bf16[256,256]{1,0:T(8,128)(2,1)S(1)}, u32[]{:S(2)}, u32[]{:S(2)}) collective-permute-start(bf16[256,256]{1,0:T(8,128)(2,1)S(1)} %pack.2), channel_id=1, source_target_pairs={{0,2},{1,3},{2,0},{3,1},{4,6},{5,7},{6,4},{7,5},{8,10},{9,11},{10,... | collective-permute-start | bytes 393224 | tf_op jit(solution)/shard_map/ppermute | solution.py:45
